TPU v7x, 32 devices: a whole 2x2x4 slice. The times are simulated.
32 devices in a mesh: mode: 4 (over y, x), mesh: 8 (over z, core).
Axes of the slice: x: 2, y: 2, z: 4, core: 2. Of those that a mesh axis runs over, the one named last changes fastest.
Arguments:
- velocity: float32 [3, 2, 64, 20480], P(None, None, 'mode', 'mesh'), may hold values from -2.1 to 2.1
- magnetic: float32 [3, 2, 64, 20480], P(None, None, 'mode', 'mesh'), may hold values from -2.1 to 2.1
- leaf_inverse: bfloat16 [64, 160, 128, 128], P('mode', 'mesh'), may hold values from -1 to 2
- leaf_coupling: bfloat16 [64, 128, 20480], P('mode', None, 'mesh'), may hold values from -0.05908203 to 0.05908203
- separator_inverse: bfloat16 [64, 1024, 128], P('mode', 'mesh'), may hold values from -1 to 2
- separator_coupling: bfloat16 [64, 1024, 128], P('mode', 'mesh'), may hold values from -0.26367188 to 0.26367188
- separator_source: float32 [2, 64, 1024], P(None, 'mode', 'mesh'), may hold values from -6 to 6
- front_rows: int32 [8, 2, 128], P('mesh'), may hold values from 0 to 127, each once within a row
Outputs:
- nonlinear: float32 [3, 2, 64, 20480], P(None, None, 'mode', 'mesh')
- azimuthal_field: float32 [2, 64, 20480], P(None, 'mode', 'mesh')
- separator_solution: float32 [2, 64, 1024], P(None, 'mode', 'mesh')
Inputs may be any that keep to these rules, and one draw needn't show every extreme that they name: front_rows[p, 0] and front_rows[p, 1] each hold every number below 128 once.
All inputs are finite; a program needn't handle non-finite values.
Results may differ from a plain program's by a relative error of at most 0.015.
Values may be sent and summed in bfloat16 or wider, within the bound.
No kernel may reach another device: no remote copies, remote signals or barrier semaphores. Data moves between devices by JAX's collectives and lax.ppermute only.
A program may use at most 128 MiB of HBM per device.

v0:
```python
import jax
import jax.numpy as jnp
from jax import lax
from jax.sharding import PartitionSpec as P

M = 64
NPHI = 192


highest = lax.Precision.HIGHEST
dt_step = 0.5


def tables():
    angles = jnp.arange(NPHI, dtype=jnp.int32)[:, None]
    orders = jnp.arange(M, dtype=jnp.int32)[None, :]
    phase = (angles * orders % NPHI).astype(jnp.float32) * (2.0 * jnp.pi / NPHI)
    forward = jnp.stack([jnp.cos(phase), jnp.sin(phase)], axis=1)
    weights = jnp.where(orders == 0, 1.0, 2.0).astype(jnp.float32) / NPHI
    backward = jnp.stack([(jnp.cos(phase) * weights).T, (jnp.sin(phase) * weights).T], axis=0)
    return (forward, backward)


def cross_terms(first, second):
    return jnp.stack(
        [
            first[1] * second[2] - first[2] * second[1],
            first[2] * second[0] - first[0] * second[2],
            first[0] * second[1] - first[1] * second[0],
        ]
    )


def forward_fields(forward, velocity, magnetic):
    return (
        jnp.einsum("kam,camn->ckn", forward, velocity, precision=highest),
        jnp.einsum("kam,camn->ckn", forward, magnetic, precision=highest),
    )


def gather_children(values):
    return lax.all_gather(values, "mesh", axis=2, tiled=True)


def gather_parents(values):
    return lax.all_gather(values, "mesh", axis=2, tiled=True)


def block_of(whole, index, partitions, sep_rows):
    start = (jnp.clip(index, 0, partitions - 1) * sep_rows).astype(jnp.int32)
    return lax.dynamic_slice_in_dim(whole, start, sep_rows, 2)


def shards(
    velocity,
    magnetic,
    leaf_inverse,
    leaf_coupling,
    separator_inverse,
    separator_coupling,
    separator_source,
    front_rows,
):
    modes_dev = velocity.shape[2]
    nodes_dev = velocity.shape[3]
    forward, backward = tables()
    spread_velocity, spread_magnetic = (
        lax.all_to_all(
            velocity.astype(jnp.bfloat16), "mode", split_axis=3, concat_axis=2, tiled=True
        ).astype(velocity.dtype),
        lax.all_to_all(
            magnetic.astype(jnp.bfloat16), "mode", split_axis=3, concat_axis=2, tiled=True
        ).astype(magnetic.dtype),
    )
    phys_velocity, phys_magnetic = forward_fields(forward, spread_velocity, spread_magnetic)
    local_terms = jnp.einsum(
        "amk,ckn->camn", backward, cross_terms(phys_velocity, phys_magnetic), precision=highest
    )
    nonlinear = lax.all_to_all(
        local_terms.astype(jnp.bfloat16), "mode", split_axis=2, concat_axis=3, tiled=True
    ).astype(local_terms.dtype)
    blocks_dev = leaf_inverse.shape[1]
    block_width = leaf_inverse.shape[2]
    sep_rows = separator_source.shape[2]
    source = (magnetic[1] + dt_step * nonlinear[1]).astype(jnp.bfloat16)
    leaf_solved = (
        jnp.einsum(
            "mkij,cmkj->cmki",
            leaf_inverse,
            source.reshape(2, modes_dev, blocks_dev, block_width),
            preferred_element_type=jnp.float32,
        )
        .reshape(2, modes_dev, nodes_dev)
        .astype(jnp.bfloat16)
    )
    row_order = front_rows[0]
    leaf_map = jnp.take(leaf_coupling, row_order[0], axis=1)
    upward_map = jnp.take(separator_coupling, row_order[1], axis=1)
    leaf_update = jnp.einsum(
        "mij,cmj->cmi", leaf_map, leaf_solved, preferred_element_type=jnp.float32
    )
    partitions = lax.axis_size("mesh")
    levels = partitions.bit_length() - 1
    position = lax.axis_index("mesh")
    depth_now = sum(
        [(position % 2**bit_now == 0).astype(jnp.int32) for bit_now in range(1, levels + 1)]
    )
    level_here = depth_now + 1

    def settle(arrived, height, reduced, outgoing):
        fresh = jnp.einsum(
            "mij,cmj->cmi",
            separator_inverse,
            (separator_source - arrived).astype(jnp.bfloat16),
            preferred_element_type=jnp.float32,
        ).astype(jnp.bfloat16)
        sending = jnp.einsum("mij,cmj->cmi", upward_map, fresh, preferred_element_type=jnp.float32)
        active = level_here == height
        return (jnp.where(active, fresh, reduced), jnp.where(active, sending, outgoing))

    reduced = jnp.zeros(separator_source.shape, jnp.bfloat16)
    outgoing = jnp.zeros(separator_source.shape, jnp.float32)
    everyone = gather_children(leaf_update)
    arrived = block_of(everyone, position - 1, partitions, sep_rows) + block_of(
        everyone, position, partitions, sep_rows
    )
    reduced, outgoing = settle(arrived, 1, reduced, outgoing)
    for height in range(2, levels + 1):
        gap = 2 ** (height - 2)
        everyone = gather_children(outgoing)
        arrived = block_of(everyone, position - gap, partitions, sep_rows) + block_of(
            everyone, position + gap, partitions, sep_rows
        )
        reduced, outgoing = settle(arrived, height, reduced, outgoing)
    everyone = gather_children(outgoing)
    reduced, outgoing = settle(
        block_of(everyone, partitions // 2, partitions, sep_rows), levels + 1, reduced, outgoing
    )
    top_value = jnp.einsum(
        "mij,cmi->cmj", separator_inverse, reduced, preferred_element_type=jnp.float32
    )
    solution = jnp.where(
        level_here == levels + 1, top_value, jnp.zeros(separator_source.shape, jnp.float32)
    )
    for height in range(levels, 0, -1):
        everyone = gather_parents(solution.astype(jnp.bfloat16))
        if height == levels:
            parent = position * 0
        else:
            parent = position // 2 ** (height + 1) * 2 ** (height + 1) + 2**height
        above = block_of(everyone, parent, partitions, sep_rows)
        residue = reduced.astype(jnp.float32) - jnp.einsum(
            "mij,cmi->cmj", upward_map, above, preferred_element_type=jnp.float32
        )
        fresh = jnp.einsum(
            "mij,cmi->cmj",
            separator_inverse,
            residue.astype(jnp.bfloat16),
            preferred_element_type=jnp.float32,
        )
        solution = jnp.where(level_here == height, fresh, solution)
    everyone = gather_parents(solution.astype(jnp.bfloat16))
    above = block_of(everyone, 2 * (position // 2) + 1, partitions, sep_rows)
    residue = leaf_solved.astype(jnp.float32) - jnp.einsum(
        "mij,cmi->cmj", leaf_map, above, preferred_element_type=jnp.float32
    )
    azimuthal_field = jnp.einsum(
        "mkji,cmkj->cmki",
        leaf_inverse,
        residue.astype(jnp.bfloat16).reshape(2, modes_dev, blocks_dev, block_width),
        preferred_element_type=jnp.float32,
    ).reshape(2, modes_dev, nodes_dev)
    return (nonlinear, azimuthal_field, solution)


def solution(mesh):
    in_specs = (
        P(None, None, "mode", "mesh"),
        P(None, None, "mode", "mesh"),
        P("mode", "mesh", None, None),
        P("mode", None, "mesh"),
        P("mode", "mesh", None),
        P("mode", "mesh", None),
        P(None, "mode", "mesh"),
        P("mesh", None, None),
    )
    out_specs = (P(None, None, "mode", "mesh"), P(None, "mode", "mesh"), P(None, "mode", "mesh"))
    return jax.shard_map(shards, mesh=mesh, in_specs=in_specs, out_specs=out_specs, check_vma=False)
```

profile of v0, /device:TPU:9, one launch (start us, length us, event | category | flops | bytes accessed | tf_op | source)
XLA Modules:
  0.0 204.3 jit_solution(15129035748217924793)
XLA Ops:
  0.6 0.0 copy-start
  0.6 0.0 copy-start.4
  0.7 1.4 convert_element_type.163
  2.0 5.2 %copy.84 = bf16[3,2,16,2560]{2,0,1,3:T(4,128)(2,1)} copy(bf16[3,2,16,2560]{3,2,1,0:T(8,128)(2,1)S(1)} %convert_element_type.163) | data formatting | bytes 983040 | tf_op jit(solution)/shard_map/convert_element_type | solution.py:72
  7.2 6.7 %reshape.281 = bf16[4,2,30720]{2,1,0:T(2,128)(2,1)} reshape(bf16[2560,2,3,16]{3,2,1,0:T(4,128)(2,1)} %bitcast.190) | data formatting | bytes 983040
  13.9 3.5 %all-to-all-start.1 = ((bf16[4,2,30720]{2,1,0:T(2,128)(2,1)}), bf16[4,2,30720]{2,1,0:T(2,128)(2,1)S(1)}, u32[]{:S(2)}, u32[]{:S(2)}) async-start(bf16[4,2,30720]{2,1,0:T(2,128)(2,1)} %reshape.281), calls=%async_computation.1 | async-start | bytes 983040 | tf_op jit(solution)/shard_map/all_to_all | solution.py:71
  17.4 0.0 copy-done.4
  17.4 0.1 convert_element_type.162
  17.4 5.2 %copy.82 = bf16[3,2,16,2560]{2,0,1,3:T(4,128)(2,1)} copy(bf16[3,2,16,2560]{3,2,1,0:T(8,128)(2,1)S(1)} %convert_element_type.162) | data formatting | bytes 983040 | tf_op jit(solution)/shard_map/convert_element_type | solution.py:69
  22.6 6.7 %reshape.279 = bf16[4,2,30720]{2,1,0:T(2,128)(2,1)} reshape(bf16[2560,2,3,16]{3,2,1,0:T(4,128)(2,1)} %bitcast.191) | data formatting | bytes 983040
  29.3 0.0 copy-done.6
  29.3 0.0 all-to-all-done.1
  29.3 3.6 %all-to-all-start = ((bf16[4,2,30720]{2,1,0:T(2,128)(2,1)}), bf16[4,2,30720]{2,1,0:T(2,128)(2,1)S(1)}, u32[]{:S(2)}, u32[]{:S(2)}) async-start(bf16[4,2,30720]{2,1,0:T(2,128)(2,1)} %reshape.279), calls=%async_computation | async-start | bytes 983040 | tf_op jit(solution)/shard_map/all_to_all | solution.py:68
  32.9 0.3 fusion.66
  33.2 0.3 cosine_multiply_fusion
  33.5 6.0 %reshape.282 = bf16[2560,2,3,16]{3,2,1,0:T(4,128)(2,1)} reshape(bf16[4,2,30720]{2,1,0:T(2,128)(2,1)S(1)} %all-to-all-done.1) | data formatting | bytes 983040
  39.4 5.8 %copy.85 = bf16[3,2,16,4,640]{4,2,3,1,0:T(8,128)(2,1)S(1)} copy(bf16[3,2,16,4,640]{2,0,1,4,3:T(4,128)(2,1)} %bitcast.192) | data formatting | bytes 983040 | tf_op jit(solution)/shard_map/all_to_all | solution.py:71
  45.2 0.0 all-to-all-done
  45.2 6.0 %reshape.280 = bf16[2560,2,3,16]{3,2,1,0:T(4,128)(2,1)} reshape(bf16[4,2,30720]{2,1,0:T(2,128)(2,1)S(1)} %all-to-all-done) | data formatting | bytes 983040
  51.2 5.8 %copy.83 = bf16[3,2,16,4,640]{4,2,3,1,0:T(8,128)(2,1)S(1)} copy(bf16[3,2,16,4,640]{2,0,1,4,3:T(4,128)(2,1)} %bitcast.193) | data formatting | bytes 983040 | tf_op jit(solution)/shard_map/all_to_all | solution.py:68
  57.0 0.8 convolution_bitcast_fusion
  57.8 0.8 convolution_bitcast_fusion.1
  58.6 0.2 multiply_subtract_fusion.2
  58.8 1.2 fusion.19
  59.9 1.3 copy.86
  61.2 3.6 %all-to-all-start.2 = ((bf16[3,2,64,640]{3,1,0,2:T(2,128)(2,1)}), bf16[3,2,64,640]{3,1,0,2:T(2,128)(2,1)S(1)}, u32[]{:S(2)}, u32[]{:S(2)}) async-start(bf16[3,2,64,640]{3,1,0,2:T(2,128)(2,1)} %copy.86), calls=%async_computation.2 | async-start | bytes 983040 | tf_op jit(solution)/shard_map/all_to_all | solution.py:79
  65.0 0.0 copy-done
  65.0 2.8 %gather_fusion.1 = bf16[128,16,128]{2,0,1:T(8,128)(2,1)S(1)} fusion(bf16[16,128,128]{2,1,0:T(8,128)(2,1)S(1)} %copy-done, s32[1024]{0:T(1024)S(1)} %pad_clamp_fusion), kind=kCustom, calls=%fused_computation.1 | custom fusion | bytes 1049088 | tf_op jit(solution)/shard_map/jit(_take)/gather | solution.py:98
  67.8 24.7 %gather_fusion = bf16[128,16,2560]{2,0,1:T(8,128)(2,1)} fusion(bf16[16,128,2560]{2,1,0:T(8,128)(2,1)} %param.11, s32[1024]{0:T(1024)S(1)} %pad_clamp_fusion.1), kind=kCustom, calls=%fused_computation | custom fusion | bytes 20972032 | tf_op jit(solution)/shard_map/jit(_take)/gather | solution.py:97
  92.4 0.0 all-to-all-done.2
  92.4 0.1 copy.87
  92.6 1.0 add_convert_fusion
  93.6 0.1 convert_element_type.172
  93.7 0.0 copy-start.2
  93.7 1.0 copy.104
  94.8 9.0 %fusion.20 = bf16[2,16,2560]{2,0,1:T(2,128)(2,1)S(1)} fusion(bf16[16,20,128,128]{3,2,1,0:T(8,128)(2,1)} %param.10, bf16[2,16,20,128]{3,2,1,0:T(8,128)(2,1)S(1)} %convert_element_type.172), kind=kOutput, calls=%fused_computation.22 | convolution fusion | flops 21053440 | bytes 10813440 | tf_op jit(solution)/shard_map/mkij,cmkj->cmki/dot_general | solution.py:87
  103.8 0.0 copy-start.3
  103.8 0.0 copy-start.5
  103.8 0.0 copy-done.2
  103.8 2.9 %fusion.26 = f32[2,16,128]{2,0,1:T(2,128)S(1)} fusion(bf16[2,16,2560]{2,0,1:T(2,128)(2,1)S(1)} %fusion.20, bf16[128,16,2560]{2,0,1:T(8,128)(2,1)S(1)} %copy-done.2, pred[128]{0:T(512)(128)(4,1)S(1)} %get-tuple-element.25), kind=kOutput, calls=%fused_computation.24 | convolution fusion | flops 26214400 | bytes 10666112 | tf_op jit(solution)/shard_map/mij,cmj->cmi/dot_general | solution.py:99
  106.6 11.3 %all_gather.24 = f32[2,16,1024]{2,0,1:T(2,128)S(1)} all-gather(f32[2,16,128]{2,0,1:T(2,128)S(1)} %fusion.26), channel_id=1, replica_groups=mesh['mode'=4,'mesh'=8] {'mesh'}, dimensions={2}, use_global_device_ids=true | all-gather | bytes 147456 | tf_op jit(solution)/shard_map/all_gather | solution.py:42
  118.0 0.0 copy-done.3
  118.0 0.0 copy-done.5
  118.0 0.4 fusion.39
  118.4 0.4 fusion.35
  118.8 12.3 %all_gather.25 = f32[2,16,1024]{2,0,1:T(2,128)S(1)} all-gather(f32[2,16,128]{2,0,1:T(2,128)S(1)} %fusion.35), channel_id=1, replica_groups=mesh['mode'=4,'mesh'=8] {'mesh'}, dimensions={2}, use_global_device_ids=true | all-gather | bytes 147456 | tf_op jit(solution)/shard_map/all_gather | solution.py:42
  131.1 0.4 fusion.40
  131.5 0.4 fusion.34
  131.9 9.3 %all_gather.26 = f32[2,16,1024]{2,0,1:T(2,128)S(1)} all-gather(f32[2,16,128]{2,0,1:T(2,128)S(1)} %fusion.34), channel_id=1, replica_groups=mesh['mode'=4,'mesh'=8] {'mesh'}, dimensions={2}, use_global_device_ids=true | all-gather | bytes 147456 | tf_op jit(solution)/shard_map/all_gather | solution.py:42
  141.2 0.4 fusion.41
  141.6 0.4 fusion.33
  142.0 10.6 %all_gather.27 = f32[2,16,1024]{2,0,1:T(2,128)S(1)} all-gather(f32[2,16,128]{2,0,1:T(2,128)S(1)} %fusion.33), channel_id=1, replica_groups=mesh['mode'=4,'mesh'=8] {'mesh'}, dimensions={2}, use_global_device_ids=true | all-gather | bytes 147456 | tf_op jit(solution)/shard_map/all_gather | solution.py:42
  152.6 0.4 fusion.43
  153.0 0.3 convolution_select_fusion.3
  153.3 9.1 %all_gather.28 = bf16[2,16,1024]{2,0,1:T(2,128)(2,1)S(1)} all-gather(bf16[2,16,128]{2,0,1:T(2,128)(2,1)S(1)} %convert_bitcast_fusion.2), channel_id=1, replica_groups=mesh['mode'=4,'mesh'=8] {'mesh'}, dimensions={2}, use_global_device_ids=true | all-gather | bytes 73728 | tf_op jit(solution)/shard_map/all_gather | solution.py:46
  162.4 0.4 convolution_select_fusion.2
  162.8 10.3 %all_gather.29 = bf16[2,16,1024]{2,0,1:T(2,128)(2,1)S(1)} all-gather(bf16[2,16,128]{2,0,1:T(2,128)(2,1)S(1)} %convert_bitcast_fusion.1), channel_id=1, replica_groups=mesh['mode'=4,'mesh'=8] {'mesh'}, dimensions={2}, use_global_device_ids=true | all-gather | bytes 73728 | tf_op jit(solution)/shard_map/all_gather | solution.py:46
  173.2 0.4 convolution_select_fusion.1
  173.6 9.0 %all_gather.30 = bf16[2,16,1024]{2,0,1:T(2,128)(2,1)S(1)} all-gather(bf16[2,16,128]{2,0,1:T(2,128)(2,1)S(1)} %convert_bitcast_fusion), channel_id=1, replica_groups=mesh['mode'=4,'mesh'=8] {'mesh'}, dimensions={2}, use_global_device_ids=true | all-gather | bytes 73728 | tf_op jit(solution)/shard_map/all_gather | solution.py:46
  182.6 0.5 fusion.105
  183.1 0.6 copy.98
  183.7 10.4 %all_gather.31 = bf16[2,16,1024]{2,0,1:T(2,128)(2,1)S(1)} all-gather(bf16[2,16,128]{2,0,1:T(2,128)(2,1)S(1)} %get-tuple-element.30), channel_id=1, replica_groups=mesh['mode'=4,'mesh'=8] {'mesh'}, dimensions={2}, use_global_device_ids=true | all-gather | bytes 73728 | tf_op jit(solution)/shard_map/all_gather | solution.py:46
  194.1 9.3 %convolution_bitcast_fusion.2 = f32[2,16,20,128]{3,0,2,1:T(2,128)S(1)} fusion(bf16[16,20,128,128]{3,2,1,0:T(8,128)(2,1)} %param.10, bf16[128,16,2560]{2,0,1:T(8,128)(2,1)} %gather_fusion, pred[128]{0:T(512)(128)(4,1)S(1)} %get-tuple-element.25, bf16[2,16,2560]{2,0,1:T(2,128)(2,1)S(1)} %fusion.20, bf16[2,16,1024]{2,0,1:T(2,128)(2,1)S(1)} %all_gather.31, ...), kind=kOutput, calls=%fused_computation.20 | convolution fusion | flops 47431680 | bytes 21471748 | tf_op jit(solution)/shard_map/mkji,cmkj->cmki/dot_general | solution.py:167
  203.5 0.8 reshape.255
  (14 shorter events, 0.2 us)
Async XLA Ops:
  0.6 64.4 %copy-start = (bf16[16,128,128]{2,1,0:T(8,128)(2,1)S(1)}, bf16[16,128,128]{2,1,0:T(8,128)(2,1)}, u32[]{:S(2)}) copy-start(bf16[16,128,128]{2,1,0:T(8,128)(2,1)} %param.13) | copy-start | bytes 1572868
  0.6 16.7 %copy-start.4 = (f32[3,2,16,2560]{3,2,1,0:T(8,128)S(1)}, f32[3,2,16,2560]{3,2,1,0:T(8,128)}, u32[]{:S(2)}) copy-start(f32[3,2,16,2560]{3,2,1,0:T(8,128)} %param.8) | copy-start | bytes 2949124
  7.2 22.1 %copy-start.6 = (s32[1,2,128]{2,1,0:T(2,128)S(1)}, s32[1,2,128]{2,1,0:T(2,128)}, u32[]{:S(2)}) copy-start(s32[1,2,128]{2,1,0:T(2,128)} %param.15) | copy-start | bytes 3076
  13.9 15.4 %all-to-all-start.1 = ((bf16[4,2,30720]{2,1,0:T(2,128)(2,1)}), bf16[4,2,30720]{2,1,0:T(2,128)(2,1)S(1)}, u32[]{:S(2)}, u32[]{:S(2)}) async-start(bf16[4,2,30720]{2,1,0:T(2,128)(2,1)} %reshape.281), calls=%async_computation.1 | async-start | bytes 983040 | tf_op jit(solution)/shard_map/all_to_all | solution.py:71
  29.3 15.9 %all-to-all-start = ((bf16[4,2,30720]{2,1,0:T(2,128)(2,1)}), bf16[4,2,30720]{2,1,0:T(2,128)(2,1)S(1)}, u32[]{:S(2)}, u32[]{:S(2)}) async-start(bf16[4,2,30720]{2,1,0:T(2,128)(2,1)} %reshape.279), calls=%async_computation | async-start | bytes 983040 | tf_op jit(solution)/shard_map/all_to_all | solution.py:68
  61.2 31.2 %all-to-all-start.2 = ((bf16[3,2,64,640]{3,1,0,2:T(2,128)(2,1)}), bf16[3,2,64,640]{3,1,0,2:T(2,128)(2,1)S(1)}, u32[]{:S(2)}, u32[]{:S(2)}) async-start(bf16[3,2,64,640]{3,1,0,2:T(2,128)(2,1)} %copy.86), calls=%async_computation.2 | async-start | bytes 983040 | tf_op jit(solution)/shard_map/all_to_all | solution.py:79
  93.7 10.1 %copy-start.2 = (bf16[128,16,2560]{2,0,1:T(8,128)(2,1)S(1)}, bf16[128,16,2560]{2,0,1:T(8,128)(2,1)}, u32[]{:S(2)}) copy-start(bf16[128,16,2560]{2,0,1:T(8,128)(2,1)} %gather_fusion) | copy-start | bytes 31457284
  103.8 14.2 %copy-start.3 = (bf16[16,128,128]{2,1,0:T(8,128)(2,1)S(1)}, bf16[16,128,128]{2,1,0:T(8,128)(2,1)}, u32[]{:S(2)}) copy-start(bf16[16,128,128]{2,1,0:T(8,128)(2,1)} %param.12) | copy-start | bytes 1572868
  103.8 14.2 %copy-start.5 = (f32[2,16,128]{2,1,0:T(8,128)S(1)}, f32[2,16,128]{2,1,0:T(8,128)}, u32[]{:S(2)}) copy-start(f32[2,16,128]{2,1,0:T(8,128)} %param.14) | copy-start | bytes 49156
  183.7 20.6 %copy-start.1 = (bf16[16,128,128]{2,1,0:T(8,128)(2,1)S(1)}, bf16[16,128,128]{2,1,0:T(8,128)(2,1)}, u32[]{:S(2)}) copy-start(bf16[16,128,128]{2,1,0:T(8,128)(2,1)} %param.13) | copy-start | bytes 1572868
where the time goes:
time: 206 us; the launch traced here: 204 us
  blocking collectives  82.4 us (40%)
  local copies, waits for them, and re-layouts  78.6 us (38%)
  matrix products  28.4 us (14%)
  starting transfers between devices  10.7 us (5%)
  other arithmetic  3.23 us (2%)
    all_gather x4, blocking collectives, gather_children(): return lax.all_gather(values, 'mesh', axis=2, tiled=True)  43.5 us
    all_gather x4, blocking collectives, gather_parents(): return lax.all_gather(values, 'mesh', axis=2, tiled=True)  38.8 us
    unnamed x19, local copies, waits for them, and re-layouts  25.9 us
    gather x1, local copies, waits for them, and re-layouts, shards(): leaf_map = jnp.take(leaf_coupling, row_order[0], axis=1)  24.7 us
    dot_general x1, matrix products, shards(): jnp.einsum('mkji,cmkj->cmki', leaf_inverse, residue.astype(jnp.bfloat16)....  9.34 us
    dot_general x1, matrix products, shards(): jnp.einsum('mkij,cmkj->cmki', leaf_inverse, source.reshape(2, modes_dev,...  8.98 us
    all_to_all x1, local copies, waits for them, and re-layouts, shards(): lax.all_to_all(magnetic.astype(jnp.bfloat16), 'mode', split_axis=3, conca...  5.77 us
    all_to_all x1, local copies, waits for them, and re-layouts, shards(): lax.all_to_all(velocity.astype(jnp.bfloat16), 'mode', split_axis=3, conca...  5.77 us
  transfers between devices with their start and end apart: 3, of which 0 were waited for; matrix products, arithmetic and copies ran while one was open for 25% of the time, Pallas kernels for 0%

commit v1 on v0

v1 whole, which is shorter than its diff:
```python
import functools

import jax
import jax.numpy as jnp
from jax import lax
from jax.experimental import pallas as pl
from jax.experimental.pallas import tpu as pltpu
from jax.sharding import PartitionSpec as P

NPHI = 192
DT_STEP = 0.5
VMEM = pltpu.VMEM
SMEM = pltpu.SMEM
BF16 = jnp.bfloat16
F32 = jnp.float32
NT = (((1,), (1,)), ((), ()))
NN = (((1,), (0,)), ((), ()))


def dot(a, b, dims=NN, precision=None):
    return lax.dot_general(a, b, dims, precision=precision, preferred_element_type=F32)


def tables(me, groups, modes_dev):
    steps = jnp.bitwise_xor(me, jnp.arange(groups, dtype=jnp.int32))
    orders = (steps[:, None] * modes_dev + jnp.arange(modes_dev, dtype=jnp.int32)[None, :])[:, None, :]
    angles = jnp.arange(NPHI, dtype=jnp.int32)[:, None, None, None]
    phase = (angles * orders[None] % NPHI).astype(F32) * (2.0 * jnp.pi / NPHI)
    forward = jnp.concatenate([jnp.cos(phase), jnp.sin(phase)], axis=2)
    weights = jnp.where(orders == 0, 1.0, 2.0).astype(F32)[None] / NPHI
    rows = groups * 2 * modes_dev
    return (
        forward.reshape(NPHI, rows).astype(BF16),
        (forward * weights).reshape(NPHI, rows).T.astype(BF16),
    )


def pack_kernel(groups, me_ref, v_ref, b_ref, *outs):
    rows, width = v_ref.shape[0], outs[0].shape[1]
    for k in range(groups):
        span = pl.ds(pl.multiple_of(jnp.bitwise_xor(me_ref[0], k) * width, 128), width)
        outs[k][:rows, :] = v_ref[:, span].astype(BF16)
        outs[k][rows:, :] = b_ref[:, span].astype(BF16)


def pack(me, velocity, magnetic, groups):
    rows, nodes = velocity.shape
    width = nodes // groups
    return pl.pallas_call(
        functools.partial(pack_kernel, groups),
        out_shape=[jax.ShapeDtypeStruct((2 * rows, width), BF16)] * groups,
        in_specs=[pl.BlockSpec(memory_space=SMEM)] + [pl.BlockSpec(memory_space=VMEM)] * 2,
        out_specs=[pl.BlockSpec(memory_space=VMEM)] * groups,
        compiler_params=pltpu.CompilerParams(vmem_limit_bytes=16 * 2**20),
        name="pack",
    )(me, velocity, magnetic)


def transform_kernel(groups, fwd_ref, bwd_ref, *refs):
    ins, azi, rest = refs[:groups], refs[groups : 2 * groups], refs[2 * groups :]
    rows = ins[0].shape[0] // 6
    fwd, bwd = fwd_ref[...], bwd_ref[...]
    phys = []
    for field in range(6):
        coef = jnp.concatenate([r[field * rows : (field + 1) * rows, :] for r in ins], axis=0)
        phys.append(dot(fwd, coef))
    v, b = phys[:3], phys[3:]
    for c in range(3):
        p, q = (c + 1) % 3, (c + 2) % 3
        crossed = (v[p] * b[q] - v[q] * b[p]).astype(BF16)
        terms = dot(bwd, crossed).astype(BF16)
        for k in range(groups):
            block = terms[k * rows : (k + 1) * rows, :]
            if c == 1:
                azi[k][...] = block
            else:
                at = 0 if c == 0 else rows
                rest[k][at : at + rows, :] = block


def transform(fwd, bwd, pieces):
    groups = len(pieces)
    rows, width = pieces[0].shape
    rows = rows // 6
    out = pl.pallas_call(
        functools.partial(transform_kernel, groups),
        out_shape=[jax.ShapeDtypeStruct((rows, width), BF16)] * groups
        + [jax.ShapeDtypeStruct((2 * rows, width), BF16)] * groups,
        in_specs=[pl.BlockSpec(memory_space=VMEM)] * (2 + groups),
        out_specs=[pl.BlockSpec(memory_space=VMEM)] * (2 * groups),
        compiler_params=pltpu.CompilerParams(vmem_limit_bytes=24 * 2**20),
        name="transform",
    )(fwd, bwd, *pieces)
    return out[:groups], out[groups:]


def one_hot(rows_ref):
    n = rows_ref.shape[1]
    return lax.broadcasted_iota(jnp.int32, (n, n), 0) == rows_ref[0:1, :]


def fetch(modes, pairs, sems):
    def copy(which, m):
        src, dst = pairs[which]
        return pltpu.make_async_copy(src.at[m], dst.at[m], sems.at[which, m])

    def start(m, carry):
        for which in range(len(pairs)):
            copy(which, m).start()
        return carry

    lax.fori_loop(0, modes, start, 0)
    return copy


def leaf_up_kernel(groups, me_ref, rows_ref, mag_ref, *refs):
    pieces = refs[:groups]
    inv_hbm, cpl_hbm, solved_ref, update_ref, inv_v, cpl_v, src_v, upd_v, sems = refs[groups:]
    _, modes, nodes = mag_ref.shape
    width = nodes // groups
    blocks, size = inv_v.shape[1], inv_v.shape[2]
    copy = fetch(modes, ((inv_hbm, inv_v), (cpl_hbm, cpl_v)), sems)
    for k in range(groups):
        span = pl.ds(pl.multiple_of(jnp.bitwise_xor(me_ref[0], k) * width, 128), width)
        for a in range(2):
            term = pieces[k][a * modes : (a + 1) * modes, :].astype(F32)
            src_v[a, :, span] = (mag_ref[a, :, span] + DT_STEP * term).astype(BF16).astype(F32)

    def one_mode(m, carry):
        copy(0, m).wait()
        source = src_v[:, pl.ds(m, 1), :].reshape(2, nodes).astype(BF16)
        solved = jnp.concatenate(
            [
                dot(source[:, b * size : (b + 1) * size], inv_v[m, b], NT)
                for b in range(blocks)
            ],
            axis=1,
        ).astype(BF16)
        solved_ref[:, pl.ds(m, 1), :] = solved.astype(F32).reshape(2, 1, nodes)
        copy(1, m).wait()
        upd_v[:, pl.ds(m, 1), :] = dot(solved, cpl_v[m], NT).reshape(2, 1, size)
        return carry

    lax.fori_loop(0, modes, one_mode, 0)
    select = one_hot(rows_ref).astype(F32)
    for a in range(2):
        update_ref[a] = dot(upd_v[a], select, precision=lax.Precision.HIGHEST)


def leaf_up(me, rows, mag, pieces, inverse, coupling):
    _, modes, nodes = mag.shape
    groups = len(pieces)
    front = coupling.shape[1]
    any_spec, vmem_spec = pl.BlockSpec(memory_space=pl.ANY), pl.BlockSpec(memory_space=VMEM)
    return pl.pallas_call(
        functools.partial(leaf_up_kernel, groups),
        out_shape=[
            jax.ShapeDtypeStruct((2, modes, nodes), F32),
            jax.ShapeDtypeStruct((2, modes, front), F32),
        ],
        in_specs=[pl.BlockSpec(memory_space=SMEM)] + [vmem_spec] * (2 + groups) + [any_spec] * 2,
        out_specs=[vmem_spec] * 2,
        scratch_shapes=[
            VMEM(inverse.shape, BF16),
            VMEM(coupling.shape, BF16),
            VMEM((2, modes, nodes), F32),
            VMEM((2, modes, front), F32),
            pltpu.SemaphoreType.DMA((2, modes)),
        ],
        compiler_params=pltpu.CompilerParams(vmem_limit_bytes=48 * 2**20),
        name="leaf_up",
    )(me, rows, mag, *pieces, inverse, coupling)


def leaf_down_kernel(rows_ref, above_ref, solved_ref, inv_hbm, cpl_hbm, out_ref, inv_v, cpl_v, x_v, sems):
    _, modes, nodes = solved_ref.shape
    blocks, size = inv_v.shape[1], inv_v.shape[2]
    copy = fetch(modes, ((inv_hbm, inv_v), (cpl_hbm, cpl_v)), sems)
    select = one_hot(rows_ref).astype(F32).astype(BF16)
    for a in range(2):
        x_v[a] = dot(above_ref[a].astype(BF16), select, NT)

    def one_mode(m, carry):
        copy(1, m).wait()
        x = x_v[:, pl.ds(m, 1), :].reshape(2, size).astype(BF16)
        residue = (solved_ref[:, pl.ds(m, 1), :].reshape(2, nodes) - dot(x, cpl_v[m])).astype(BF16)
        copy(0, m).wait()
        field = jnp.concatenate(
            [dot(residue[:, b * size : (b + 1) * size], inv_v[m, b]) for b in range(blocks)],
            axis=1,
        )
        out_ref[:, pl.ds(m, 1), :] = field.reshape(2, 1, nodes)
        return carry

    lax.fori_loop(0, modes, one_mode, 0)


def leaf_down(rows, above, solved, inverse, coupling):
    any_spec, vmem_spec = pl.BlockSpec(memory_space=pl.ANY), pl.BlockSpec(memory_space=VMEM)
    modes = solved.shape[1]
    return pl.pallas_call(
        leaf_down_kernel,
        out_shape=jax.ShapeDtypeStruct(solved.shape, F32),
        in_specs=[vmem_spec] * 3 + [any_spec] * 2,
        out_specs=vmem_spec,
        scratch_shapes=[
            VMEM(inverse.shape, BF16),
            VMEM(coupling.shape, BF16),
            VMEM(above.shape, F32),
            pltpu.SemaphoreType.DMA((2, modes)),
        ],
        compiler_params=pltpu.CompilerParams(vmem_limit_bytes=48 * 2**20),
        name="leaf_down",
    )(rows, above, solved, inverse, coupling)


def spread_kernel(groups, me_ref, *refs):
    azi, rest, out_ref = refs[:groups], refs[groups : 2 * groups], refs[2 * groups]
    rows, width = azi[0].shape
    for k in range(groups):
        span = pl.ds(pl.multiple_of(jnp.bitwise_xor(me_ref[0], k) * width, 128), width)
        out_ref[:rows, span] = rest[k][:rows, :].astype(F32)
        out_ref[rows : 2 * rows, span] = azi[k][...].astype(F32)
        out_ref[2 * rows :, span] = rest[k][rows:, :].astype(F32)


def spread(me, azi, rest):
    groups = len(azi)
    rows, width = azi[0].shape
    return pl.pallas_call(
        functools.partial(spread_kernel, groups),
        out_shape=jax.ShapeDtypeStruct((3 * rows, groups * width), F32),
        in_specs=[pl.BlockSpec(memory_space=SMEM)] + [pl.BlockSpec(memory_space=VMEM)] * (2 * groups),
        out_specs=pl.BlockSpec(memory_space=VMEM),
        compiler_params=pltpu.CompilerParams(vmem_limit_bytes=16 * 2**20),
        name="spread",
    )(me, *azi, *rest)


def level_of(q, levels):
    return levels + 1 if q == 0 else (q & -q).bit_length()


def shards(
    velocity,
    magnetic,
    leaf_inverse,
    leaf_coupling,
    separator_inverse,
    separator_coupling,
    separator_source,
    front_rows,
):
    groups = lax.axis_size("mode")
    partitions = lax.axis_size("mesh")
    levels = partitions.bit_length() - 1
    modes, nodes = velocity.shape[2], velocity.shape[3]
    sep_rows = separator_source.shape[2]
    here = lax.axis_index("mode")
    me = here.reshape(1).astype(jnp.int32)
    position = lax.axis_index("mesh")
    exchange = [[(g, g ^ k) for g in range(groups)] for k in range(groups)]

    def swap(pieces):
        return [pieces[0]] + [
            lax.ppermute(pieces[k], "mode", exchange[k]) for k in range(1, groups)
        ]

    fwd, bwd = tables(here, groups, modes)
    packed = pack(me, velocity.reshape(6 * modes, nodes), magnetic.reshape(6 * modes, nodes), groups)
    azi, rest = transform(fwd, bwd, swap(packed))
    azi = swap(azi)
    rest = swap(rest)
    row_order = front_rows[0]
    solved, update = leaf_up(me, row_order[0:1], magnetic[1], azi, leaf_inverse, leaf_coupling)
    nonlinear = spread(me, azi, rest).reshape(3, 2, modes, nodes)

    select = (jnp.arange(sep_rows, dtype=jnp.int32)[:, None] == row_order[1][None, :]).astype(F32)
    level_here = sum((position % 2**t == 0).astype(jnp.int32) for t in range(1, levels + 1)) + 1
    of_level = [[q for q in range(partitions) if level_of(q, levels) == h] for h in range(levels + 2)]

    def settle(arrived, height, reduced, outgoing):
        fresh = jnp.einsum(
            "mij,cmj->cmi",
            separator_inverse,
            (separator_source - arrived).astype(BF16),
            preferred_element_type=F32,
        ).astype(BF16)
        active = level_here == height
        reduced = jnp.where(active, fresh, reduced)
        if height <= levels:
            sending = jnp.einsum("mij,cmj->cmi", separator_coupling, fresh, preferred_element_type=F32)
            sending = jnp.einsum(
                "cmj,ji->cmi", sending, select, precision=lax.Precision.HIGHEST,
                preferred_element_type=F32,
            )
            outgoing = jnp.where(active, sending, outgoing)
        return reduced, outgoing

    reduced = jnp.zeros(separator_source.shape, BF16)
    outgoing = jnp.zeros(separator_source.shape, F32)
    arrived = update + lax.ppermute(update, "mesh", [(q - 1, q) for q in of_level[1]])
    reduced, outgoing = settle(arrived, 1, reduced, outgoing)
    for height in range(2, levels + 1):
        gap = 2 ** (height - 2)
        arrived = lax.ppermute(outgoing, "mesh", [(q - gap, q) for q in of_level[height]])
        arrived += lax.ppermute(outgoing, "mesh", [(q + gap, q) for q in of_level[height]])
        reduced, outgoing = settle(arrived, height, reduced, outgoing)
    arrived = lax.ppermute(outgoing, "mesh", [(partitions // 2, 0)])
    reduced, outgoing = settle(arrived, levels + 1, reduced, outgoing)

    top = jnp.einsum("mij,cmi->cmj", separator_inverse, reduced, preferred_element_type=F32)
    solution = jnp.where(level_here == levels + 1, top, jnp.zeros(separator_source.shape, F32))
    for height in range(levels, 0, -1):
        sending = solution.astype(BF16)
        if height == levels:
            above = lax.ppermute(sending, "mesh", [(0, partitions // 2)])
        else:
            gap = 2 ** (height - 1)
            parents = of_level[height + 1]
            above = lax.ppermute(sending, "mesh", [(q, q - gap) for q in parents])
            above += lax.ppermute(sending, "mesh", [(q, q + gap) for q in parents])
        above = jnp.einsum(
            "cmi,ji->cmj", above, select.astype(BF16), preferred_element_type=F32
        ).astype(BF16)
        residue = reduced.astype(F32) - jnp.einsum(
            "mij,cmi->cmj", separator_coupling, above, preferred_element_type=F32
        )
        fresh = jnp.einsum(
            "mij,cmi->cmj", separator_inverse, residue.astype(BF16), preferred_element_type=F32
        )
        solution = jnp.where(level_here == height, fresh, solution)
    sending = solution.astype(BF16)
    beside = lax.ppermute(sending, "mesh", [(q, q - 1) for q in of_level[1]])
    above = jnp.where(level_here == 1, sending, beside)
    azimuthal = leaf_down(row_order[0:1], above.astype(F32), solved, leaf_inverse, leaf_coupling)
    return (nonlinear, azimuthal, solution)


def solution(mesh):
    in_specs = (
        P(None, None, "mode", "mesh"),
        P(None, None, "mode", "mesh"),
        P("mode", "mesh", None, None),
        P("mode", None, "mesh"),
        P("mode", "mesh", None),
        P("mode", "mesh", None),
        P(None, "mode", "mesh"),
        P("mesh", None, None),
    )
    out_specs = (P(None, None, "mode", "mesh"), P(None, "mode", "mesh"), P(None, "mode", "mesh"))
    return jax.shard_map(shards, mesh=mesh, in_specs=in_specs, out_specs=out_specs, check_vma=False)
```

time: 206 us -> 97 us (0.47)
  blocking collectives: 82.4 us -> 0 us
  local copies, waits for them, and re-layouts: 78.6 us -> 3.47 us
  Pallas kernels: 0 us -> 31.2 us
  waiting for transfers between devices: 0.01 us -> 30.7 us
  matrix products: 28.4 us -> 5.28 us
  starting transfers between devices: 10.7 us -> 23.6 us
    all_gather x8 -> x0, blocking collectives: 82.4 us -> none  [the longest x4 43.5 us: gather_children(): return lax.all_gather(values, 'mesh', axis=2, tiled=True)]
    pallas_call x0 -> x5, Pallas kernels: none -> 31.2 us  [the longest x1 19 us: leaf_up(): pl.pallas_call(functools.partial(leaf_up_kernel, groups), out_shape=[jax....]
    ppermute x0 -> x21, waiting for transfers between devices: none -> 30.7 us  [the longest x2 14.4 us: shards(): above += lax.ppermute(sending, 'mesh', [(q, q + gap) for q in parents])]
    gather x2 -> x0, local copies, waits for them, and re-layouts: 27.4 us -> none  [the longest x1 24.7 us: shards(): leaf_map = jnp.take(leaf_coupling, row_order[0], axis=1)]
    ppermute x0 -> x21, starting transfers between devices: none -> 23.6 us  [the longest x9 8.14 us: swap(): lax.ppermute(pieces[k], 'mode', exchange[k])]
    unnamed x19 -> x10, local copies, waits for them, and re-layouts: 25.9 us -> 2.47 us
    dot_general x12 -> x15, matrix products: 26.6 us -> 3.55 us  [the longest x3 1.16 us: settle(): jnp.einsum('mij,cmj->cmi', separator_coupling, fresh, preferred_element_t...]
    convert_element_type x6 -> x1, local copies, waits for them, and re-layouts: 12.9 us -> 0.11 us  [tables(): forward.reshape(NPHI, rows).astype(BF16)]
  transfers between devices with their start and end apart: 3 -> 21, of which waited for: 0 -> 8; matrix products, arithmetic and copies ran while one was open for 25% -> 3% of each run, Pallas kernels for 0% -> 1%
where the time goes in v1:
time: 97 us; the launch traced here: 96.5 us
  Pallas kernels  31.2 us (32%)
  waiting for transfers between devices  30.7 us (32%)
  starting transfers between devices  23.6 us (24%)
  matrix products  5.28 us (5%)
  local copies, waits for them, and re-layouts  3.47 us (4%)
  other arithmetic  1.35 us (1%)
  between operations  1 us (1%)
    pallas_call x1, Pallas kernels, leaf_up(): pl.pallas_call(functools.partial(leaf_up_kernel, groups), out_shape=[jax....  19 us
    ppermute x2, waiting for transfers between devices, shards(): above += lax.ppermute(sending, 'mesh', [(q, q + gap) for q in parents])  14.4 us
    ppermute x9, waiting for transfers between devices, swap(): lax.ppermute(pieces[k], 'mode', exchange[k])  11.4 us
    pallas_call x1, Pallas kernels, leaf_down(): pl.pallas_call(leaf_down_kernel, out_shape=jax.ShapeDtypeStruct(solved.sh...  10.2 us
    ppermute x9, starting transfers between devices, swap(): lax.ppermute(pieces[k], 'mode', exchange[k])  8.14 us
    ppermute x1, starting transfers between devices, shards(): beside = lax.ppermute(sending, 'mesh', [(q, q - 1) for q in of_level[1]])  4.81 us
    ppermute x1, waiting for transfers between devices, shards(): lax.ppermute(update, 'mesh', [(q - 1, q) for q in of_level[1]])  4.13 us
    ppermute x2, starting transfers between devices, shards(): lax.ppermute(outgoing, 'mesh', [(q + gap, q) for q in of_level[height]])  3.36 us
  transfers between devices with their start and end apart: 21, of which 8 were waited for; matrix products, arithmetic and copies ran while one was open for 3% of the time, Pallas kernels for 1%

profile of v1, /device:TPU:9, one launch (start us, length us, event | category | flops | bytes accessed | tf_op | source)
XLA Modules:
  0.0 96.5 jit_solution(9532860903546146569)
XLA Ops:
  0.7 1.2 %copy-done.1 = f32[3,2,16,2560]{3,2,1,0:T(8,128)S(1)} copy-done((f32[3,2,16,2560]{3,2,1,0:T(8,128)S(1)}, f32[3,2,16,2560]{3,2,1,0:T(8,128)}, u32[]{:S(2)}) %copy-start.1) | copy-done | bytes 983064
  1.9 1.2 %copy-done.2 = f32[3,2,16,2560]{3,2,1,0:T(8,128)S(1)} copy-done((f32[3,2,16,2560]{3,2,1,0:T(8,128)S(1)}, f32[3,2,16,2560]{3,2,1,0:T(8,128)}, u32[]{:S(2)}) %copy-start.2) | copy-done | bytes 983064
  3.1 0.1 pack.1
  3.2 1.3 %collective-permute-start = (bf16[192,640]{1,0:T(8,128)(2,1)S(1)}, bf16[192,640]{1,0:T(8,128)(2,1)S(1)}, u32[]{:S(2)}, u32[]{:S(2)}) collective-permute-start(bf16[192,640]{1,0:T(8,128)(2,1)S(1)} %get-tuple-element.18), channel_id=1, source_target_pairs={{0,8},{8,0},{16,24},{24,16},{1,9},{9,1},{17,25},{25,17},{2,10},{10... | collective-permute-start | bytes 737288 | tf_op jit(solution)/shard_map/ppermute | solution.py:266
  4.5 1.2 %collective-permute-start.1 = (bf16[192,640]{1,0:T(8,128)(2,1)S(1)}, bf16[192,640]{1,0:T(8,128)(2,1)S(1)}, u32[]{:S(2)}, u32[]{:S(2)}) collective-permute-start(bf16[192,640]{1,0:T(8,128)(2,1)S(1)} %get-tuple-element.19), channel_id=1, source_target_pairs={{0,16},{8,24},{16,0},{24,8},{1,17},{9,25},{17,1},{25,9},{2,18},{10... | collective-permute-start | bytes 737288 | tf_op jit(solution)/shard_map/ppermute | solution.py:266
  5.7 0.2 collective-permute-start.2
  6.0 0.1 iota_add_fusion
  6.0 0.3 fusion.10
  6.4 0.1 select_multiply_fusion
  6.5 0.1 mul.71
  6.6 0.1 copy.11.fwd_ref
  6.7 0.1 fusion
  6.8 3.3 %collective-permute-done.refs_1_ = bf16[192,640]{1,0:T(8,128)(2,1)S(1)} collective-permute-done((bf16[192,640]{1,0:T(8,128)(2,1)S(1)}, bf16[192,640]{1,0:T(8,128)(2,1)S(1)}, u32[]{:S(2)}, u32[]{:S(2)}) %collective-permute-start) | collective-permute-done | bytes 245792 | tf_op jit(solution)/shard_map/ppermute | solution.py:266
  10.1 0.9 collective-permute-done.1.refs_2_
  11.1 5.3 %collective-permute-done.2.refs_3_ = bf16[192,640]{1,0:T(8,128)(2,1)S(1)} collective-permute-done((bf16[192,640]{1,0:T(8,128)(2,1)S(1)}, bf16[192,640]{1,0:T(8,128)(2,1)S(1)}, u32[]{:S(2)}, u32[]{:S(2)}) %collective-permute-start.2) | collective-permute-done | bytes 245792 | tf_op jit(solution)/shard_map/ppermute | solution.py:266
  16.4 0.8 transform.1
  17.2 1.2 %collective-permute-start.3 = (bf16[32,640]{1,0:T(8,128)(2,1)S(1)}, bf16[32,640]{1,0:T(8,128)(2,1)S(1)}, u32[]{:S(2)}, u32[]{:S(2)}) collective-permute-start(bf16[32,640]{1,0:T(8,128)(2,1)S(1)} %get-tuple-element.22), channel_id=1, source_target_pairs={{0,8},{8,0},{16,24},{24,16},{1,9},{9,1},{17,25},{25,17},{2,10},{10... | collective-permute-start | bytes 122888 | tf_op jit(solution)/shard_map/ppermute | solution.py:266
  18.5 0.3 collective-permute-start.4
  18.7 1.2 %collective-permute-start.5 = (bf16[32,640]{1,0:T(8,128)(2,1)S(1)}, bf16[32,640]{1,0:T(8,128)(2,1)S(1)}, u32[]{:S(2)}, u32[]{:S(2)}) collective-permute-start(bf16[32,640]{1,0:T(8,128)(2,1)S(1)} %get-tuple-element.24), channel_id=1, source_target_pairs={{0,24},{8,16},{16,8},{24,0},{1,25},{9,17},{17,9},{25,1},{2,26},{10... | collective-permute-start | bytes 122888 | tf_op jit(solution)/shard_map/ppermute | solution.py:266
  20.0 0.8 slice_bitcast_fusion.1
  20.7 0.6 collective-permute-done.4.refs_2_
  21.3 1.2 %collective-permute-done.5.refs_3_ = bf16[32,640]{1,0:T(8,128)(2,1)S(1)} collective-permute-done((bf16[32,640]{1,0:T(8,128)(2,1)S(1)}, bf16[32,640]{1,0:T(8,128)(2,1)S(1)}, u32[]{:S(2)}, u32[]{:S(2)}) %collective-permute-start.5) | collective-permute-done | bytes 40992 | tf_op jit(solution)/shard_map/ppermute | solution.py:266
  22.5 19.0 %leaf_up.1 = (f32[2,16,2560]{2,1,0:T(8,128)S(1)}, f32[2,16,128]{2,1,0:T(8,128)S(1)}) custom-call(s32[1]{0:T(128)} %bitcast.me_ref, s32[1,128]{1,0:T(1,128)S(1)} %get-tuple-element.38.rows_ref, f32[2,16,2560]{2,1,0:T(8,128)S(1)} %slice_bitcast_fusion.mag_ref, bf16[32,640]{1,0:T(8,128)(2,1)S(1)} %get-tuple-element.21.refs_0_, ...), custom_call_target="tpu_custom_call" | custom-call | tf_op jit(solution)/shard_map/leaf_up/pallas_call | solution.py:155
  41.5 1.3 %collective-permute-start.9 = (f32[2,16,128]{2,1,0:T(8,128)S(1)}, f32[2,16,128]{2,1,0:T(8,128)S(1)}, u32[]{:S(2)}, u32[]{:S(2)}) collective-permute-start(f32[2,16,128]{2,1,0:T(8,128)S(1)} %get-tuple-element.29), channel_id=1, source_target_pairs={{0,1},{2,3},{4,5},{6,7},{8,9},{10,11},{12,13},{14,15},{16,17},{18,... | collective-permute-start | bytes 49160 | tf_op jit(solution)/shard_map/ppermute | solution.py:302
  42.9 4.1 %collective-permute-done.9 = f32[2,16,128]{2,1,0:T(8,128)S(1)} collective-permute-done((f32[2,16,128]{2,1,0:T(8,128)S(1)}, f32[2,16,128]{2,1,0:T(8,128)S(1)}, u32[]{:S(2)}, u32[]{:S(2)}) %collective-permute-start.9) | collective-permute-done | bytes 16416 | tf_op jit(solution)/shard_map/ppermute | solution.py:302
  47.0 0.4 fusion.63
  47.4 0.4 fusion.47
  47.8 0.1 convolution_select_fusion.2
  47.9 0.7 collective-permute-start.10
  48.6 2.7 %collective-permute-start.11 = (f32[2,16,128]{2,1,0:T(8,128)S(1)}, f32[2,16,128]{2,1,0:T(8,128)S(1)}, u32[]{:S(2)}, u32[]{:S(2)}) collective-permute-start(f32[2,16,128]{2,1,0:T(8,128)S(1)} %convolution_select_fusion.2), channel_id=1, source_target_pairs={{3,2},{7,6},{11,10},{15,14},{19,18},{23,22},{27,26},{31,30}} | collective-permute-start | bytes 49160 | tf_op jit(solution)/shard_map/ppermute | solution.py:307
  51.4 0.8 collective-permute-done.11
  52.2 0.4 fusion.61
  52.5 0.4 fusion.45
  52.9 0.1 convolution_select_fusion.1
  53.1 0.7 collective-permute-start.12
  53.8 0.7 collective-permute-start.13
  54.5 0.4 fusion.59
  54.9 0.4 convolution_bitcast_fusion
  55.2 0.1 convolution_select_fusion
  55.4 0.7 collective-permute-start.14
  56.1 0.4 fusion.57
  56.5 0.2 fusion.55
  56.8 0.7 collective-permute-start.15
  57.4 0.1 convolution_convert_fusion.2
  57.6 0.3 fusion.42
  57.9 0.2 fusion.53
  58.1 0.7 collective-permute-start.16
  58.8 0.7 collective-permute-start.17
  59.5 0.1 convolution_convert_fusion.1
  59.6 0.3 fusion.40
  59.9 0.2 fusion.51
  60.1 0.7 collective-permute-start.18
  60.8 1.3 %collective-permute-start.19 = (bf16[2,16,128]{2,1,0:T(8,128)(2,1)S(1)}, bf16[2,16,128]{2,1,0:T(8,128)(2,1)S(1)}, u32[]{:S(2)}, u32[]{:S(2)}) collective-permute-start(bf16[2,16,128]{2,1,0:T(8,128)(2,1)S(1)} %convert_bitcast_fusion), channel_id=1, source_target_pairs={{2,3},{6,7},{10,11},{14,15},{18,19},{22,23},{26,27},{30,31}} | collective-permute-start | bytes 24584 | tf_op jit(solution)/shard_map/ppermute | solution.py:322
  62.1 1.3 %collective-permute-start.6 = (bf16[64,640]{1,0:T(8,128)(2,1)S(1)}, bf16[64,640]{1,0:T(8,128)(2,1)S(1)}, u32[]{:S(2)}, u32[]{:S(2)}) collective-permute-start(bf16[64,640]{1,0:T(8,128)(2,1)S(1)} %get-tuple-element.26), channel_id=1, source_target_pairs={{0,8},{8,0},{16,24},{24,16},{1,9},{9,1},{17,25},{25,17},{2,10},{10... | collective-permute-start | bytes 245768 | tf_op jit(solution)/shard_map/ppermute | solution.py:266
  63.4 0.2 collective-permute-start.7
  63.6 1.2 %collective-permute-start.8 = (bf16[64,640]{1,0:T(8,128)(2,1)S(1)}, bf16[64,640]{1,0:T(8,128)(2,1)S(1)}, u32[]{:S(2)}, u32[]{:S(2)}) collective-permute-start(bf16[64,640]{1,0:T(8,128)(2,1)S(1)} %get-tuple-element.28), channel_id=1, source_target_pairs={{0,24},{8,16},{16,8},{24,0},{1,25},{9,17},{17,9},{25,1},{2,26},{10... | collective-permute-start | bytes 245768 | tf_op jit(solution)/shard_map/ppermute | solution.py:266
  64.8 14.4 %collective-permute-done.19 = bf16[2,16,128]{2,1,0:T(8,128)(2,1)S(1)} collective-permute-done((bf16[2,16,128]{2,1,0:T(8,128)(2,1)S(1)}, bf16[2,16,128]{2,1,0:T(8,128)(2,1)S(1)}, u32[]{:S(2)}, u32[]{:S(2)}) %collective-permute-start.19) | collective-permute-done | bytes 8224 | tf_op jit(solution)/shard_map/ppermute | solution.py:322
  79.2 0.1 convolution_convert_fusion
  79.3 0.3 fusion.38
  79.6 0.3 fusion.49
  79.9 0.6 fusion.67
  80.5 4.8 %collective-permute-start.20 = (bf16[2,16,128]{2,1,0:T(8,128)(2,1)S(1)}, bf16[2,16,128]{2,1,0:T(8,128)(2,1)S(1)}, u32[]{:S(2)}, u32[]{:S(2)}) collective-permute-start(bf16[2,16,128]{2,1,0:T(8,128)(2,1)S(1)} %get-tuple-element.31), channel_id=1, source_target_pairs={{1,0},{3,2},{5,4},{7,6},{9,8},{11,10},{13,12},{15,14},{17,16},{19,... | collective-permute-start | bytes 24584 | tf_op jit(solution)/shard_map/ppermute | solution.py:334
  85.3 1.0 %spread.1 = f32[96,2560]{1,0:T(8,128)} custom-call(s32[1]{0:T(128)} %bitcast.me_ref, bf16[32,640]{1,0:T(8,128)(2,1)S(1)} %get-tuple-element.21.refs_0_, bf16[32,640]{1,0:T(8,128)(2,1)S(1)} %collective-permute-done.3.refs_1_, bf16[32,640]{1,0:T(8,128)(2,1)S(1)} %collective-permute-done.4.refs_2_, bf16[32,640]{1,0:T(8,128)(2,1)S(1)} %collective-permute-done.5.refs_3_, ...), custom_call_target="tpu_custom_call" | custom-call | tf_op jit(solution)/shard_map/spread/pallas_call | solution.py:230
  86.4 10.2 %leaf_down.1 = f32[2,16,2560]{2,1,0:T(8,128)} custom-call(s32[1,128]{1,0:T(1,128)S(1)} %get-tuple-element.38.rows_ref, f32[2,16,128]{2,1,0:T(8,128)S(1)} %select_convert_fusion.above_ref, f32[2,16,2560]{2,1,0:T(8,128)S(1)} %get-tuple-element.30.solved_ref, bf16[16,20,128,128]{3,2,1,0:T(8,128)(2,1)} %inv_hbm.1, bf16[16,128,2560]{2,1,0:T(8,128)(2,1)} %cpl_hbm.1), custom_call_target="tpu_custom_call" | custom-call | tf_op jit(solution)/shard_map/leaf_down/pallas_call | solution.py:201
  (41 shorter events, 0.2 us)
Async XLA Ops:
  0.6 46.4 %copy-start = (bf16[16,128,128]{2,1,0:T(8,128)(2,1)S(1)}, bf16[16,128,128]{2,1,0:T(8,128)(2,1)}, u32[]{:S(2)}) copy-start(bf16[16,128,128]{2,1,0:T(8,128)(2,1)} %param.12) | copy-start | bytes 1572868
  0.7 1.3 %copy-start.1 = (f32[3,2,16,2560]{3,2,1,0:T(8,128)S(1)}, f32[3,2,16,2560]{3,2,1,0:T(8,128)}, u32[]{:S(2)}) copy-start(f32[3,2,16,2560]{3,2,1,0:T(8,128)} %param.9) | copy-start | bytes 2949124
  1.9 1.2 %copy-start.2 = (f32[3,2,16,2560]{3,2,1,0:T(8,128)S(1)}, f32[3,2,16,2560]{3,2,1,0:T(8,128)}, u32[]{:S(2)}) copy-start(f32[3,2,16,2560]{3,2,1,0:T(8,128)} %param.8) | copy-start | bytes 2949124
  3.2 6.9 %collective-permute-start = (bf16[192,640]{1,0:T(8,128)(2,1)S(1)}, bf16[192,640]{1,0:T(8,128)(2,1)S(1)}, u32[]{:S(2)}, u32[]{:S(2)}) collective-permute-start(bf16[192,640]{1,0:T(8,128)(2,1)S(1)} %get-tuple-element.18), channel_id=1, source_target_pairs={{0,8},{8,0},{16,24},{24,16},{1,9},{9,1},{17,25},{25,17},{2,10},{10... | collective-permute-start | bytes 737288 | tf_op jit(solution)/shard_map/ppermute | solution.py:266
  4.5 6.6 %collective-permute-start.1 = (bf16[192,640]{1,0:T(8,128)(2,1)S(1)}, bf16[192,640]{1,0:T(8,128)(2,1)S(1)}, u32[]{:S(2)}, u32[]{:S(2)}) collective-permute-start(bf16[192,640]{1,0:T(8,128)(2,1)S(1)} %get-tuple-element.19), channel_id=1, source_target_pairs={{0,16},{8,24},{16,0},{24,8},{1,17},{9,25},{17,1},{25,9},{2,18},{10... | collective-permute-start | bytes 737288 | tf_op jit(solution)/shard_map/ppermute | solution.py:266
  5.7 10.7 %collective-permute-start.2 = (bf16[192,640]{1,0:T(8,128)(2,1)S(1)}, bf16[192,640]{1,0:T(8,128)(2,1)S(1)}, u32[]{:S(2)}, u32[]{:S(2)}) collective-permute-start(bf16[192,640]{1,0:T(8,128)(2,1)S(1)} %get-tuple-element.20), channel_id=1, source_target_pairs={{0,24},{8,16},{16,8},{24,0},{1,25},{9,17},{17,9},{25,1},{2,26},{10... | collective-permute-start | bytes 737288 | tf_op jit(solution)/shard_map/ppermute | solution.py:266
  17.2 3.5 %collective-permute-start.3 = (bf16[32,640]{1,0:T(8,128)(2,1)S(1)}, bf16[32,640]{1,0:T(8,128)(2,1)S(1)}, u32[]{:S(2)}, u32[]{:S(2)}) collective-permute-start(bf16[32,640]{1,0:T(8,128)(2,1)S(1)} %get-tuple-element.22), channel_id=1, source_target_pairs={{0,8},{8,0},{16,24},{24,16},{1,9},{9,1},{17,25},{25,17},{2,10},{10... | collective-permute-start | bytes 122888 | tf_op jit(solution)/shard_map/ppermute | solution.py:266
  18.5 2.9 %collective-permute-start.4 = (bf16[32,640]{1,0:T(8,128)(2,1)S(1)}, bf16[32,640]{1,0:T(8,128)(2,1)S(1)}, u32[]{:S(2)}, u32[]{:S(2)}) collective-permute-start(bf16[32,640]{1,0:T(8,128)(2,1)S(1)} %get-tuple-element.23), channel_id=1, source_target_pairs={{0,16},{8,24},{16,0},{24,8},{1,17},{9,25},{17,1},{25,9},{2,18},{10... | collective-permute-start | bytes 122888 | tf_op jit(solution)/shard_map/ppermute | solution.py:266
  18.7 3.8 %collective-permute-start.5 = (bf16[32,640]{1,0:T(8,128)(2,1)S(1)}, bf16[32,640]{1,0:T(8,128)(2,1)S(1)}, u32[]{:S(2)}, u32[]{:S(2)}) collective-permute-start(bf16[32,640]{1,0:T(8,128)(2,1)S(1)} %get-tuple-element.24), channel_id=1, source_target_pairs={{0,24},{8,16},{16,8},{24,0},{1,25},{9,17},{17,9},{25,1},{2,26},{10... | collective-permute-start | bytes 122888 | tf_op jit(solution)/shard_map/ppermute | solution.py:266
  22.5 24.5 %copy-start.4 = (f32[2,16,128]{2,1,0:T(8,128)S(1)}, f32[2,16,128]{2,1,0:T(8,128)}, u32[]{:S(2)}) copy-start(f32[2,16,128]{2,1,0:T(8,128)} %param.14) | copy-start | bytes 49156
  22.5 24.9 %copy-start.3 = (bf16[16,128,128]{2,1,0:T(8,128)(2,1)S(1)}, bf16[16,128,128]{2,1,0:T(8,128)(2,1)}, u32[]{:S(2)}) copy-start(bf16[16,128,128]{2,1,0:T(8,128)(2,1)} %param.13) | copy-start | bytes 1572868
  41.5 5.5 %collective-permute-start.9 = (f32[2,16,128]{2,1,0:T(8,128)S(1)}, f32[2,16,128]{2,1,0:T(8,128)S(1)}, u32[]{:S(2)}, u32[]{:S(2)}) collective-permute-start(f32[2,16,128]{2,1,0:T(8,128)S(1)} %get-tuple-element.29), channel_id=1, source_target_pairs={{0,1},{2,3},{4,5},{6,7},{8,9},{10,11},{12,13},{14,15},{16,17},{18,... | collective-permute-start | bytes 49160 | tf_op jit(solution)/shard_map/ppermute | solution.py:302
  47.9 3.4 %collective-permute-start.10 = (f32[2,16,128]{2,1,0:T(8,128)S(1)}, f32[2,16,128]{2,1,0:T(8,128)S(1)}, u32[]{:S(2)}, u32[]{:S(2)}) collective-permute-start(f32[2,16,128]{2,1,0:T(8,128)S(1)} %convolution_select_fusion.2), channel_id=1, source_target_pairs={{1,2},{5,6},{9,10},{13,14},{17,18},{21,22},{25,26},{29,30}} | collective-permute-start | bytes 49160 | tf_op jit(solution)/shard_map/ppermute | solution.py:306
  48.6 3.5 %collective-permute-start.11 = (f32[2,16,128]{2,1,0:T(8,128)S(1)}, f32[2,16,128]{2,1,0:T(8,128)S(1)}, u32[]{:S(2)}, u32[]{:S(2)}) collective-permute-start(f32[2,16,128]{2,1,0:T(8,128)S(1)} %convolution_select_fusion.2), channel_id=1, source_target_pairs={{3,2},{7,6},{11,10},{15,14},{19,18},{23,22},{27,26},{31,30}} | collective-permute-start | bytes 49160 | tf_op jit(solution)/shard_map/ppermute | solution.py:307
  53.1 1.4 %collective-permute-start.12 = (f32[2,16,128]{2,1,0:T(8,128)S(1)}, f32[2,16,128]{2,1,0:T(8,128)S(1)}, u32[]{:S(2)}, u32[]{:S(2)}) collective-permute-start(f32[2,16,128]{2,1,0:T(8,128)S(1)} %convolution_select_fusion.1), channel_id=1, source_target_pairs={{2,4},{10,12},{18,20},{26,28}} | collective-permute-start | bytes 49160 | tf_op jit(solution)/shard_map/ppermute | solution.py:306
  53.8 0.7 collective-permute-start.13
  55.4 0.7 collective-permute-start.14
  56.8 0.7 collective-permute-start.15
  58.1 1.3 %collective-permute-start.16 = (bf16[2,16,128]{2,1,0:T(8,128)(2,1)S(1)}, bf16[2,16,128]{2,1,0:T(8,128)(2,1)S(1)}, u32[]{:S(2)}, u32[]{:S(2)}) collective-permute-start(bf16[2,16,128]{2,1,0:T(8,128)(2,1)S(1)} %get-tuple-element.33), channel_id=1, source_target_pairs={{4,2},{12,10},{20,18},{28,26}} | collective-permute-start | bytes 24584 | tf_op jit(solution)/shard_map/ppermute | solution.py:321
  58.8 0.7 collective-permute-start.17
  60.1 4.7 %collective-permute-start.18 = (bf16[2,16,128]{2,1,0:T(8,128)(2,1)S(1)}, bf16[2,16,128]{2,1,0:T(8,128)(2,1)S(1)}, u32[]{:S(2)}, u32[]{:S(2)}) collective-permute-start(bf16[2,16,128]{2,1,0:T(8,128)(2,1)S(1)} %convert_bitcast_fusion), channel_id=1, source_target_pairs={{2,1},{6,5},{10,9},{14,13},{18,17},{22,21},{26,25},{30,29}} | collective-permute-start | bytes 24584 | tf_op jit(solution)/shard_map/ppermute | solution.py:321
  60.8 18.4 %collective-permute-start.19 = (bf16[2,16,128]{2,1,0:T(8,128)(2,1)S(1)}, bf16[2,16,128]{2,1,0:T(8,128)(2,1)S(1)}, u32[]{:S(2)}, u32[]{:S(2)}) collective-permute-start(bf16[2,16,128]{2,1,0:T(8,128)(2,1)S(1)} %convert_bitcast_fusion), channel_id=1, source_target_pairs={{2,3},{6,7},{10,11},{14,15},{18,19},{22,23},{26,27},{30,31}} | collective-permute-start | bytes 24584 | tf_op jit(solution)/shard_map/ppermute | solution.py:322
  62.1 23.2 %collective-permute-start.6 = (bf16[64,640]{1,0:T(8,128)(2,1)S(1)}, bf16[64,640]{1,0:T(8,128)(2,1)S(1)}, u32[]{:S(2)}, u32[]{:S(2)}) collective-permute-start(bf16[64,640]{1,0:T(8,128)(2,1)S(1)} %get-tuple-element.26), channel_id=1, source_target_pairs={{0,8},{8,0},{16,24},{24,16},{1,9},{9,1},{17,25},{25,17},{2,10},{10... | collective-permute-start | bytes 245768 | tf_op jit(solution)/shard_map/ppermute | solution.py:266
  63.4 21.9 %collective-permute-start.7 = (bf16[64,640]{1,0:T(8,128)(2,1)S(1)}, bf16[64,640]{1,0:T(8,128)(2,1)S(1)}, u32[]{:S(2)}, u32[]{:S(2)}) collective-permute-start(bf16[64,640]{1,0:T(8,128)(2,1)S(1)} %get-tuple-element.27), channel_id=1, source_target_pairs={{0,16},{8,24},{16,0},{24,8},{1,17},{9,25},{17,1},{25,9},{2,18},{10... | collective-permute-start | bytes 245768 | tf_op jit(solution)/shard_map/ppermute | solution.py:266
  63.6 21.7 %collective-permute-start.8 = (bf16[64,640]{1,0:T(8,128)(2,1)S(1)}, bf16[64,640]{1,0:T(8,128)(2,1)S(1)}, u32[]{:S(2)}, u32[]{:S(2)}) collective-permute-start(bf16[64,640]{1,0:T(8,128)(2,1)S(1)} %get-tuple-element.28), channel_id=1, source_target_pairs={{0,24},{8,16},{16,8},{24,0},{1,25},{9,17},{17,9},{25,1},{2,26},{10... | collective-permute-start | bytes 245768 | tf_op jit(solution)/shard_map/ppermute | solution.py:266
  80.5 5.9 %collective-permute-start.20 = (bf16[2,16,128]{2,1,0:T(8,128)(2,1)S(1)}, bf16[2,16,128]{2,1,0:T(8,128)(2,1)S(1)}, u32[]{:S(2)}, u32[]{:S(2)}) collective-permute-start(bf16[2,16,128]{2,1,0:T(8,128)(2,1)S(1)} %get-tuple-element.31), channel_id=1, source_target_pairs={{1,0},{3,2},{5,4},{7,6},{9,8},{11,10},{13,12},{15,14},{17,16},{19,... | collective-permute-start | bytes 24584 | tf_op jit(solution)/shard_map/ppermute | solution.py:334

commit v2 on v1

v2 whole, which is shorter than its diff:
```python
import functools

import jax
import jax.numpy as jnp
from jax import lax
from jax.experimental import pallas as pl
from jax.experimental.pallas import tpu as pltpu
from jax.sharding import PartitionSpec as P

NPHI = 192
DT_STEP = 0.5
VMEM = pltpu.VMEM
SMEM = pltpu.SMEM
BF16 = jnp.bfloat16
F32 = jnp.float32
NT = (((1,), (1,)), ((), ()))
NN = (((1,), (0,)), ((), ()))
SMALL = 8 * 2**20
LARGE = 8 * 2**20
COMPOSE = 8 * 2**20


def dot(a, b, dims=NN, precision=None):
    return lax.dot_general(a, b, dims, precision=precision, preferred_element_type=F32)


def tables_kernel(modes, me_ref, fwd_ref, bwd_ref):
    def phase(shape, angle_axis):
        angle = lax.broadcasted_iota(jnp.int32, shape, angle_axis)
        at = lax.broadcasted_iota(jnp.int32, shape, 1 - angle_axis)
        step, kind, mode = at // (2 * modes), (at // modes) % 2, at % modes
        order = jnp.bitwise_xor(step, me_ref[0]) * modes + mode
        turn = (angle * order).astype(F32)
        turn = turn - NPHI * jnp.floor((turn + 0.5) * (1.0 / NPHI))
        return turn * (2.0 * jnp.pi / NPHI), kind, order

    at, kind, _ = phase(fwd_ref.shape, 0)
    fwd_ref[...] = jnp.where(kind == 0, jnp.cos(at), jnp.sin(at)).astype(BF16)
    at, kind, order = phase(bwd_ref.shape, 1)
    weight = jnp.where(order == 0, 1.0, 2.0) / NPHI
    bwd_ref[...] = (jnp.where(kind == 0, jnp.cos(at), jnp.sin(at)) * weight).astype(BF16)


def tables(me, groups, modes):
    rows = groups * 2 * modes
    return pl.pallas_call(
        functools.partial(tables_kernel, modes),
        out_shape=[jax.ShapeDtypeStruct((NPHI, rows), BF16), jax.ShapeDtypeStruct((rows, NPHI), BF16)],
        in_specs=[pl.BlockSpec(memory_space=SMEM)],
        out_specs=[pl.BlockSpec(memory_space=VMEM)] * 2,
        compiler_params=pltpu.CompilerParams(vmem_limit_bytes=SMALL),
        name="tables",
    )(me)


def pack_kernel(groups, me_ref, v_ref, b_ref, *outs):
    rows, width = v_ref.shape[0], outs[0].shape[1]
    for k in range(groups):
        span = pl.ds(pl.multiple_of(jnp.bitwise_xor(me_ref[0], k) * width, 128), width)
        outs[k][:rows, :] = v_ref[:, span].astype(BF16)
        outs[k][rows:, :] = b_ref[:, span].astype(BF16)


def pack(me, velocity, magnetic, groups):
    rows, nodes = velocity.shape
    width = nodes // groups
    return pl.pallas_call(
        functools.partial(pack_kernel, groups),
        out_shape=[jax.ShapeDtypeStruct((2 * rows, width), BF16)] * groups,
        in_specs=[pl.BlockSpec(memory_space=SMEM)] + [pl.BlockSpec(memory_space=VMEM)] * 2,
        out_specs=[pl.BlockSpec(memory_space=VMEM)] * groups,
        compiler_params=pltpu.CompilerParams(vmem_limit_bytes=16 * 2**20),
        name="pack",
    )(me, velocity, magnetic)


def transform_kernel(groups, fwd_ref, bwd_ref, *refs):
    ins, azi, rest = refs[:groups], refs[groups : 2 * groups], refs[2 * groups :]
    rows = ins[0].shape[0] // 6
    fwd, bwd = fwd_ref[...], bwd_ref[...]
    phys = []
    for field in range(6):
        coef = jnp.concatenate([r[field * rows : (field + 1) * rows, :] for r in ins], axis=0)
        phys.append(dot(fwd, coef))
    v, b = phys[:3], phys[3:]
    for c in range(3):
        p, q = (c + 1) % 3, (c + 2) % 3
        crossed = (v[p] * b[q] - v[q] * b[p]).astype(BF16)
        terms = dot(bwd, crossed).astype(BF16)
        for k in range(groups):
            block = terms[k * rows : (k + 1) * rows, :]
            if c == 1:
                azi[k][...] = block
            else:
                at = 0 if c == 0 else rows
                rest[k][at : at + rows, :] = block


def transform(fwd, bwd, pieces):
    groups = len(pieces)
    rows, width = pieces[0].shape
    rows = rows // 6
    out = pl.pallas_call(
        functools.partial(transform_kernel, groups),
        out_shape=[jax.ShapeDtypeStruct((rows, width), BF16)] * groups
        + [jax.ShapeDtypeStruct((2 * rows, width), BF16)] * groups,
        in_specs=[pl.BlockSpec(memory_space=VMEM)] * (2 + groups),
        out_specs=[pl.BlockSpec(memory_space=VMEM)] * (2 * groups),
        compiler_params=pltpu.CompilerParams(vmem_limit_bytes=24 * 2**20),
        name="transform",
    )(fwd, bwd, *pieces)
    return out[:groups], out[groups:]


def one_hot(rows_ref):
    n = rows_ref.shape[1]
    return lax.broadcasted_iota(jnp.int32, (n, n), 0) == rows_ref[0:1, :]


def compose_kernel(inv_hbm, cpl_hbm, square_ref, joint_ref, inv_v, cpl_v, sems):
    modes, front, nodes = joint_ref.shape
    blocks, size = inv_v.shape[1], inv_v.shape[2]
    depth = inv_v.shape[0]
    zero = jnp.zeros((size, size), BF16)

    def copies(m):
        slot = m % depth
        return (
            pltpu.make_async_copy(inv_hbm.at[m], inv_v.at[slot], sems.at[0, slot]),
            pltpu.make_async_copy(cpl_hbm.at[m], cpl_v.at[slot], sems.at[1, slot]),
        )

    for m in range(depth):
        for copy in copies(m):
            copy.start()

    def one_mode(m, carry):
        slot = m % depth
        for copy in copies(m):
            copy.wait()
        for b in range(0, blocks, 2):
            first, second = inv_v[slot, b], inv_v[slot, b + 1]
            weights = jnp.concatenate(
                [jnp.concatenate([first, zero], axis=1), jnp.concatenate([zero, second], axis=1)],
                axis=0,
            )
            span = slice(b * size, (b + 2) * size)
            rows = jnp.concatenate(
                [cpl_v[slot, :, span], jnp.concatenate([first.T, second.T], axis=1)], axis=0
            )
            out = dot(rows, weights).astype(BF16)
            joint_ref[m, :, span] = out[:front]
            square_ref[m, b] = out[front:, :size]
            square_ref[m, b + 1] = out[front:, size:]

        @pl.when(m + depth < modes)
        def _():
            for copy in copies(m + depth):
                copy.start()

        return carry

    lax.fori_loop(0, modes, one_mode, 0)


def compose(inverse, coupling, depth=4):
    modes, blocks, size, _ = inverse.shape
    front, nodes = coupling.shape[1:]
    return pl.pallas_call(
        compose_kernel,
        out_shape=[
            jax.ShapeDtypeStruct(inverse.shape, BF16),
            jax.ShapeDtypeStruct(coupling.shape, BF16),
        ],
        in_specs=[pl.BlockSpec(memory_space=pl.ANY)] * 2,
        out_specs=[pl.BlockSpec(memory_space=VMEM)] * 2,
        scratch_shapes=[
            VMEM((depth, blocks, size, size), BF16),
            VMEM((depth, front, nodes), BF16),
            pltpu.SemaphoreType.DMA((2, depth)),
        ],
        compiler_params=pltpu.CompilerParams(vmem_limit_bytes=COMPOSE),
        cost_estimate=pl.CostEstimate(
            flops=4 * modes * nodes * size * (front + size),
            bytes_accessed=4 * (inverse.size + coupling.size),
            transcendentals=0,
        ),
        name="compose",
    )(inverse, coupling)


def leaf_up_kernel(groups, me_ref, rows_ref, mag_ref, joint_ref, *refs):
    pieces = refs[:groups]
    source_ref, update_ref, turned_v = refs[groups:]
    modes, front, nodes = joint_ref.shape
    width = nodes // groups
    for k in range(groups):
        span = pl.ds(pl.multiple_of(jnp.bitwise_xor(me_ref[0], k) * width, 128), width)
        for a in range(2):
            term = pieces[k][a * modes : (a + 1) * modes, :].astype(F32)
            source_ref[a, :, span] = mag_ref[0, a, :, span] + DT_STEP * term
    turned_v[...] = source_ref[...].reshape(2 * modes, nodes).T.astype(BF16)
    turned = turned_v[...]
    lane = lax.broadcasted_iota(jnp.int32, (front, 2 * modes), 1) % modes

    def one_mode(m, total):
        return total + jnp.where(lane == m, dot(joint_ref[m], turned), 0.0)

    total = lax.fori_loop(0, modes, one_mode, jnp.zeros((front, 2 * modes), F32), unroll=2)
    select = one_hot(rows_ref).astype(F32)
    update_ref[...] = dot(total.T, select, precision=lax.Precision.HIGHEST).reshape(update_ref.shape)


def leaf_up(me, rows, magnetic, pieces, joint):
    modes, front, nodes = joint.shape
    groups = len(pieces)
    whole = pl.BlockSpec(memory_space=VMEM)
    return pl.pallas_call(
        functools.partial(leaf_up_kernel, groups),
        grid=(1,),
        out_shape=[
            jax.ShapeDtypeStruct((2, modes, nodes), F32),
            jax.ShapeDtypeStruct((2, modes, front), F32),
        ],
        in_specs=[
            pl.BlockSpec(memory_space=SMEM),
            whole,
            pl.BlockSpec((1, 2, modes, nodes), lambda i: (1, 0, 0, 0)),
        ]
        + [whole] * (1 + groups),
        out_specs=[whole] * 2,
        scratch_shapes=[VMEM((nodes, 2 * modes), BF16)],
        compiler_params=pltpu.CompilerParams(vmem_limit_bytes=LARGE),
        cost_estimate=pl.CostEstimate(
            flops=128 * modes * nodes * front, bytes_accessed=2 * joint.size, transcendentals=0
        ),
        name="leaf_up",
    )(me, rows, magnetic, joint, *pieces)


def leaf_local_kernel(source_ref, square_ref, out_ref):
    modes, blocks, size, _ = square_ref.shape
    nodes = blocks * size
    zero = jnp.zeros((2, size), BF16)

    def one_mode(m, carry):
        source = source_ref[:, pl.ds(m, 1), :].reshape(2, nodes).astype(BF16)
        parts = []
        for b in range(0, blocks, 2):
            one = source[:, b * size : (b + 1) * size]
            two = source[:, (b + 1) * size : (b + 2) * size]
            left = jnp.concatenate(
                [jnp.concatenate([one, zero], axis=1), jnp.concatenate([zero, two], axis=1)], axis=0
            )
            pair = dot(left, square_ref[m, b : b + 2].reshape(2 * size, size))
            parts += [pair[:2], pair[2:]]
        out_ref[:, pl.ds(m, 1), :] = jnp.concatenate(parts, axis=1).reshape(2, 1, nodes)
        return carry

    lax.fori_loop(0, modes, one_mode, 0, unroll=2)


def leaf_local(source, square):
    whole = pl.BlockSpec(memory_space=VMEM)
    return pl.pallas_call(
        leaf_local_kernel,
        out_shape=jax.ShapeDtypeStruct(source.shape, F32),
        in_specs=[whole] * 2,
        out_specs=whole,
        compiler_params=pltpu.CompilerParams(vmem_limit_bytes=LARGE),
        cost_estimate=pl.CostEstimate(
            flops=128 * square.size, bytes_accessed=2 * square.size, transcendentals=0
        ),
        name="leaf_local",
    )(source, square)


def leaf_down_kernel(own_ref, rows_ref, here_ref, beside_ref, local_ref, joint_ref, out_ref, x_v):
    modes, front, nodes = joint_ref.shape
    select = one_hot(rows_ref).astype(F32).astype(BF16)
    above = jnp.where(own_ref[0] == 1, here_ref[...].astype(F32), beside_ref[...].astype(F32))
    x_v[...] = dot(above.reshape(2 * modes, front).astype(BF16), select, NT).reshape(2, modes, front)
    zero = jnp.zeros((2, front), F32)

    def two_modes(i, carry):
        one = x_v[:, pl.ds(2 * i, 1), :].reshape(2, front)
        two = x_v[:, pl.ds(2 * i + 1, 1), :].reshape(2, front)
        left = jnp.concatenate(
            [jnp.concatenate([one, zero], axis=1), jnp.concatenate([zero, two], axis=1)], axis=0
        ).astype(BF16)
        out = dot(left, joint_ref[pl.ds(2 * i, 2)].reshape(2 * front, nodes))
        for half in range(2):
            place = pl.ds(2 * i + half, 1)
            value = local_ref[:, place, :].reshape(2, nodes) - out[2 * half : 2 * half + 2]
            out_ref[:, place, :] = value.reshape(2, 1, nodes)
        return carry

    lax.fori_loop(0, modes // 2, two_modes, 0, unroll=2)


def leaf_down(own, rows, here, beside, local, joint):
    whole = pl.BlockSpec(memory_space=VMEM)
    return pl.pallas_call(
        leaf_down_kernel,
        out_shape=jax.ShapeDtypeStruct(local.shape, F32),
        in_specs=[pl.BlockSpec(memory_space=SMEM)] + [whole] * 5,
        out_specs=whole,
        scratch_shapes=[VMEM(here.shape, F32)],
        compiler_params=pltpu.CompilerParams(vmem_limit_bytes=LARGE),
        name="leaf_down",
    )(own, rows, here, beside, local, joint)


def spread_kernel(groups, me_ref, *refs):
    azi, rest, out_ref = refs[:groups], refs[groups : 2 * groups], refs[2 * groups]
    rows, width = azi[0].shape
    for k in range(groups):
        span = pl.ds(pl.multiple_of(jnp.bitwise_xor(me_ref[0], k) * width, 128), width)
        out_ref[:rows, span] = rest[k][:rows, :].astype(F32)
        out_ref[rows : 2 * rows, span] = azi[k][...].astype(F32)
        out_ref[2 * rows :, span] = rest[k][rows:, :].astype(F32)


def spread(me, azi, rest):
    groups = len(azi)
    rows, width = azi[0].shape
    return pl.pallas_call(
        functools.partial(spread_kernel, groups),
        out_shape=jax.ShapeDtypeStruct((3 * rows, groups * width), F32),
        in_specs=[pl.BlockSpec(memory_space=SMEM)] + [pl.BlockSpec(memory_space=VMEM)] * (2 * groups),
        out_specs=pl.BlockSpec(memory_space=VMEM),
        compiler_params=pltpu.CompilerParams(vmem_limit_bytes=16 * 2**20),
        name="spread",
    )(me, *azi, *rest)


def fronts_kernel(rows_ref, inv_ref, cpl_ref, out_ref):
    modes, size, _ = inv_ref.shape
    out_ref[0] = inv_ref[...]
    select = one_hot(rows_ref).astype(F32).T.astype(BF16)
    for m in range(modes):
        out_ref[1, m] = dot(select, cpl_ref[m]).astype(BF16)


def fronts(rows, inverse, coupling):
    return pl.pallas_call(
        fronts_kernel,
        out_shape=jax.ShapeDtypeStruct((2,) + inverse.shape, BF16),
        in_specs=[pl.BlockSpec(memory_space=VMEM)] * 3,
        out_specs=pl.BlockSpec(memory_space=VMEM),
        compiler_params=pltpu.CompilerParams(vmem_limit_bytes=SMALL),
        name="fronts",
    )(rows, inverse, coupling)


def apply_rows(x, matrix):
    modes, size, _ = matrix.shape
    wide = dot(x, matrix.reshape(modes * size, size), NT)
    row = lax.broadcasted_iota(jnp.int32, x.shape, 0) % modes
    total = jnp.zeros(x.shape, F32)
    for m in range(modes):
        total += jnp.where(row == m, wide[:, m * size : (m + 1) * size], 0.0)
    return total


def apply_columns(x, matrix):
    modes, size, _ = matrix.shape
    row = lax.broadcasted_iota(jnp.int32, x.shape, 0) % modes
    x = x.astype(F32)
    wide = jnp.concatenate([jnp.where(row == m, x, 0.0).astype(BF16) for m in range(modes)], axis=1)
    return dot(wide, matrix.reshape(modes * size, size))


def flat(ref):
    return ref[...].reshape(ref.shape[0] * ref.shape[1], ref.shape[2])


def rise_kernel(one_ref, two_ref, source_ref, front_ref, reduced_ref, outgoing_ref):
    g = (flat(source_ref) - (flat(one_ref) + flat(two_ref))).astype(BF16)
    reduced = apply_rows(g, front_ref[0]).astype(BF16)
    reduced_ref[...] = reduced.astype(F32).reshape(reduced_ref.shape)
    outgoing_ref[...] = apply_rows(reduced, front_ref[1]).reshape(outgoing_ref.shape)


def small_call(kernel, name, outs, args, scalars=0):
    return pl.pallas_call(
        kernel,
        out_shape=outs,
        in_specs=[pl.BlockSpec(memory_space=SMEM)] * scalars
        + [pl.BlockSpec(memory_space=VMEM)] * (len(args) - scalars),
        out_specs=[pl.BlockSpec(memory_space=VMEM)] * len(outs),
        compiler_params=pltpu.CompilerParams(vmem_limit_bytes=SMALL),
        name=name,
    )(*args)


def crown_kernel(high_ref, one_ref, two_ref, reduced_ref, front_ref, fa_ref, sa_ref, fb_ref, sb_ref, x_ref, x16_ref, far_ref):
    def solve(f_mid, s_mid, f_top, s_top, send_mid):
        g = (flat(s_mid) - (flat(one_ref) + flat(two_ref))).astype(BF16)
        mid = apply_rows(g, f_mid[0]).astype(BF16)
        g = (flat(s_top) - apply_rows(mid, f_mid[1])).astype(BF16)
        top = apply_columns(apply_rows(g, f_top[0]).astype(BF16), f_top[0])
        residue = mid.astype(F32) - apply_columns(top.astype(BF16), f_mid[1])
        x_mid = apply_columns(residue.astype(BF16), f_mid[0])
        far_ref[...] = (x_mid if send_mid else top).reshape(far_ref.shape)
        residue = flat(reduced_ref) - apply_columns(x_mid.astype(BF16), front_ref[1])
        x = apply_columns(residue.astype(BF16), front_ref[0])
        x_ref[...] = x.reshape(x_ref.shape)
        x16_ref[...] = x.astype(BF16).reshape(x_ref.shape)

    @pl.when(high_ref[0] == 0)
    def _():
        solve(fa_ref, sa_ref, fb_ref, sb_ref, False)

    @pl.when(high_ref[0] != 0)
    def _():
        solve(fb_ref, sb_ref, fa_ref, sa_ref, True)


def sink_kernel(one_ref, two_ref, reduced_ref, front_ref, x_ref, x16_ref):
    above = (flat(one_ref).astype(F32) + flat(two_ref).astype(F32)).astype(BF16)
    residue = flat(reduced_ref) - apply_columns(above, front_ref[1])
    x = apply_columns(residue.astype(BF16), front_ref[0])
    x_ref[...] = x.reshape(x_ref.shape)
    x16_ref[...] = x.astype(BF16).reshape(x_ref.shape)


def level_of(q, levels):
    return levels + 1 if q == 0 else (q & -q).bit_length()


def choose_kernel(level_ref, *refs):
    for at, ref in enumerate(refs[:-1]):

        @pl.when(level_ref[0] == at)
        def _(ref=ref):
            refs[-1][...] = ref[...]


def shards(
    velocity,
    magnetic,
    leaf_inverse,
    leaf_coupling,
    separator_inverse,
    separator_coupling,
    separator_source,
    front_rows,
):
    groups = lax.axis_size("mode")
    partitions = lax.axis_size("mesh")
    levels = partitions.bit_length() - 1
    modes, nodes = velocity.shape[2], velocity.shape[3]
    here = lax.axis_index("mode")
    me = here.reshape(1).astype(jnp.int32)
    position = lax.axis_index("mesh")
    exchange = [[(g, g ^ k) for g in range(groups)] for k in range(groups)]
    low, mid, high = partitions // 4, partitions // 2, 3 * partitions // 4

    def swap(pieces):
        return [pieces[0]] + [
            lax.ppermute(pieces[k], "mode", exchange[k]) for k in range(1, groups)
        ]

    def hop(value, pairs):
        return lax.ppermute(value, "mesh", pairs)

    packed = pack(me, velocity.reshape(6 * modes, nodes), magnetic.reshape(6 * modes, nodes), groups)
    spread_in = swap(packed)
    fwd, bwd = tables(me, groups, modes)
    rows_leaf, rows_front = front_rows[0, 0:1], front_rows[0, 1:2]
    front = fronts(rows_front, separator_inverse, separator_coupling)
    to_a, to_b = [(mid, low), (0, high)], [(mid, high), (0, low)]
    front_a, front_b = hop(front, to_a), hop(front, to_b)
    source_a, source_b = hop(separator_source, to_a), hop(separator_source, to_b)
    square, joint = compose(leaf_inverse, leaf_coupling)
    azi, rest = transform(fwd, bwd, spread_in)
    azi = swap(azi)
    rest = swap(rest)
    source, update = leaf_up(me, rows_leaf, magnetic, azi, joint)
    local = leaf_local(source, square)
    nonlinear = spread(me, azi, rest).reshape(3, 2, modes, nodes)

    of_level = [[q for q in range(partitions) if level_of(q, levels) == h] for h in range(levels + 2)]
    wide = jax.ShapeDtypeStruct(separator_source.shape, F32)
    half = jax.ShapeDtypeStruct(separator_source.shape, BF16)
    reduced = [None] * (levels + 1)
    one, two = update, hop(update, [(q - 1, q) for q in of_level[1]])
    for height in range(1, levels):
        if height > 1:
            gap = 2 ** (height - 2)
            one = hop(outgoing, [(q - gap, q) for q in of_level[height]])
            two = hop(outgoing, [(q + gap, q) for q in of_level[height]])
        reduced[height], outgoing = small_call(
            rise_kernel, "rise", [wide, wide], [one, two, separator_source, front]
        )
    other = hop(outgoing, [(low, high), (high, low)])
    is_high = (position == high).astype(jnp.int32).reshape(1)
    x, x16, far = small_call(
        crown_kernel,
        "crown",
        [wide, half, wide],
        [is_high, outgoing, other, reduced[levels - 1], front, front_a, source_a, front_b, source_b],
        scalars=1,
    )
    answers = [(levels - 1, x)]
    for height in range(levels - 2, 0, -1):
        gap = 2 ** (height - 1)
        one = hop(x16, [(q, q - gap) for q in of_level[height + 1]])
        two = hop(x16, [(q, q + gap) for q in of_level[height + 1]])
        x, x16 = small_call(sink_kernel, "sink", [wide, half], [one, two, reduced[height], front])
        answers.append((height, x))
    far = hop(far, [(low, 0), (high, mid)])
    beside = hop(x16, [(q, q - 1) for q in of_level[1]])
    level_here = sum((position % 2**t == 0).astype(jnp.int32) for t in range(1, levels + 1)) + 1
    own = (level_here == 1).astype(jnp.int32).reshape(1)
    azimuthal = leaf_down(own, rows_leaf, x16, beside, local, joint)
    answers.reverse()
    place = (jnp.minimum(level_here, levels) - 1).reshape(1)
    (solution,) = small_call(
        choose_kernel, "choose", [wide], [place] + [x for _, x in answers] + [far], scalars=1
    )
    return (nonlinear, azimuthal, solution)


def solution(mesh):
    in_specs = (
        P(None, None, "mode", "mesh"),
        P(None, None, "mode", "mesh"),
        P("mode", "mesh", None, None),
        P("mode", None, "mesh"),
        P("mode", "mesh", None),
        P("mode", "mesh", None),
        P(None, "mode", "mesh"),
        P("mesh", None, None),
    )
    out_specs = (P(None, None, "mode", "mesh"), P(None, "mode", "mesh"), P(None, "mode", "mesh"))
    return jax.shard_map(shards, mesh=mesh, in_specs=in_specs, out_specs=out_specs, check_vma=False)
```

time: 97 us -> 110 us (1.13)
  local copies, waits for them, and re-layouts: 3.47 us -> 31.5 us
  waiting for transfers between devices: 30.7 us -> 19.9 us
  matrix products: 5.28 us -> 0 us
  Pallas kernels: 31.2 us -> 34.1 us
  other arithmetic: 1.35 us -> 0 us
  starting transfers between devices: 23.6 us -> 22.5 us
    unnamed x10 -> x70, local copies, waits for them, and re-layouts: 2.47 us -> 30.3 us
    ppermute x12, waiting for transfers between devices: 19.3 us -> 11.5 us  [hop(): return lax.ppermute(value, 'mesh', pairs)]
    dot_general x20 -> x0, matrix products: 5.28 us -> none  [the longest x4 1.48 us: settle(): jnp.einsum('mij,cmj->cmi', separator_inverse, (separator_source - arrived...]
    ppermute x9, waiting for transfers between devices: 11.4 us -> 8.41 us  [swap(): lax.ppermute(pieces[k], 'mode', exchange[k])]
    pallas_call x2 -> x11, Pallas kernels: 29.2 us -> 30.5 us  [the longest x1 15.2 us: compose(): pl.pallas_call(compose_kernel, out_shape=[jax.ShapeDtypeStruct(inverse.sh...]
    squeeze x1, local copies, waits for them, and re-layouts: 0.02 us -> 1.26 us  [shards(): rows_leaf, rows_front = (front_rows[0, 0:1], front_rows[0, 1:2])]
  transfers between devices with their start and end apart: 21 -> 21, of which waited for: 8 -> 5; matrix products, arithmetic and copies ran while one was open for 3% -> 0% of each run, Pallas kernels for 1% -> 30%
where the time goes in v2:
time: 110 us; the launch traced here: 109 us
  Pallas kernels  34.1 us (31%)
  local copies, waits for them, and re-layouts  31.5 us (29%)
  starting transfers between devices  22.5 us (20%)
  waiting for transfers between devices  19.9 us (18%)
    unnamed x70, local copies, waits for them, and re-layouts  30.3 us
    pallas_call x1, Pallas kernels, compose(): pl.pallas_call(compose_kernel, out_shape=[jax.ShapeDtypeStruct(inverse.sh...  15.2 us
    ppermute x12, starting transfers between devices, hop(): return lax.ppermute(value, 'mesh', pairs)  14.5 us
    ppermute x12, waiting for transfers between devices, hop(): return lax.ppermute(value, 'mesh', pairs)  11.5 us
    ppermute x9, waiting for transfers between devices, swap(): lax.ppermute(pieces[k], 'mode', exchange[k])  8.41 us
    ppermute x9, starting transfers between devices, swap(): lax.ppermute(pieces[k], 'mode', exchange[k])  8.01 us
    pallas_call x1, Pallas kernels, leaf_up(): pl.pallas_call(functools.partial(leaf_up_kernel, groups), grid=(1,), out_...  4.68 us
    pallas_call x5, Pallas kernels, small_call(): pl.pallas_call(kernel, out_shape=outs, in_specs=[pl.BlockSpec(memory_spac...  4.29 us
  transfers between devices with their start and end apart: 21, of which 5 were waited for; matrix products, arithmetic and copies ran while one was open for 0% of the time, Pallas kernels for 30%

profile of v2, /device:TPU:9, one launch (start us, length us, event | category | flops | bytes accessed | tf_op | source)
XLA Modules:
  0.0 109.2 jit_solution(5617057827306788709)
XLA Ops:
  0.6 1.3 %slice_bitcast_fusion = (s32[1,128]{1,0:T(1,128)S(1)}, s32[1,128]{1,0:T(1,128)}) fusion(s32[1,2,128]{2,1,0:T(2,128)} %param.15), kind=kLoop, calls=%fused_computation | loop fusion | bytes 2048 | tf_op jit(solution)/shard_map/squeeze | solution.py:471
  1.9 1.0 copy-done.9
  2.9 1.0 copy-done.10
  4.0 0.4 fronts.1.front_ref
  4.4 0.7 collective-permute-start.13
  5.1 0.7 collective-permute-start.15
  5.9 1.2 %copy-done.6 = f32[3,2,16,2560]{3,2,1,0:T(8,128)S(1)} copy-done((f32[3,2,16,2560]{3,2,1,0:T(8,128)S(1)}, f32[3,2,16,2560]{3,2,1,0:T(8,128)}, u32[]{:S(2)}) %copy-start.6) | copy-done | bytes 983064
  7.1 1.2 %copy-done.8 = f32[3,2,16,2560]{3,2,1,0:T(8,128)S(1)} copy-done((f32[3,2,16,2560]{3,2,1,0:T(8,128)S(1)}, f32[3,2,16,2560]{3,2,1,0:T(8,128)}, u32[]{:S(2)}) %copy-start.8) | copy-done | bytes 983064
  8.3 0.1 pack.1
  8.4 1.3 %collective-permute-start = (bf16[192,640]{1,0:T(8,128)(2,1)S(1)}, bf16[192,640]{1,0:T(8,128)(2,1)S(1)}, u32[]{:S(2)}, u32[]{:S(2)}) collective-permute-start(bf16[192,640]{1,0:T(8,128)(2,1)S(1)} %get-tuple-element.33), channel_id=1, source_target_pairs={{0,8},{8,0},{16,24},{24,16},{1,9},{9,1},{17,25},{25,17},{2,10},{10... | collective-permute-start | bytes 737288 | tf_op jit(solution)/shard_map/ppermute | solution.py:462
  9.7 1.2 %collective-permute-start.1 = (bf16[192,640]{1,0:T(8,128)(2,1)S(1)}, bf16[192,640]{1,0:T(8,128)(2,1)S(1)}, u32[]{:S(2)}, u32[]{:S(2)}) collective-permute-start(bf16[192,640]{1,0:T(8,128)(2,1)S(1)} %get-tuple-element.34), channel_id=1, source_target_pairs={{0,16},{8,24},{16,0},{24,8},{1,17},{9,25},{17,1},{25,9},{2,18},{10... | collective-permute-start | bytes 737288 | tf_op jit(solution)/shard_map/ppermute | solution.py:462
  10.9 0.2 collective-permute-start.2
  11.1 0.9 tables.1
  12.0 2.2 %collective-permute-done.refs_1_ = bf16[192,640]{1,0:T(8,128)(2,1)S(1)} collective-permute-done((bf16[192,640]{1,0:T(8,128)(2,1)S(1)}, bf16[192,640]{1,0:T(8,128)(2,1)S(1)}, u32[]{:S(2)}, u32[]{:S(2)}) %collective-permute-start) | collective-permute-done | bytes 245792 | tf_op jit(solution)/shard_map/ppermute | solution.py:462
  14.2 1.3 %collective-permute-done.1.refs_2_ = bf16[192,640]{1,0:T(8,128)(2,1)S(1)} collective-permute-done((bf16[192,640]{1,0:T(8,128)(2,1)S(1)}, bf16[192,640]{1,0:T(8,128)(2,1)S(1)}, u32[]{:S(2)}, u32[]{:S(2)}) %collective-permute-start.1) | collective-permute-done | bytes 245792 | tf_op jit(solution)/shard_map/ppermute | solution.py:462
  15.4 5.0 %collective-permute-done.2.refs_3_ = bf16[192,640]{1,0:T(8,128)(2,1)S(1)} collective-permute-done((bf16[192,640]{1,0:T(8,128)(2,1)S(1)}, bf16[192,640]{1,0:T(8,128)(2,1)S(1)}, u32[]{:S(2)}, u32[]{:S(2)}) %collective-permute-start.2) | collective-permute-done | bytes 245792 | tf_op jit(solution)/shard_map/ppermute | solution.py:462
  20.4 1.5 %transform.1 = (bf16[32,640]{1,0:T(8,128)(2,1)S(1)}, bf16[32,640]{1,0:T(8,128)(2,1)S(1)}, bf16[32,640]{1,0:T(8,128)(2,1)S(1)}, bf16[32,640]{1,0:T(8,128)(2,1)S(1...) custom-call(bf16[192,128]{1,0:T(8,128)(2,1)S(1)} %get-tuple-element., ...), custom_call_target="tpu_custom_call" | custom-call | tf_op jit(solution)/shard_map/transform/pallas_call | solution.py:103
  21.9 0.6 copy-done.15
  22.5 1.2 %collective-permute-start.3 = (bf16[32,640]{1,0:T(8,128)(2,1)S(1)}, bf16[32,640]{1,0:T(8,128)(2,1)S(1)}, u32[]{:S(2)}, u32[]{:S(2)}) collective-permute-start(bf16[32,640]{1,0:T(8,128)(2,1)S(1)} %get-tuple-element.37), channel_id=1, source_target_pairs={{0,8},{8,0},{16,24},{24,16},{1,9},{9,1},{17,25},{25,17},{2,10},{10... | collective-permute-start | bytes 122888 | tf_op jit(solution)/shard_map/ppermute | solution.py:462
  23.7 0.2 collective-permute-start.4
  24.0 1.2 %collective-permute-start.5 = (bf16[32,640]{1,0:T(8,128)(2,1)S(1)}, bf16[32,640]{1,0:T(8,128)(2,1)S(1)}, u32[]{:S(2)}, u32[]{:S(2)}) collective-permute-start(bf16[32,640]{1,0:T(8,128)(2,1)S(1)} %get-tuple-element.39), channel_id=1, source_target_pairs={{0,24},{8,16},{16,8},{24,0},{1,25},{9,17},{17,9},{25,1},{2,26},{10... | collective-permute-start | bytes 122888 | tf_op jit(solution)/shard_map/ppermute | solution.py:462
  25.2 4.0 %copy-done.2 = bf16[16,20,128,128]{3,2,1,0:T(8,128)(2,1)S(1)} copy-done((bf16[16,20,128,128]{3,2,1,0:T(8,128)(2,1)S(1)}, bf16[16,20,128,128]{3,2,1,0:T(8,128)(2,1)}, u32[]{:S(2)}) %copy-start.2) | copy-done | bytes 10485784
  29.1 4.0 %copy-done.3 = bf16[16,128,2560]{2,1,0:T(8,128)(2,1)S(1)} copy-done((bf16[16,128,2560]{2,1,0:T(8,128)(2,1)S(1)}, bf16[16,128,2560]{2,1,0:T(8,128)(2,1)}, u32[]{:S(2)}) %copy-start.3) | copy-done | bytes 10485784
  33.1 15.2 %compose.1 = (bf16[16,20,128,128]{3,2,1,0:T(8,128)(2,1)S(1)}, bf16[16,128,2560]{2,1,0:T(8,128)(2,1)S(1)}) custom-call(bf16[16,20,128,128]{3,2,1,0:T(8,128)(2,1)S(1)} %copy-done.2, bf16[16,128,2560]{2,1,0:T(8,128)(2,1)S(1)} %copy-done.3), custom_call_target="tpu_custom_call" | custom-call | flops 5368709120 | bytes 41943040 | tf_op jit(solution)/shard_map/compose/pallas_call | solution.py:169
  48.4 4.7 %leaf_up.1 = (f32[2,16,2560]{2,1,0:T(8,128)S(1)}, f32[2,16,128]{2,1,0:T(8,128)S(1)}) custom-call(s32[1]{0:T(128)} %bitcast.me_ref, s32[1,128]{1,0:T(1,128)S(1)} %copy-done.32, f32[3,2,16,2560]{3,2,1,0:T(8,128)S(1)} %copy-done.7, bf16[16,128,2560]{2,1,0:T(8,128)(2,1)S(1)} %get-tuple-element.44.joint_ref, bf16[32,640]{1,0:T(8,128)(2,1)S(1)} %get-tuple-element.36.refs_0_, ...), custom_call_target="tpu_custom_call" | custom-call | flops 671088640 | bytes 10485760 | tf_op jit(solution)/shard_map/leaf_up/pallas_call | solution.py:218
  53.1 4.0 %copy-done = bf16[16,128,2560]{2,1,0:T(8,128)(2,1)} copy-done((bf16[16,128,2560]{2,1,0:T(8,128)(2,1)}, bf16[16,128,2560]{2,1,0:T(8,128)(2,1)S(1)}, u32[]{:S(2)}) %copy-start) | copy-done | bytes 10485784
  57.1 1.3 %collective-permute-start.9 = (f32[2,16,128]{2,1,0:T(8,128)S(1)}, f32[2,16,128]{2,1,0:T(8,128)S(1)}, u32[]{:S(2)}, u32[]{:S(2)}) collective-permute-start(f32[2,16,128]{2,1,0:T(8,128)S(1)} %get-tuple-element.45.one_ref), channel_id=1, source_target_pairs={{0,1},{2,3},{4,5},{6,7},{8,9},{10,11},{12,13},{14,15},{16,17},{18,... | collective-permute-start | bytes 49160 | tf_op jit(solution)/shard_map/ppermute | solution.py:466
  58.4 4.4 %collective-permute-done.9.two_ref = f32[2,16,128]{2,1,0:T(8,128)S(1)} collective-permute-done((f32[2,16,128]{2,1,0:T(8,128)S(1)}, f32[2,16,128]{2,1,0:T(8,128)S(1)}, u32[]{:S(2)}, u32[]{:S(2)}) %collective-permute-start.9) | collective-permute-done | bytes 16416 | tf_op jit(solution)/shard_map/ppermute | solution.py:466
  62.8 0.5 rise.2
  63.3 0.6 copy-done.18
  63.9 0.7 collective-permute-start.10
  64.6 2.7 %collective-permute-start.11 = (f32[2,16,128]{2,1,0:T(8,128)S(1)}, f32[2,16,128]{2,1,0:T(8,128)S(1)}, u32[]{:S(2)}, u32[]{:S(2)}) collective-permute-start(f32[2,16,128]{2,1,0:T(8,128)S(1)} %get-tuple-element.46), channel_id=1, source_target_pairs={{3,2},{7,6},{11,10},{15,14},{19,18},{23,22},{27,26},{31,30}} | collective-permute-start | bytes 49160 | tf_op jit(solution)/shard_map/ppermute | solution.py:466
  67.3 0.7 collective-permute-start.14
  68.0 0.7 collective-permute-start.16
  68.7 0.5 rise.3
  69.2 0.6 copy-done.24
  69.8 0.7 collective-permute-start.12
  70.5 0.6 copy-done.26
  71.1 0.6 copy-done.20
  71.7 0.9 collective-permute-start.6
  72.6 0.6 copy-done.22
  73.2 0.6 collective-permute-start.7
  73.8 0.6 copy-done.28
  74.4 1.2 %collective-permute-start.8 = (bf16[64,640]{1,0:T(8,128)(2,1)}, bf16[64,640]{1,0:T(8,128)(2,1)}, u32[]{:S(2)}, u32[]{:S(2)}) collective-permute-start(bf16[64,640]{1,0:T(8,128)(2,1)} %get-tuple-element.43), channel_id=1, source_target_pairs={{0,24},{8,16},{16,8},{24,0},{1,25},{9,17},{17,9},{25,1},{2,26},{10... | collective-permute-start | bytes 245768 | tf_op jit(solution)/shard_map/ppermute | solution.py:462
  75.5 0.7 copy-done.21
  76.3 0.7 copy-done.23
  77.0 0.7 copy-done.25
  77.7 0.7 copy-done.27
  78.4 0.7 copy-done.29
  79.1 2.3 %crown.1 = (f32[2,16,128]{2,1,0:T(8,128)S(1)}, bf16[2,16,128]{2,1,0:T(8,128)(2,1)}, f32[2,16,128]{2,1,0:T(8,128)S(1)}) custom-call(s32[1]{0:T(128)} %bitcast.6.high_ref, f32[2,16,128]{2,1,0:T(8,128)S(1)} %copy-done.27, f32[2,16,128]{2,1,0:T(8,128)S(1)} %copy-done.29, f32[2,16,128]{2,1,0:T(8,128)S(1)} %copy-done.25, ...), custom_call_target="tpu_custom_call" | custom-call | tf_op jit(solution)/shard_map/crown/pallas_call | solution.py:386
  81.4 0.6 copy-done.30
  82.0 0.6 copy-done.34
  82.6 0.8 collective-permute-start.17
  83.4 1.3 %collective-permute-start.18 = (bf16[2,16,128]{2,1,0:T(8,128)(2,1)}, bf16[2,16,128]{2,1,0:T(8,128)(2,1)S(1)}, u32[]{:S(2)}, u32[]{:S(2)}) collective-permute-start(bf16[2,16,128]{2,1,0:T(8,128)(2,1)} %get-tuple-element.49), channel_id=1, source_target_pairs={{2,3},{6,7},{10,11},{14,15},{18,19},{22,23},{26,27},{30,31}} | collective-permute-start | bytes 24584 | tf_op jit(solution)/shard_map/ppermute | solution.py:466
  84.8 0.8 collective-permute-start.20
  85.6 7.1 %collective-permute-done.18.two_ref = bf16[2,16,128]{2,1,0:T(8,128)(2,1)S(1)} collective-permute-done((bf16[2,16,128]{2,1,0:T(8,128)(2,1)}, bf16[2,16,128]{2,1,0:T(8,128)(2,1)S(1)}, u32[]{:S(2)}, u32[]{:S(2)}) %collective-permute-start.18) | collective-permute-done | bytes 8224 | tf_op jit(solution)/shard_map/ppermute | solution.py:466
  92.7 0.7 copy-done.19
  93.4 0.4 sink.1
  93.8 3.6 %collective-permute-start.19 = (bf16[2,16,128]{2,1,0:T(8,128)(2,1)S(1)}, bf16[2,16,128]{2,1,0:T(8,128)(2,1)S(1)}, u32[]{:S(2)}, u32[]{:S(2)}) collective-permute-start(bf16[2,16,128]{2,1,0:T(8,128)(2,1)S(1)} %get-tuple-element.51.here_ref), channel_id=1, source_target_pairs={{1,0},{3,2},{5,4},{7,6},{9,8},{11,10},{13,12},{15,14},{17,16},{19,... | collective-permute-start | bytes 24584 | tf_op jit(solution)/shard_map/ppermute | solution.py:466
  97.4 4.0 %copy-done.5 = bf16[16,20,128,128]{3,2,1,0:T(8,128)(2,1)S(1)} copy-done((bf16[16,20,128,128]{3,2,1,0:T(8,128)(2,1)S(1)}, bf16[16,20,128,128]{3,2,1,0:T(8,128)(2,1)}, u32[]{:S(2)}) %copy-start.5) | copy-done | bytes 10485784
  101.4 2.4 %leaf_local.1.local_ref = f32[2,16,2560]{2,1,0:T(8,128)S(1)} custom-call(f32[2,16,2560]{2,1,0:T(8,128)S(1)} %get-tuple-element.52.source_ref, bf16[16,20,128,128]{3,2,1,0:T(8,128)(2,1)S(1)} %copy-done.5), custom_call_target="tpu_custom_call" | custom-call | flops 671088640 | bytes 10485760 | tf_op jit(solution)/shard_map/leaf_local/pallas_call | solution.py:265
  103.8 2.0 %spread.1 = f32[96,2560]{1,0:T(8,128)} custom-call(s32[1]{0:T(128)} %bitcast.me_ref, bf16[32,640]{1,0:T(8,128)(2,1)S(1)} %get-tuple-element.36.refs_0_, bf16[32,640]{1,0:T(8,128)(2,1)S(1)} %collective-permute-done.3.refs_1_, bf16[32,640]{1,0:T(8,128)(2,1)S(1)} %copy-done.12, bf16[32,640]{1,0:T(8,128)(2,1)S(1)} %copy-done.14, bf16[64,640]{1,0:T(8,128)(2,1)S(1)} %copy-done.16, ...), custom_call_target="tpu_custom_call" | custom-call | tf_op jit(solution)/shard_map/spread/pallas_call | solution.py:327
  105.8 2.8 %leaf_down.1 = f32[2,16,2560]{2,1,0:T(8,128)} custom-call(s32[1]{0:T(128)} %bitcast.4.own_ref, s32[1,128]{1,0:T(1,128)S(1)} %copy-done.33, bf16[2,16,128]{2,1,0:T(8,128)(2,1)S(1)} %get-tuple-element.51.here_ref, bf16[2,16,128]{2,1,0:T(8,128)(2,1)S(1)} %collective-permute-done.19.beside_ref, f32[2,16,2560]{2,1,0:T(8,128)S(1)} %leaf_local.1.local_ref, ...), custom_call_target="tpu_custom_call" | custom-call | tf_op jit(solution)/shard_map/leaf_down/pallas_call | solution.py:303
  108.6 0.6 choose.1
  (63 shorter events, 0.2 us)
Async XLA Ops:
  1.9 1.0 copy-start.9
  2.9 1.0 copy-start.10
  4.4 71.1 %collective-permute-start.13 = (bf16[2,16,128,128]{3,2,1,0:T(8,128)(2,1)S(1)}, bf16[2,16,128,128]{3,2,1,0:T(8,128)(2,1)S(1)}, u32[]{:S(2)}, u32[]{:S(2)}) collective-permute-start(bf16[2,16,128,128]{3,2,1,0:T(8,128)(2,1)S(1)} %fronts.1.front_ref), channel_id=1, source_target_pairs={{4,2},{0,6},{12,10},{8,14},{20,18},{16,22},{28,26},{24,30}} | collective-permute-start | bytes 3145736 | tf_op jit(solution)/shard_map/ppermute | solution.py:466
  5.1 70.4 %collective-permute-start.15 = (bf16[2,16,128,128]{3,2,1,0:T(8,128)(2,1)S(1)}, bf16[2,16,128,128]{3,2,1,0:T(8,128)(2,1)S(1)}, u32[]{:S(2)}, u32[]{:S(2)}) collective-permute-start(bf16[2,16,128,128]{3,2,1,0:T(8,128)(2,1)S(1)} %fronts.1.front_ref), channel_id=1, source_target_pairs={{4,6},{0,2},{12,14},{8,10},{20,22},{16,18},{28,30},{24,26}} | collective-permute-start | bytes 3145736 | tf_op jit(solution)/shard_map/ppermute | solution.py:466
  5.9 1.2 %copy-start.6 = (f32[3,2,16,2560]{3,2,1,0:T(8,128)S(1)}, f32[3,2,16,2560]{3,2,1,0:T(8,128)}, u32[]{:S(2)}) copy-start(f32[3,2,16,2560]{3,2,1,0:T(8,128)} %mag_ref.1) | copy-start | bytes 2949124
  7.1 1.2 %copy-start.8 = (f32[3,2,16,2560]{3,2,1,0:T(8,128)S(1)}, f32[3,2,16,2560]{3,2,1,0:T(8,128)}, u32[]{:S(2)}) copy-start(f32[3,2,16,2560]{3,2,1,0:T(8,128)} %param.8) | copy-start | bytes 2949124
  8.4 5.8 %collective-permute-start = (bf16[192,640]{1,0:T(8,128)(2,1)S(1)}, bf16[192,640]{1,0:T(8,128)(2,1)S(1)}, u32[]{:S(2)}, u32[]{:S(2)}) collective-permute-start(bf16[192,640]{1,0:T(8,128)(2,1)S(1)} %get-tuple-element.33), channel_id=1, source_target_pairs={{0,8},{8,0},{16,24},{24,16},{1,9},{9,1},{17,25},{25,17},{2,10},{10... | collective-permute-start | bytes 737288 | tf_op jit(solution)/shard_map/ppermute | solution.py:462
  9.7 5.8 %collective-permute-start.1 = (bf16[192,640]{1,0:T(8,128)(2,1)S(1)}, bf16[192,640]{1,0:T(8,128)(2,1)S(1)}, u32[]{:S(2)}, u32[]{:S(2)}) collective-permute-start(bf16[192,640]{1,0:T(8,128)(2,1)S(1)} %get-tuple-element.34), channel_id=1, source_target_pairs={{0,16},{8,24},{16,0},{24,8},{1,17},{9,25},{17,1},{25,9},{2,18},{10... | collective-permute-start | bytes 737288 | tf_op jit(solution)/shard_map/ppermute | solution.py:462
  10.9 9.5 %collective-permute-start.2 = (bf16[192,640]{1,0:T(8,128)(2,1)S(1)}, bf16[192,640]{1,0:T(8,128)(2,1)S(1)}, u32[]{:S(2)}, u32[]{:S(2)}) collective-permute-start(bf16[192,640]{1,0:T(8,128)(2,1)S(1)} %get-tuple-element.35), channel_id=1, source_target_pairs={{0,24},{8,16},{16,8},{24,0},{1,25},{9,17},{17,9},{25,1},{2,26},{10... | collective-permute-start | bytes 737288 | tf_op jit(solution)/shard_map/ppermute | solution.py:462
  21.9 0.6 copy-start.15
  22.5 25.8 %collective-permute-start.3 = (bf16[32,640]{1,0:T(8,128)(2,1)S(1)}, bf16[32,640]{1,0:T(8,128)(2,1)S(1)}, u32[]{:S(2)}, u32[]{:S(2)}) collective-permute-start(bf16[32,640]{1,0:T(8,128)(2,1)S(1)} %get-tuple-element.37), channel_id=1, source_target_pairs={{0,8},{8,0},{16,24},{24,16},{1,9},{9,1},{17,25},{25,17},{2,10},{10... | collective-permute-start | bytes 122888 | tf_op jit(solution)/shard_map/ppermute | solution.py:462
  23.7 24.6 %collective-permute-start.4 = (bf16[32,640]{1,0:T(8,128)(2,1)S(1)}, bf16[32,640]{1,0:T(8,128)(2,1)S(1)}, u32[]{:S(2)}, u32[]{:S(2)}) collective-permute-start(bf16[32,640]{1,0:T(8,128)(2,1)S(1)} %get-tuple-element.38), channel_id=1, source_target_pairs={{0,16},{8,24},{16,0},{24,8},{1,17},{9,25},{17,1},{25,9},{2,18},{10... | collective-permute-start | bytes 122888 | tf_op jit(solution)/shard_map/ppermute | solution.py:462
  24.0 24.4 %collective-permute-start.5 = (bf16[32,640]{1,0:T(8,128)(2,1)S(1)}, bf16[32,640]{1,0:T(8,128)(2,1)S(1)}, u32[]{:S(2)}, u32[]{:S(2)}) collective-permute-start(bf16[32,640]{1,0:T(8,128)(2,1)S(1)} %get-tuple-element.39), channel_id=1, source_target_pairs={{0,24},{8,16},{16,8},{24,0},{1,25},{9,17},{17,9},{25,1},{2,26},{10... | collective-permute-start | bytes 122888 | tf_op jit(solution)/shard_map/ppermute | solution.py:462
  25.2 4.0 %copy-start.2 = (bf16[16,20,128,128]{3,2,1,0:T(8,128)(2,1)S(1)}, bf16[16,20,128,128]{3,2,1,0:T(8,128)(2,1)}, u32[]{:S(2)}) copy-start(bf16[16,20,128,128]{3,2,1,0:T(8,128)(2,1)} %inv_hbm.1) | copy-start | bytes 31457284
  29.1 4.0 %copy-start.3 = (bf16[16,128,2560]{2,1,0:T(8,128)(2,1)S(1)}, bf16[16,128,2560]{2,1,0:T(8,128)(2,1)}, u32[]{:S(2)}) copy-start(bf16[16,128,2560]{2,1,0:T(8,128)(2,1)} %cpl_hbm.1) | copy-start | bytes 31457284
  33.1 15.2 %copy-start.7 = (f32[3,2,16,2560]{3,2,1,0:T(8,128)S(1)}, f32[3,2,16,2560]{3,2,1,0:T(8,128)}, u32[]{:S(2)}) copy-start(f32[3,2,16,2560]{3,2,1,0:T(8,128)} %mag_ref.1) | copy-start | bytes 2949124
  33.1 15.2 %copy-start.32 = (s32[1,128]{1,0:T(1,128)S(1)}, s32[1,128]{1,0:T(1,128)}, u32[]{:S(2)}) copy-start(s32[1,128]{1,0:T(1,128)} %get-tuple-element.58.rows_ref) | copy-start | bytes 1540
  48.3 4.8 %copy-start.4 = (bf16[16,20,128,128]{3,2,1,0:T(8,128)(2,1)}, bf16[16,20,128,128]{3,2,1,0:T(8,128)(2,1)S(1)}, u32[]{:S(2)}) copy-start(bf16[16,20,128,128]{3,2,1,0:T(8,128)(2,1)S(1)} %get-tuple-element.53.square_ref) | copy-start | bytes 31457284
  48.3 14.5 %copy-start.17 = (f32[2,16,128]{2,1,0:T(8,128)S(1)}, f32[2,16,128]{2,1,0:T(8,128)}, u32[]{:S(2)}) copy-start(f32[2,16,128]{2,1,0:T(8,128)} %source_ref.3) | copy-start | bytes 49156
  48.3 8.8 %copy-start.11 = (bf16[32,640]{1,0:T(8,128)(2,1)}, bf16[32,640]{1,0:T(8,128)(2,1)S(1)}, u32[]{:S(2)}) copy-start(bf16[32,640]{1,0:T(8,128)(2,1)S(1)} %collective-permute-done.4.refs_2_) | copy-start | bytes 122884
  48.3 10.1 %copy-start.13 = (bf16[32,640]{1,0:T(8,128)(2,1)}, bf16[32,640]{1,0:T(8,128)(2,1)S(1)}, u32[]{:S(2)}) copy-start(bf16[32,640]{1,0:T(8,128)(2,1)S(1)} %collective-permute-done.5.refs_3_) | copy-start | bytes 122884
  53.1 4.1 %copy-start = (bf16[16,128,2560]{2,1,0:T(8,128)(2,1)}, bf16[16,128,2560]{2,1,0:T(8,128)(2,1)S(1)}, u32[]{:S(2)}) copy-start(bf16[16,128,2560]{2,1,0:T(8,128)(2,1)S(1)} %get-tuple-element.44.joint_ref) | copy-start | bytes 31457284
  57.1 5.7 %collective-permute-start.9 = (f32[2,16,128]{2,1,0:T(8,128)S(1)}, f32[2,16,128]{2,1,0:T(8,128)S(1)}, u32[]{:S(2)}, u32[]{:S(2)}) collective-permute-start(f32[2,16,128]{2,1,0:T(8,128)S(1)} %get-tuple-element.45.one_ref), channel_id=1, source_target_pairs={{0,1},{2,3},{4,5},{6,7},{8,9},{10,11},{12,13},{14,15},{16,17},{18,... | collective-permute-start | bytes 49160 | tf_op jit(solution)/shard_map/ppermute | solution.py:466
  63.3 0.6 copy-start.18
  63.9 4.0 %collective-permute-start.10 = (f32[2,16,128]{2,1,0:T(8,128)S(1)}, f32[2,16,128]{2,1,0:T(8,128)S(1)}, u32[]{:S(2)}, u32[]{:S(2)}) collective-permute-start(f32[2,16,128]{2,1,0:T(8,128)S(1)} %get-tuple-element.46), channel_id=1, source_target_pairs={{1,2},{5,6},{9,10},{13,14},{17,18},{21,22},{25,26},{29,30}} | collective-permute-start | bytes 49160 | tf_op jit(solution)/shard_map/ppermute | solution.py:466
  64.6 4.1 %collective-permute-start.11 = (f32[2,16,128]{2,1,0:T(8,128)S(1)}, f32[2,16,128]{2,1,0:T(8,128)S(1)}, u32[]{:S(2)}, u32[]{:S(2)}) collective-permute-start(f32[2,16,128]{2,1,0:T(8,128)S(1)} %get-tuple-element.46), channel_id=1, source_target_pairs={{3,2},{7,6},{11,10},{15,14},{19,18},{23,22},{27,26},{31,30}} | collective-permute-start | bytes 49160 | tf_op jit(solution)/shard_map/ppermute | solution.py:466
  67.3 3.8 %collective-permute-start.14 = (f32[2,16,128]{2,1,0:T(8,128)S(1)}, f32[2,16,128]{2,1,0:T(8,128)S(1)}, u32[]{:S(2)}, u32[]{:S(2)}) collective-permute-start(f32[2,16,128]{2,1,0:T(8,128)S(1)} %copy-done.17), channel_id=1, source_target_pairs={{4,2},{0,6},{12,10},{8,14},{20,18},{16,22},{28,26},{24,30}} | collective-permute-start | bytes 49160 | tf_op jit(solution)/shard_map/ppermute | solution.py:466
  68.0 4.6 %collective-permute-start.16 = (f32[2,16,128]{2,1,0:T(8,128)S(1)}, f32[2,16,128]{2,1,0:T(8,128)S(1)}, u32[]{:S(2)}, u32[]{:S(2)}) collective-permute-start(f32[2,16,128]{2,1,0:T(8,128)S(1)} %copy-done.17), channel_id=1, source_target_pairs={{4,6},{0,2},{12,14},{8,10},{20,22},{16,18},{28,30},{24,26}} | collective-permute-start | bytes 49160 | tf_op jit(solution)/shard_map/ppermute | solution.py:466
  69.2 0.6 copy-start.24
  69.8 4.0 %collective-permute-start.12 = (f32[2,16,128]{2,1,0:T(8,128)S(1)}, f32[2,16,128]{2,1,0:T(8,128)S(1)}, u32[]{:S(2)}, u32[]{:S(2)}) collective-permute-start(f32[2,16,128]{2,1,0:T(8,128)S(1)} %get-tuple-element.47.one_ref), channel_id=1, source_target_pairs={{2,6},{6,2},{10,14},{14,10},{18,22},{22,18},{26,30},{30,26}} | collective-permute-start | bytes 49160 | tf_op jit(solution)/shard_map/ppermute | solution.py:466
  70.5 0.6 copy-start.26
  71.1 0.6 copy-start.20
  71.7 32.1 %collective-permute-start.6 = (bf16[64,640]{1,0:T(8,128)(2,1)}, bf16[64,640]{1,0:T(8,128)(2,1)}, u32[]{:S(2)}, u32[]{:S(2)}) collective-permute-start(bf16[64,640]{1,0:T(8,128)(2,1)} %get-tuple-element.41), channel_id=1, source_target_pairs={{0,8},{8,0},{16,24},{24,16},{1,9},{9,1},{17,25},{25,17},{2,10},{10... | collective-permute-start | bytes 245768 | tf_op jit(solution)/shard_map/ppermute | solution.py:462
  72.6 0.6 copy-start.22
  73.2 30.6 %collective-permute-start.7 = (bf16[64,640]{1,0:T(8,128)(2,1)}, bf16[64,640]{1,0:T(8,128)(2,1)}, u32[]{:S(2)}, u32[]{:S(2)}) collective-permute-start(bf16[64,640]{1,0:T(8,128)(2,1)} %get-tuple-element.42), channel_id=1, source_target_pairs={{0,16},{8,24},{16,0},{24,8},{1,17},{9,25},{17,1},{25,9},{2,18},{10... | collective-permute-start | bytes 245768 | tf_op jit(solution)/shard_map/ppermute | solution.py:462
  73.8 0.6 copy-start.28
  74.4 29.4 %collective-permute-start.8 = (bf16[64,640]{1,0:T(8,128)(2,1)}, bf16[64,640]{1,0:T(8,128)(2,1)}, u32[]{:S(2)}, u32[]{:S(2)}) collective-permute-start(bf16[64,640]{1,0:T(8,128)(2,1)} %get-tuple-element.43), channel_id=1, source_target_pairs={{0,24},{8,16},{16,8},{24,0},{1,25},{9,17},{17,9},{25,1},{2,26},{10... | collective-permute-start | bytes 245768 | tf_op jit(solution)/shard_map/ppermute | solution.py:462
  75.5 0.7 copy-start.21
  76.3 0.7 copy-start.23
  77.0 0.7 copy-start.25
  77.7 0.7 copy-start.27
  78.4 0.7 copy-start.29
  81.4 0.6 copy-start.30
  82.0 0.6 copy-start.34
  82.6 21.1 %copy-start.12 = (bf16[32,640]{1,0:T(8,128)(2,1)S(1)}, bf16[32,640]{1,0:T(8,128)(2,1)}, u32[]{:S(2)}) copy-start(bf16[32,640]{1,0:T(8,128)(2,1)} %copy-done.11) | copy-start | bytes 122884
  82.6 23.1 %copy-start.33 = (s32[1,128]{1,0:T(1,128)S(1)}, s32[1,128]{1,0:T(1,128)}, u32[]{:S(2)}) copy-start(s32[1,128]{1,0:T(1,128)} %get-tuple-element.58.rows_ref) | copy-start | bytes 1540
  82.6 2.1 %collective-permute-start.17 = (bf16[2,16,128]{2,1,0:T(8,128)(2,1)}, bf16[2,16,128]{2,1,0:T(8,128)(2,1)S(1)}, u32[]{:S(2)}, u32[]{:S(2)}) collective-permute-start(bf16[2,16,128]{2,1,0:T(8,128)(2,1)} %get-tuple-element.49), channel_id=1, source_target_pairs={{2,1},{6,5},{10,9},{14,13},{18,17},{22,21},{26,25},{30,29}} | collective-permute-start | bytes 24584 | tf_op jit(solution)/shard_map/ppermute | solution.py:466
  83.4 9.2 %collective-permute-start.18 = (bf16[2,16,128]{2,1,0:T(8,128)(2,1)}, bf16[2,16,128]{2,1,0:T(8,128)(2,1)S(1)}, u32[]{:S(2)}, u32[]{:S(2)}) collective-permute-start(bf16[2,16,128]{2,1,0:T(8,128)(2,1)} %get-tuple-element.49), channel_id=1, source_target_pairs={{2,3},{6,7},{10,11},{14,15},{18,19},{22,23},{26,27},{30,31}} | collective-permute-start | bytes 24584 | tf_op jit(solution)/shard_map/ppermute | solution.py:466
  84.8 21.0 %copy-start.1 = (bf16[16,128,2560]{2,1,0:T(8,128)(2,1)S(1)}, bf16[16,128,2560]{2,1,0:T(8,128)(2,1)}, u32[]{:S(2)}) copy-start(bf16[16,128,2560]{2,1,0:T(8,128)(2,1)} %copy-done) | copy-start | bytes 31457284
  84.8 23.8 %collective-permute-start.20 = (f32[2,16,128]{2,1,0:T(8,128)}, f32[2,16,128]{2,1,0:T(8,128)S(1)}, u32[]{:S(2)}, u32[]{:S(2)}) collective-permute-start(f32[2,16,128]{2,1,0:T(8,128)} %copy-done.34), channel_id=1, source_target_pairs={{2,0},{6,4},{10,8},{14,12},{18,16},{22,20},{26,24},{30,28}} | collective-permute-start | bytes 49160 | tf_op jit(solution)/shard_map/ppermute | solution.py:466
  92.7 0.7 copy-start.19
  93.8 12.0 %collective-permute-start.19 = (bf16[2,16,128]{2,1,0:T(8,128)(2,1)S(1)}, bf16[2,16,128]{2,1,0:T(8,128)(2,1)S(1)}, u32[]{:S(2)}, u32[]{:S(2)}) collective-permute-start(bf16[2,16,128]{2,1,0:T(8,128)(2,1)S(1)} %get-tuple-element.51.here_ref), channel_id=1, source_target_pairs={{1,0},{3,2},{5,4},{7,6},{9,8},{11,10},{13,12},{15,14},{17,16},{19,... | collective-permute-start | bytes 24584 | tf_op jit(solution)/shard_map/ppermute | solution.py:466
  97.4 4.0 %copy-start.5 = (bf16[16,20,128,128]{3,2,1,0:T(8,128)(2,1)S(1)}, bf16[16,20,128,128]{3,2,1,0:T(8,128)(2,1)}, u32[]{:S(2)}) copy-start(bf16[16,20,128,128]{3,2,1,0:T(8,128)(2,1)} %copy-done.4) | copy-start | bytes 31457284
  101.4 2.4 %copy-start.14 = (bf16[32,640]{1,0:T(8,128)(2,1)S(1)}, bf16[32,640]{1,0:T(8,128)(2,1)}, u32[]{:S(2)}) copy-start(bf16[32,640]{1,0:T(8,128)(2,1)} %copy-done.13) | copy-start | bytes 122884
  101.4 2.4 %copy-start.16 = (bf16[64,640]{1,0:T(8,128)(2,1)S(1)}, bf16[64,640]{1,0:T(8,128)(2,1)}, u32[]{:S(2)}) copy-start(bf16[64,640]{1,0:T(8,128)(2,1)} %copy-done.15) | copy-start | bytes 245764
  101.4 7.2 %copy-start.31 = (f32[2,16,128]{2,1,0:T(8,128)S(1)}, f32[2,16,128]{2,1,0:T(8,128)}, u32[]{:S(2)}) copy-start(f32[2,16,128]{2,1,0:T(8,128)} %copy-done.30) | copy-start | bytes 49156

commit v3 on v2

--- a/solution.py
+++ b/solution.py
@@ -7,10 +7,10 @@
 from jax.experimental.pallas import tpu as pltpu
 from jax.sharding import PartitionSpec as P
 
+
 NPHI = 192
 DT_STEP = 0.5
 VMEM = pltpu.VMEM
-SMEM = pltpu.SMEM
 BF16 = jnp.bfloat16
 F32 = jnp.float32
 NT = (((1,), (1,)), ((), ()))
@@ -20,16 +20,20 @@
 COMPOSE = 8 * 2**20
 
 
+def stay(value):
+    return pltpu.with_memory_space_constraint(value, pltpu.HBM)
+
+
 def dot(a, b, dims=NN, precision=None):
     return lax.dot_general(a, b, dims, precision=precision, preferred_element_type=F32)
 
 
-def tables_kernel(modes, me_ref, fwd_ref, bwd_ref):
+def tables_kernel(modes, fwd_ref, bwd_ref):
     def phase(shape, angle_axis):
         angle = lax.broadcasted_iota(jnp.int32, shape, angle_axis)
         at = lax.broadcasted_iota(jnp.int32, shape, 1 - angle_axis)
         step, kind, mode = at // (2 * modes), (at // modes) % 2, at % modes
-        order = jnp.bitwise_xor(step, me_ref[0]) * modes + mode
+        order = jnp.bitwise_xor(step, lax.axis_index("mode")) * modes + mode
         turn = (angle * order).astype(F32)
         turn = turn - NPHI * jnp.floor((turn + 0.5) * (1.0 / NPHI))
         return turn * (2.0 * jnp.pi / NPHI), kind, order
@@ -41,37 +45,48 @@
     bwd_ref[...] = (jnp.where(kind == 0, jnp.cos(at), jnp.sin(at)) * weight).astype(BF16)
 
 
-def tables(me, groups, modes):
+def tables(groups, modes):
     rows = groups * 2 * modes
     return pl.pallas_call(
         functools.partial(tables_kernel, modes),
         out_shape=[jax.ShapeDtypeStruct((NPHI, rows), BF16), jax.ShapeDtypeStruct((rows, NPHI), BF16)],
-        in_specs=[pl.BlockSpec(memory_space=SMEM)],
         out_specs=[pl.BlockSpec(memory_space=VMEM)] * 2,
         compiler_params=pltpu.CompilerParams(vmem_limit_bytes=SMALL),
         name="tables",
-    )(me)
-
-
-def pack_kernel(groups, me_ref, v_ref, b_ref, *outs):
-    rows, width = v_ref.shape[0], outs[0].shape[1]
-    for k in range(groups):
-        span = pl.ds(pl.multiple_of(jnp.bitwise_xor(me_ref[0], k) * width, 128), width)
-        outs[k][:rows, :] = v_ref[:, span].astype(BF16)
-        outs[k][rows:, :] = b_ref[:, span].astype(BF16)
-
-
-def pack(me, velocity, magnetic, groups):
+    )()
+
+
+def pack_kernel(groups, v_hbm, b_hbm, *refs):
+    outs, held, sems = refs[:groups], refs[groups], refs[groups + 1]
+    rows, width = v_hbm.shape[0], outs[0].shape[1]
+
+    def copy(field, k):
+        span = pl.ds(pl.multiple_of((lax.axis_index("mode") ^ k) * width, 128), width)
+        source = (v_hbm, b_hbm)[field].at[:, span]
+        return pltpu.make_async_copy(source, held.at[k, field], sems.at[k, field])
+
+    order = list(range(1, groups)) + [0]
+    for k in order:
+        for field in range(2):
+            copy(field, k).start()
+    for k in order:
+        for field in range(2):
+            copy(field, k).wait()
+            outs[k][field * rows : (field + 1) * rows, :] = held[k, field].astype(BF16)
+
+
+def pack(velocity, magnetic, groups):
     rows, nodes = velocity.shape
     width = nodes // groups
     return pl.pallas_call(
         functools.partial(pack_kernel, groups),
         out_shape=[jax.ShapeDtypeStruct((2 * rows, width), BF16)] * groups,
-        in_specs=[pl.BlockSpec(memory_space=SMEM)] + [pl.BlockSpec(memory_space=VMEM)] * 2,
+        in_specs=[pl.BlockSpec(memory_space=pltpu.HBM)] * 2,
         out_specs=[pl.BlockSpec(memory_space=VMEM)] * groups,
-        compiler_params=pltpu.CompilerParams(vmem_limit_bytes=16 * 2**20),
+        scratch_shapes=[VMEM((groups, 2, rows, width), F32), pltpu.SemaphoreType.DMA((groups, 2))],
+        compiler_params=pltpu.CompilerParams(vmem_limit_bytes=SMALL),
         name="pack",
-    )(me, velocity, magnetic)
+    )(velocity, magnetic)
 
 
 def transform_kernel(groups, fwd_ref, bwd_ref, *refs):
@@ -112,13 +127,13 @@
     return out[:groups], out[groups:]
 
 
-def one_hot(rows_ref):
-    n = rows_ref.shape[1]
-    return lax.broadcasted_iota(jnp.int32, (n, n), 0) == rows_ref[0:1, :]
+def one_hot(rows_ref, which):
+    n = rows_ref.shape[2]
+    return lax.broadcasted_iota(jnp.int32, (n, n), 0) == rows_ref[0, which : which + 1, :]
 
 
 def compose_kernel(inv_hbm, cpl_hbm, square_ref, joint_ref, inv_v, cpl_v, sems):
-    modes, front, nodes = joint_ref.shape
+    modes, front, _ = joint_ref.shape
     blocks, size = inv_v.shape[1], inv_v.shape[2]
     depth = inv_v.shape[0]
     zero = jnp.zeros((size, size), BF16)
@@ -172,7 +187,7 @@
             jax.ShapeDtypeStruct(inverse.shape, BF16),
             jax.ShapeDtypeStruct(coupling.shape, BF16),
         ],
-        in_specs=[pl.BlockSpec(memory_space=pl.ANY)] * 2,
+        in_specs=[pl.BlockSpec(memory_space=pltpu.HBM)] * 2,
         out_specs=[pl.BlockSpec(memory_space=VMEM)] * 2,
         scratch_shapes=[
             VMEM((depth, blocks, size, size), BF16),
@@ -189,16 +204,19 @@
     )(inverse, coupling)
 
 
-def leaf_up_kernel(groups, me_ref, rows_ref, mag_ref, joint_ref, *refs):
+def leaf_up_kernel(groups, rows_ref, mag_hbm, joint_ref, *refs):
     pieces = refs[:groups]
-    source_ref, update_ref, turned_v = refs[groups:]
+    source_ref, update_ref, turned_v, mag_v, sem = refs[groups:]
+    copy = pltpu.make_async_copy(mag_hbm.at[1], mag_v, sem)
+    copy.start()
+    copy.wait()
     modes, front, nodes = joint_ref.shape
     width = nodes // groups
     for k in range(groups):
-        span = pl.ds(pl.multiple_of(jnp.bitwise_xor(me_ref[0], k) * width, 128), width)
+        span = pl.ds(pl.multiple_of((lax.axis_index("mode") ^ k) * width, 128), width)
         for a in range(2):
             term = pieces[k][a * modes : (a + 1) * modes, :].astype(F32)
-            source_ref[a, :, span] = mag_ref[0, a, :, span] + DT_STEP * term
+            source_ref[a, :, span] = mag_v[a, :, span] + DT_STEP * term
     turned_v[...] = source_ref[...].reshape(2 * modes, nodes).T.astype(BF16)
     turned = turned_v[...]
     lane = lax.broadcasted_iota(jnp.int32, (front, 2 * modes), 1) % modes
@@ -207,35 +225,37 @@
         return total + jnp.where(lane == m, dot(joint_ref[m], turned), 0.0)
 
     total = lax.fori_loop(0, modes, one_mode, jnp.zeros((front, 2 * modes), F32), unroll=2)
-    select = one_hot(rows_ref).astype(F32)
+    select = one_hot(rows_ref, 0).astype(F32)
     update_ref[...] = dot(total.T, select, precision=lax.Precision.HIGHEST).reshape(update_ref.shape)
 
 
-def leaf_up(me, rows, magnetic, pieces, joint):
+def leaf_up(rows, magnetic, pieces, joint):
     modes, front, nodes = joint.shape
     groups = len(pieces)
     whole = pl.BlockSpec(memory_space=VMEM)
     return pl.pallas_call(
         functools.partial(leaf_up_kernel, groups),
-        grid=(1,),
         out_shape=[
             jax.ShapeDtypeStruct((2, modes, nodes), F32),
             jax.ShapeDtypeStruct((2, modes, front), F32),
         ],
         in_specs=[
-            pl.BlockSpec(memory_space=SMEM),
             whole,
-            pl.BlockSpec((1, 2, modes, nodes), lambda i: (1, 0, 0, 0)),
+            pl.BlockSpec(memory_space=pltpu.HBM),
         ]
         + [whole] * (1 + groups),
         out_specs=[whole] * 2,
-        scratch_shapes=[VMEM((nodes, 2 * modes), BF16)],
+        scratch_shapes=[
+            VMEM((nodes, 2 * modes), BF16),
+            VMEM((2, modes, nodes), F32),
+            pltpu.SemaphoreType.DMA(()),
+        ],
         compiler_params=pltpu.CompilerParams(vmem_limit_bytes=LARGE),
         cost_estimate=pl.CostEstimate(
             flops=128 * modes * nodes * front, bytes_accessed=2 * joint.size, transcendentals=0
         ),
         name="leaf_up",
-    )(me, rows, magnetic, joint, *pieces)
+    )(rows, magnetic, joint, *pieces)
 
 
 def leaf_local_kernel(source_ref, square_ref, out_ref):
@@ -275,10 +295,10 @@
     )(source, square)
 
 
-def leaf_down_kernel(own_ref, rows_ref, here_ref, beside_ref, local_ref, joint_ref, out_ref, x_v):
+def leaf_down_kernel(rows_ref, here_ref, beside_ref, local_ref, joint_ref, out_ref, x_v):
     modes, front, nodes = joint_ref.shape
-    select = one_hot(rows_ref).astype(F32).astype(BF16)
-    above = jnp.where(own_ref[0] == 1, here_ref[...].astype(F32), beside_ref[...].astype(F32))
+    select = one_hot(rows_ref, 0).astype(F32).astype(BF16)
+    above = jnp.where(lax.axis_index("mesh") % 2 == 1, here_ref[...].astype(F32), beside_ref[...].astype(F32))
     x_v[...] = dot(above.reshape(2 * modes, front).astype(BF16), select, NT).reshape(2, modes, front)
     zero = jnp.zeros((2, front), F32)
 
@@ -298,59 +318,84 @@
     lax.fori_loop(0, modes // 2, two_modes, 0, unroll=2)
 
 
-def leaf_down(own, rows, here, beside, local, joint):
+def leaf_down(rows, here, beside, local, joint):
     whole = pl.BlockSpec(memory_space=VMEM)
     return pl.pallas_call(
         leaf_down_kernel,
         out_shape=jax.ShapeDtypeStruct(local.shape, F32),
-        in_specs=[pl.BlockSpec(memory_space=SMEM)] + [whole] * 5,
+        in_specs=[whole] * 5,
         out_specs=whole,
         scratch_shapes=[VMEM(here.shape, F32)],
         compiler_params=pltpu.CompilerParams(vmem_limit_bytes=LARGE),
         name="leaf_down",
-    )(own, rows, here, beside, local, joint)
-
-
-def spread_kernel(groups, me_ref, *refs):
+    )(rows, here, beside, local, joint)
+
+
+def spread_kernel(groups, *refs):
     azi, rest, out_ref = refs[:groups], refs[groups : 2 * groups], refs[2 * groups]
     rows, width = azi[0].shape
     for k in range(groups):
-        span = pl.ds(pl.multiple_of(jnp.bitwise_xor(me_ref[0], k) * width, 128), width)
+        span = pl.ds(pl.multiple_of((lax.axis_index("mode") ^ k) * width, 128), width)
         out_ref[:rows, span] = rest[k][:rows, :].astype(F32)
         out_ref[rows : 2 * rows, span] = azi[k][...].astype(F32)
         out_ref[2 * rows :, span] = rest[k][rows:, :].astype(F32)
 
 
-def spread(me, azi, rest):
+def spread(azi, rest):
     groups = len(azi)
     rows, width = azi[0].shape
     return pl.pallas_call(
         functools.partial(spread_kernel, groups),
         out_shape=jax.ShapeDtypeStruct((3 * rows, groups * width), F32),
-        in_specs=[pl.BlockSpec(memory_space=SMEM)] + [pl.BlockSpec(memory_space=VMEM)] * (2 * groups),
+        in_specs=[pl.BlockSpec(memory_space=VMEM)] * (2 * groups),
         out_specs=pl.BlockSpec(memory_space=VMEM),
         compiler_params=pltpu.CompilerParams(vmem_limit_bytes=16 * 2**20),
         name="spread",
-    )(me, *azi, *rest)
-
-
-def fronts_kernel(rows_ref, inv_ref, cpl_ref, out_ref):
+    )(*azi, *rest)
+
+
+def fronts_kernel(rows_ref, inv_ref, cpl_ref, source_ref, out_ref):
     modes, size, _ = inv_ref.shape
-    out_ref[0] = inv_ref[...]
-    select = one_hot(rows_ref).astype(F32).T.astype(BF16)
+    half = modes * size
+    out_ref[:half, :] = inv_ref[...].reshape(half, size)
+    select = one_hot(rows_ref, 1).astype(F32).T.astype(BF16)
     for m in range(modes):
-        out_ref[1, m] = dot(select, cpl_ref[m]).astype(BF16)
-
-
-def fronts(rows, inverse, coupling):
+        at = half + m * size
+        out_ref[at : at + size, :] = dot(select, cpl_ref[m]).astype(BF16)
+    rest = flat(source_ref)
+    for part in range(3):
+        at = 2 * half + part * rest.shape[0]
+        term = rest.astype(BF16)
+        out_ref[at : at + rest.shape[0], :] = term
+        rest = rest - term.astype(F32)
+
+
+def fronts(rows, inverse, coupling, source):
+    modes, size, _ = inverse.shape
+    total = 2 * modes * size + 3 * 2 * modes
     return pl.pallas_call(
         fronts_kernel,
-        out_shape=jax.ShapeDtypeStruct((2,) + inverse.shape, BF16),
-        in_specs=[pl.BlockSpec(memory_space=VMEM)] * 3,
+        out_shape=jax.ShapeDtypeStruct((total, size), BF16),
+        in_specs=[pl.BlockSpec(memory_space=VMEM)] * 4,
         out_specs=pl.BlockSpec(memory_space=VMEM),
         compiler_params=pltpu.CompilerParams(vmem_limit_bytes=SMALL),
         name="fronts",
-    )(rows, inverse, coupling)
+    )(rows, inverse, coupling, source)
+
+
+class Front:
+    def __init__(self, ref, like):
+        count, modes, size = like.shape
+        self.ref, self.modes, self.size, self.rows = ref, modes, size, count * modes
+
+    def __getitem__(self, which):
+        half = self.modes * self.size
+        return self.ref[which * half : (which + 1) * half, :].reshape(self.modes, self.size, self.size)
+
+    def source(self):
+        at = 2 * self.modes * self.size
+        parts = [self.ref[at + p * self.rows : at + (p + 1) * self.rows, :].astype(F32) for p in range(3)]
+        return parts[0] + parts[1] + parts[2]
 
 
 def apply_rows(x, matrix):
@@ -376,29 +421,30 @@
 
 
 def rise_kernel(one_ref, two_ref, source_ref, front_ref, reduced_ref, outgoing_ref):
+    front_ref = Front(front_ref, one_ref)
     g = (flat(source_ref) - (flat(one_ref) + flat(two_ref))).astype(BF16)
     reduced = apply_rows(g, front_ref[0]).astype(BF16)
     reduced_ref[...] = reduced.astype(F32).reshape(reduced_ref.shape)
     outgoing_ref[...] = apply_rows(reduced, front_ref[1]).reshape(outgoing_ref.shape)
 
 
-def small_call(kernel, name, outs, args, scalars=0):
+def small_call(kernel, outs, args):
     return pl.pallas_call(
         kernel,
         out_shape=outs,
-        in_specs=[pl.BlockSpec(memory_space=SMEM)] * scalars
-        + [pl.BlockSpec(memory_space=VMEM)] * (len(args) - scalars),
+        in_specs=[pl.BlockSpec(memory_space=VMEM)] * len(args),
         out_specs=[pl.BlockSpec(memory_space=VMEM)] * len(outs),
         compiler_params=pltpu.CompilerParams(vmem_limit_bytes=SMALL),
-        name=name,
     )(*args)
 
 
-def crown_kernel(high_ref, one_ref, two_ref, reduced_ref, front_ref, fa_ref, sa_ref, fb_ref, sb_ref, x_ref, x16_ref, far_ref):
-    def solve(f_mid, s_mid, f_top, s_top, send_mid):
-        g = (flat(s_mid) - (flat(one_ref) + flat(two_ref))).astype(BF16)
+def crown_kernel(high, one_ref, two_ref, reduced_ref, front_ref, fa_ref, fb_ref, x_ref, x16_ref, far_ref):
+    front_ref, front_a, front_b = (Front(ref, one_ref) for ref in (front_ref, fa_ref, fb_ref))
+
+    def solve(f_mid, f_top, send_mid):
+        g = (f_mid.source() - (flat(one_ref) + flat(two_ref))).astype(BF16)
         mid = apply_rows(g, f_mid[0]).astype(BF16)
-        g = (flat(s_top) - apply_rows(mid, f_mid[1])).astype(BF16)
+        g = (f_top.source() - apply_rows(mid, f_mid[1])).astype(BF16)
         top = apply_columns(apply_rows(g, f_top[0]).astype(BF16), f_top[0])
         residue = mid.astype(F32) - apply_columns(top.astype(BF16), f_mid[1])
         x_mid = apply_columns(residue.astype(BF16), f_mid[0])
@@ -408,16 +454,17 @@
         x_ref[...] = x.reshape(x_ref.shape)
         x16_ref[...] = x.astype(BF16).reshape(x_ref.shape)
 
-    @pl.when(high_ref[0] == 0)
+    @pl.when(lax.axis_index("mesh") != high)
     def _():
-        solve(fa_ref, sa_ref, fb_ref, sb_ref, False)
-
-    @pl.when(high_ref[0] != 0)
+        solve(front_a, front_b, False)
+
+    @pl.when(lax.axis_index("mesh") == high)
     def _():
-        solve(fb_ref, sb_ref, fa_ref, sa_ref, True)
+        solve(front_b, front_a, True)
 
 
 def sink_kernel(one_ref, two_ref, reduced_ref, front_ref, x_ref, x16_ref):
+    front_ref = Front(front_ref, one_ref)
     above = (flat(one_ref).astype(F32) + flat(two_ref).astype(F32)).astype(BF16)
     residue = flat(reduced_ref) - apply_columns(above, front_ref[1])
     x = apply_columns(residue.astype(BF16), front_ref[0])
@@ -429,10 +476,15 @@
     return levels + 1 if q == 0 else (q & -q).bit_length()
 
 
-def choose_kernel(level_ref, *refs):
+def choose_kernel(*refs):
+    position = lax.axis_index("mesh")
+    last = len(refs) - 2
     for at, ref in enumerate(refs[:-1]):
-
-        @pl.when(level_ref[0] == at)
+        here = position % 2**at == 0
+        if at < last:
+            here &= position % 2 ** (at + 1) != 0
+
+        @pl.when(here)
         def _(ref=ref):
             refs[-1][...] = ref[...]
 
@@ -451,35 +503,31 @@
     partitions = lax.axis_size("mesh")
     levels = partitions.bit_length() - 1
     modes, nodes = velocity.shape[2], velocity.shape[3]
-    here = lax.axis_index("mode")
-    me = here.reshape(1).astype(jnp.int32)
-    position = lax.axis_index("mesh")
     exchange = [[(g, g ^ k) for g in range(groups)] for k in range(groups)]
     low, mid, high = partitions // 4, partitions // 2, 3 * partitions // 4
 
     def swap(pieces):
-        return [pieces[0]] + [
-            lax.ppermute(pieces[k], "mode", exchange[k]) for k in range(1, groups)
-        ]
+        out = [pieces[0]]
+        for k in range(1, groups):
+            out.append(lax.ppermute(pieces[k], "mode", exchange[k]))
+        return out
 
     def hop(value, pairs):
         return lax.ppermute(value, "mesh", pairs)
 
-    packed = pack(me, velocity.reshape(6 * modes, nodes), magnetic.reshape(6 * modes, nodes), groups)
+    packed = pack(stay(velocity.reshape(6 * modes, nodes)), stay(magnetic.reshape(6 * modes, nodes)), groups)
     spread_in = swap(packed)
-    fwd, bwd = tables(me, groups, modes)
-    rows_leaf, rows_front = front_rows[0, 0:1], front_rows[0, 1:2]
-    front = fronts(rows_front, separator_inverse, separator_coupling)
-    to_a, to_b = [(mid, low), (0, high)], [(mid, high), (0, low)]
-    front_a, front_b = hop(front, to_a), hop(front, to_b)
-    source_a, source_b = hop(separator_source, to_a), hop(separator_source, to_b)
-    square, joint = compose(leaf_inverse, leaf_coupling)
+    fwd, bwd = tables(groups, modes)
+    front = fronts(front_rows, separator_inverse, separator_coupling, separator_source)
+    front_a = hop(front, [(mid, low), (0, high)])
+    front_b = hop(front, [(mid, high), (0, low)])
+    square, joint = compose(stay(leaf_inverse), stay(leaf_coupling))
     azi, rest = transform(fwd, bwd, spread_in)
     azi = swap(azi)
     rest = swap(rest)
-    source, update = leaf_up(me, rows_leaf, magnetic, azi, joint)
+    source, update = leaf_up(front_rows, stay(magnetic), azi, joint)
     local = leaf_local(source, square)
-    nonlinear = spread(me, azi, rest).reshape(3, 2, modes, nodes)
+    nonlinear = spread(azi, rest).reshape(3, 2, modes, nodes)
 
     of_level = [[q for q in range(partitions) if level_of(q, levels) == h] for h in range(levels + 2)]
     wide = jax.ShapeDtypeStruct(separator_source.shape, F32)
@@ -491,35 +539,25 @@
             gap = 2 ** (height - 2)
             one = hop(outgoing, [(q - gap, q) for q in of_level[height]])
             two = hop(outgoing, [(q + gap, q) for q in of_level[height]])
-        reduced[height], outgoing = small_call(
-            rise_kernel, "rise", [wide, wide], [one, two, separator_source, front]
-        )
+        reduced[height], outgoing = small_call(rise_kernel, [wide, wide], [one, two, separator_source, front])
     other = hop(outgoing, [(low, high), (high, low)])
-    is_high = (position == high).astype(jnp.int32).reshape(1)
     x, x16, far = small_call(
-        crown_kernel,
-        "crown",
+        functools.partial(crown_kernel, high),
         [wide, half, wide],
-        [is_high, outgoing, other, reduced[levels - 1], front, front_a, source_a, front_b, source_b],
-        scalars=1,
+        [outgoing, other, reduced[levels - 1], front, front_a, front_b],
     )
     answers = [(levels - 1, x)]
     for height in range(levels - 2, 0, -1):
         gap = 2 ** (height - 1)
         one = hop(x16, [(q, q - gap) for q in of_level[height + 1]])
         two = hop(x16, [(q, q + gap) for q in of_level[height + 1]])
-        x, x16 = small_call(sink_kernel, "sink", [wide, half], [one, two, reduced[height], front])
+        x, x16 = small_call(sink_kernel, [wide, half], [one, two, reduced[height], front])
         answers.append((height, x))
     far = hop(far, [(low, 0), (high, mid)])
     beside = hop(x16, [(q, q - 1) for q in of_level[1]])
-    level_here = sum((position % 2**t == 0).astype(jnp.int32) for t in range(1, levels + 1)) + 1
-    own = (level_here == 1).astype(jnp.int32).reshape(1)
-    azimuthal = leaf_down(own, rows_leaf, x16, beside, local, joint)
+    azimuthal = leaf_down(front_rows, x16, beside, local, joint)
     answers.reverse()
-    place = (jnp.minimum(level_here, levels) - 1).reshape(1)
-    (solution,) = small_call(
-        choose_kernel, "choose", [wide], [place] + [x for _, x in answers] + [far], scalars=1
-    )
+    (solution,) = small_call(choose_kernel, [wide], [x for _, x in answers] + [far])
     return (nonlinear, azimuthal, solution)
 
 
@@ -535,4 +573,6 @@
         P("mesh", None, None),
     )
     out_specs = (P(None, None, "mode", "mesh"), P(None, "mode", "mesh"), P(None, "mode", "mesh"))
+
+
     return jax.shard_map(shards, mesh=mesh, in_specs=in_specs, out_specs=out_specs, check_vma=False)

time: 110 us -> 75.1 us (0.68)
  local copies, waits for them, and re-layouts: 31.5 us -> 3.48 us
  Pallas kernels: 34.1 us -> 29.1 us
  starting transfers between devices: 22.5 us -> 20.2 us
    unnamed x70 -> x12, local copies, waits for them, and re-layouts: 30.3 us -> 3.48 us
    pallas_call x1, Pallas kernels: 15.2 us -> 9.77 us  [compose(): pl.pallas_call(compose_kernel, out_shape=[jax.ShapeDtypeStruct(inverse.sh...]
    ppermute x12 -> x10, starting transfers between devices: 14.5 us -> 12 us  [hop(): return lax.ppermute(value, 'mesh', pairs)]
    pallas_call x1, Pallas kernels: 0.1 us -> 1.71 us  [pack(): pl.pallas_call(functools.partial(pack_kernel, groups), out_shape=[jax.Sha...]
    squeeze x1 -> x0, local copies, waits for them, and re-layouts: 1.26 us -> none  [shards(): rows_leaf, rows_front = (front_rows[0, 0:1], front_rows[0, 1:2])]
    ppermute x12 -> x10, waiting for transfers between devices: 11.5 us -> 11.9 us  [hop(): return lax.ppermute(value, 'mesh', pairs)]
  transfers between devices with their start and end apart: 21 -> 19, of which waited for: 5 -> 6; matrix products, arithmetic and copies ran while one was open for 0% -> 0% of each run, Pallas kernels for 30% -> 38%
where the time goes in v3:
time: 75.1 us; the launch traced here: 73.9 us
  Pallas kernels  29.1 us (39%)
  waiting for transfers between devices  20.3 us (27%)
  starting transfers between devices  20.2 us (27%)
  local copies, waits for them, and re-layouts  3.48 us (5%)
  between operations  0.88 us (1%)
    ppermute x10, starting transfers between devices, hop(): return lax.ppermute(value, 'mesh', pairs)  12 us
    ppermute x10, waiting for transfers between devices, hop(): return lax.ppermute(value, 'mesh', pairs)  11.9 us
    pallas_call x1, Pallas kernels, compose(): pl.pallas_call(compose_kernel, out_shape=[jax.ShapeDtypeStruct(inverse.sh...  9.77 us
    ppermute x9, waiting for transfers between devices, swap(): out.append(lax.ppermute(pieces[k], 'mode', exchange[k]))  8.41 us
    ppermute x9, starting transfers between devices, swap(): out.append(lax.ppermute(pieces[k], 'mode', exchange[k]))  8.14 us
    pallas_call x1, Pallas kernels, leaf_up(): pl.pallas_call(functools.partial(leaf_up_kernel, groups), out_shape=[jax....  5.65 us
    pallas_call x5, Pallas kernels, small_call(): pl.pallas_call(kernel, out_shape=outs, in_specs=[pl.BlockSpec(memory_spac...  3.66 us
    unnamed x12, local copies, waits for them, and re-layouts  3.48 us
  transfers between devices with their start and end apart: 19, of which 6 were waited for; matrix products, arithmetic and copies ran while one was open for 0% of the time, Pallas kernels for 38%

profile of v3, /device:TPU:9, one launch (start us, length us, event | category | flops | bytes accessed | tf_op | source)
XLA Modules:
  0.0 73.9 jit_solution(10430159955790676121)
XLA Ops:
  0.6 0.0 copy-start
  0.6 1.0 %copy-done = bf16[16,128,128]{2,1,0:T(8,128)(2,1)S(1)} copy-done((bf16[16,128,128]{2,1,0:T(8,128)(2,1)S(1)}, bf16[16,128,128]{2,1,0:T(8,128)(2,1)}, u32[]{:S(2)}) %copy-start) | copy-done | bytes 524312
  1.7 0.0 copy-start.1
  1.7 1.0 %copy-done.1 = bf16[16,128,128]{2,1,0:T(8,128)(2,1)S(1)} copy-done((bf16[16,128,128]{2,1,0:T(8,128)(2,1)S(1)}, bf16[16,128,128]{2,1,0:T(8,128)(2,1)}, u32[]{:S(2)}) %copy-start.1) | copy-done | bytes 524312
  2.7 0.0 copy-start.2
  2.7 0.7 copy-done.2
  3.4 0.0 copy-start.4
  3.4 0.7 copy-done.4
  4.1 0.4 fronts.1.front_ref
  4.5 0.7 collective-permute-start.13
  5.3 0.7 collective-permute-start.14
  6.0 1.7 %pack.1 = (bf16[192,640]{1,0:T(8,128)(2,1)S(1)}, bf16[192,640]{1,0:T(8,128)(2,1)S(1)}, bf16[192,640]{1,0:T(8,128)(2,1)S(1)}, bf16[192,640]{1,0:T(8,128)(2,1)S(1)}) custom-call(f32[96,2560]{1,0:T(8,128)} %bitcast.4, f32[96,2560]{1,0:T(8,128)} %bitcast.3), custom_call_target="tpu_custom_call" | custom-call | tf_op jit(solution)/shard_map/pack/pallas_call | solution.py:81
  7.7 1.3 %collective-permute-start = (bf16[192,640]{1,0:T(8,128)(2,1)S(1)}, bf16[192,640]{1,0:T(8,128)(2,1)S(1)}, u32[]{:S(2)}, u32[]{:S(2)}) collective-permute-start(bf16[192,640]{1,0:T(8,128)(2,1)S(1)} %get-tuple-element.33), channel_id=1, source_target_pairs={{0,8},{8,0},{16,24},{24,16},{1,9},{9,1},{17,25},{25,17},{2,10},{10... | collective-permute-start | bytes 737288 | tf_op jit(solution)/shard_map/ppermute | solution.py:512
  9.0 1.2 %collective-permute-start.1 = (bf16[192,640]{1,0:T(8,128)(2,1)S(1)}, bf16[192,640]{1,0:T(8,128)(2,1)S(1)}, u32[]{:S(2)}, u32[]{:S(2)}) collective-permute-start(bf16[192,640]{1,0:T(8,128)(2,1)S(1)} %get-tuple-element.34), channel_id=1, source_target_pairs={{0,16},{8,24},{16,0},{24,8},{1,17},{9,25},{17,1},{25,9},{2,18},{10... | collective-permute-start | bytes 737288 | tf_op jit(solution)/shard_map/ppermute | solution.py:512
  10.2 0.2 collective-permute-start.2
  10.4 0.9 %tables.1 = (bf16[192,128]{1,0:T(8,128)(2,1)S(1)}, bf16[128,192]{1,0:T(8,128)(2,1)S(1)}) custom-call(), custom_call_target="tpu_custom_call" | custom-call | tf_op jit(solution)/shard_map/tables/pallas_call | solution.py:50
  11.3 2.2 %collective-permute-done.refs_1_ = bf16[192,640]{1,0:T(8,128)(2,1)S(1)} collective-permute-done((bf16[192,640]{1,0:T(8,128)(2,1)S(1)}, bf16[192,640]{1,0:T(8,128)(2,1)S(1)}, u32[]{:S(2)}, u32[]{:S(2)}) %collective-permute-start) | collective-permute-done | bytes 245792 | tf_op jit(solution)/shard_map/ppermute | solution.py:512
  13.5 1.3 %collective-permute-done.1.refs_2_ = bf16[192,640]{1,0:T(8,128)(2,1)S(1)} collective-permute-done((bf16[192,640]{1,0:T(8,128)(2,1)S(1)}, bf16[192,640]{1,0:T(8,128)(2,1)S(1)}, u32[]{:S(2)}, u32[]{:S(2)}) %collective-permute-start.1) | collective-permute-done | bytes 245792 | tf_op jit(solution)/shard_map/ppermute | solution.py:512
  14.8 4.9 %collective-permute-done.2.refs_3_ = bf16[192,640]{1,0:T(8,128)(2,1)S(1)} collective-permute-done((bf16[192,640]{1,0:T(8,128)(2,1)S(1)}, bf16[192,640]{1,0:T(8,128)(2,1)S(1)}, u32[]{:S(2)}, u32[]{:S(2)}) %collective-permute-start.2) | collective-permute-done | bytes 245792 | tf_op jit(solution)/shard_map/ppermute | solution.py:512
  19.7 0.8 %transform.1 = (bf16[32,640]{1,0:T(8,128)(2,1)S(1)}, bf16[32,640]{1,0:T(8,128)(2,1)S(1)}, bf16[32,640]{1,0:T(8,128)(2,1)S(1)}, bf16[32,640]{1,0:T(8,128)(2,1)S(1...) custom-call(bf16[192,128]{1,0:T(8,128)(2,1)S(1)} %get-tuple-element., ...), custom_call_target="tpu_custom_call" | custom-call | tf_op jit(solution)/shard_map/transform/pallas_call | solution.py:118
  20.6 1.3 %collective-permute-start.3 = (bf16[32,640]{1,0:T(8,128)(2,1)S(1)}, bf16[32,640]{1,0:T(8,128)(2,1)S(1)}, u32[]{:S(2)}, u32[]{:S(2)}) collective-permute-start(bf16[32,640]{1,0:T(8,128)(2,1)S(1)} %get-tuple-element.37), channel_id=1, source_target_pairs={{0,8},{8,0},{16,24},{24,16},{1,9},{9,1},{17,25},{25,17},{2,10},{10... | collective-permute-start | bytes 122888 | tf_op jit(solution)/shard_map/ppermute | solution.py:512
  21.8 0.2 collective-permute-start.4
  22.1 0.0 copy-start.5
  22.1 1.2 %collective-permute-start.5 = (bf16[32,640]{1,0:T(8,128)(2,1)S(1)}, bf16[32,640]{1,0:T(8,128)(2,1)S(1)}, u32[]{:S(2)}, u32[]{:S(2)}) collective-permute-start(bf16[32,640]{1,0:T(8,128)(2,1)S(1)} %get-tuple-element.39), channel_id=1, source_target_pairs={{0,24},{8,16},{16,8},{24,0},{1,25},{9,17},{17,9},{25,1},{2,26},{10... | collective-permute-start | bytes 122888 | tf_op jit(solution)/shard_map/ppermute | solution.py:512
  23.3 9.8 %compose.1 = (bf16[16,20,128,128]{3,2,1,0:T(8,128)(2,1)S(1)}, bf16[16,128,2560]{2,1,0:T(8,128)(2,1)S(1)}) custom-call(bf16[16,20,128,128]{3,2,1,0:T(8,128)(2,1)} %inv_hbm.1, bf16[16,128,2560]{2,1,0:T(8,128)(2,1)} %cpl_hbm.1), custom_call_target="tpu_custom_call" | custom-call | flops 5368709120 | bytes 41943040 | tf_op jit(solution)/shard_map/compose/pallas_call | solution.py:184
  33.1 0.0 copy-start.3
  33.1 0.0 collective-permute-done.3.refs_1_
  33.1 0.0 collective-permute-done.4.refs_2_
  33.1 0.0 collective-permute-done.5.refs_3_
  33.1 0.0 copy-done.5
  33.1 5.6 %leaf_up.1 = (f32[2,16,2560]{2,1,0:T(8,128)S(1)}, f32[2,16,128]{2,1,0:T(8,128)S(1)}) custom-call(s32[1,2,128]{2,1,0:T(2,128)S(1)} %copy-done.5, f32[3,2,16,2560]{3,2,1,0:T(8,128)} %mag_hbm.1, bf16[16,128,2560]{2,1,0:T(8,128)(2,1)S(1)} %get-tuple-element.44.joint_ref, bf16[32,640]{1,0:T(8,128)(2,1)S(1)} %get-tuple-element.36.refs_0_, ...), custom_call_target="tpu_custom_call" | custom-call | flops 671088640 | bytes 10485760 | tf_op jit(solution)/shard_map/leaf_up/pallas_call | solution.py:236
  38.8 1.3 %collective-permute-start.9 = (f32[2,16,128]{2,1,0:T(8,128)S(1)}, f32[2,16,128]{2,1,0:T(8,128)S(1)}, u32[]{:S(2)}, u32[]{:S(2)}) collective-permute-start(f32[2,16,128]{2,1,0:T(8,128)S(1)} %get-tuple-element.45.one_ref), channel_id=1, source_target_pairs={{0,1},{2,3},{4,5},{6,7},{8,9},{10,11},{12,13},{14,15},{16,17},{18,... | collective-permute-start | bytes 49160 | tf_op jit(solution)/shard_map/ppermute | solution.py:516
  40.1 4.4 %collective-permute-done.9.two_ref = f32[2,16,128]{2,1,0:T(8,128)S(1)} collective-permute-done((f32[2,16,128]{2,1,0:T(8,128)S(1)}, f32[2,16,128]{2,1,0:T(8,128)S(1)}, u32[]{:S(2)}, u32[]{:S(2)}) %collective-permute-start.9) | collective-permute-done | bytes 16416 | tf_op jit(solution)/shard_map/ppermute | solution.py:516
  44.5 0.0 copy-done.3
  44.5 0.5 shard_map.103
  45.0 0.7 collective-permute-start.10
  45.7 2.7 %collective-permute-start.11 = (f32[2,16,128]{2,1,0:T(8,128)S(1)}, f32[2,16,128]{2,1,0:T(8,128)S(1)}, u32[]{:S(2)}, u32[]{:S(2)}) collective-permute-start(f32[2,16,128]{2,1,0:T(8,128)S(1)} %get-tuple-element.46), channel_id=1, source_target_pairs={{3,2},{7,6},{11,10},{15,14},{19,18},{23,22},{27,26},{31,30}} | collective-permute-start | bytes 49160 | tf_op jit(solution)/shard_map/ppermute | solution.py:516
  48.4 0.0 collective-permute-done.10.one_ref
  48.4 0.8 %collective-permute-done.11.two_ref = f32[2,16,128]{2,1,0:T(8,128)S(1)} collective-permute-done((f32[2,16,128]{2,1,0:T(8,128)S(1)}, f32[2,16,128]{2,1,0:T(8,128)S(1)}, u32[]{:S(2)}, u32[]{:S(2)}) %collective-permute-start.11) | collective-permute-done | bytes 16416 | tf_op jit(solution)/shard_map/ppermute | solution.py:516
  49.2 0.5 shard_map.104
  49.7 0.7 collective-permute-start.12
  50.4 1.0 %collective-permute-start.6 = (bf16[64,640]{1,0:T(8,128)(2,1)S(1)}, bf16[64,640]{1,0:T(8,128)(2,1)S(1)}, u32[]{:S(2)}, u32[]{:S(2)}) collective-permute-start(bf16[64,640]{1,0:T(8,128)(2,1)S(1)} %get-tuple-element.41), channel_id=1, source_target_pairs={{0,8},{8,0},{16,24},{24,16},{1,9},{9,1},{17,25},{25,17},{2,10},{10... | collective-permute-start | bytes 245768 | tf_op jit(solution)/shard_map/ppermute | solution.py:512
  51.4 0.6 collective-permute-start.7
  52.0 0.0 collective-permute-done.12.two_ref
  52.0 1.1 %collective-permute-start.8 = (bf16[64,640]{1,0:T(8,128)(2,1)S(1)}, bf16[64,640]{1,0:T(8,128)(2,1)S(1)}, u32[]{:S(2)}, u32[]{:S(2)}) collective-permute-start(bf16[64,640]{1,0:T(8,128)(2,1)S(1)} %get-tuple-element.43), channel_id=1, source_target_pairs={{0,24},{8,16},{16,8},{24,0},{1,25},{9,17},{17,9},{25,1},{2,26},{10... | collective-permute-start | bytes 245768 | tf_op jit(solution)/shard_map/ppermute | solution.py:512
  53.1 0.0 collective-permute-done.13.fa_ref
  53.1 0.0 collective-permute-done.14.fb_ref
  53.1 1.7 %shard_map.105 = (f32[2,16,128]{2,1,0:T(8,128)S(1)}, bf16[2,16,128]{2,1,0:T(8,128)(2,1)S(1)}, f32[2,16,128]{2,1,0:T(8,128)S(1)}) custom-call(f32[2,16,128]{2,1,0:T(8,128)S(1)} %get-tuple-element.47.one_ref, f32[2,16,128]{2,1,0:T(8,128)S(1)} %collective-permute-done.12.two_ref, f32[2,16,128]{2,1,0:T(8,128)S(1)} %get-tuple-element.48.reduced_ref, ...), custom_call_target="tpu_custom_call" | custom-call | tf_op jit(solution)/shard_map/pallas_call | solution.py:432
  54.8 0.7 collective-permute-start.15
  55.5 1.3 %collective-permute-start.16 = (bf16[2,16,128]{2,1,0:T(8,128)(2,1)S(1)}, bf16[2,16,128]{2,1,0:T(8,128)(2,1)S(1)}, u32[]{:S(2)}, u32[]{:S(2)}) collective-permute-start(bf16[2,16,128]{2,1,0:T(8,128)(2,1)S(1)} %get-tuple-element.49), channel_id=1, source_target_pairs={{2,3},{6,7},{10,11},{14,15},{18,19},{22,23},{26,27},{30,31}} | collective-permute-start | bytes 24584 | tf_op jit(solution)/shard_map/ppermute | solution.py:516
  56.8 0.0 collective-permute-done.15.one_ref
  56.8 0.7 collective-permute-start.18
  57.5 6.7 %collective-permute-done.16.two_ref = bf16[2,16,128]{2,1,0:T(8,128)(2,1)S(1)} collective-permute-done((bf16[2,16,128]{2,1,0:T(8,128)(2,1)S(1)}, bf16[2,16,128]{2,1,0:T(8,128)(2,1)S(1)}, u32[]{:S(2)}, u32[]{:S(2)}) %collective-permute-start.16) | collective-permute-done | bytes 8224 | tf_op jit(solution)/shard_map/ppermute | solution.py:516
  64.1 0.4 shard_map.106
  64.5 2.6 %collective-permute-start.17 = (bf16[2,16,128]{2,1,0:T(8,128)(2,1)S(1)}, bf16[2,16,128]{2,1,0:T(8,128)(2,1)S(1)}, u32[]{:S(2)}, u32[]{:S(2)}) collective-permute-start(bf16[2,16,128]{2,1,0:T(8,128)(2,1)S(1)} %get-tuple-element.51.here_ref), channel_id=1, source_target_pairs={{1,0},{3,2},{5,4},{7,6},{9,8},{11,10},{13,12},{15,14},{17,16},{19,... | collective-permute-start | bytes 24584 | tf_op jit(solution)/shard_map/ppermute | solution.py:516
  67.1 2.4 %leaf_local.1.local_ref = f32[2,16,2560]{2,1,0:T(8,128)S(1)} custom-call(f32[2,16,2560]{2,1,0:T(8,128)S(1)} %get-tuple-element.52.source_ref, bf16[16,20,128,128]{3,2,1,0:T(8,128)(2,1)S(1)} %get-tuple-element.53.square_ref), custom_call_target="tpu_custom_call" | custom-call | flops 671088640 | bytes 10485760 | tf_op jit(solution)/shard_map/leaf_local/pallas_call | solution.py:285
  69.5 0.0 collective-permute-done.6.refs_5_
  69.5 0.0 collective-permute-done.7.refs_6_
  69.5 0.0 collective-permute-done.8.refs_7_
  69.5 1.0 %spread.1 = f32[96,2560]{1,0:T(8,128)} custom-call(bf16[32,640]{1,0:T(8,128)(2,1)S(1)} %get-tuple-element.36.refs_0_, bf16[32,640]{1,0:T(8,128)(2,1)S(1)} %collective-permute-done.3.refs_1_, bf16[32,640]{1,0:T(8,128)(2,1)S(1)} %collective-permute-done.4.refs_2_, bf16[32,640]{1,0:T(8,128)(2,1)S(1)} %collective-permute-done.5.refs_3_, ...), custom_call_target="tpu_custom_call" | custom-call | tf_op jit(solution)/shard_map/spread/pallas_call | solution.py:347
  70.6 0.0 collective-permute-done.17.beside_ref
  70.6 2.8 %leaf_down.1 = f32[2,16,2560]{2,1,0:T(8,128)} custom-call(s32[1,2,128]{2,1,0:T(2,128)S(1)} %copy-done.5, bf16[2,16,128]{2,1,0:T(8,128)(2,1)S(1)} %get-tuple-element.51.here_ref, bf16[2,16,128]{2,1,0:T(8,128)(2,1)S(1)} %collective-permute-done.17.beside_ref, f32[2,16,2560]{2,1,0:T(8,128)S(1)} %leaf_local.1.local_ref, ...), custom_call_target="tpu_custom_call" | custom-call | tf_op jit(solution)/shard_map/leaf_down/pallas_call | solution.py:323
  73.3 0.0 collective-permute-done.18.refs_2_
  73.3 0.6 shard_map.107
Async XLA Ops:
  0.6 1.0 %copy-start = (bf16[16,128,128]{2,1,0:T(8,128)(2,1)S(1)}, bf16[16,128,128]{2,1,0:T(8,128)(2,1)}, u32[]{:S(2)}) copy-start(bf16[16,128,128]{2,1,0:T(8,128)(2,1)} %inv_ref.1) | copy-start | bytes 1572868
  1.7 1.0 %copy-start.1 = (bf16[16,128,128]{2,1,0:T(8,128)(2,1)S(1)}, bf16[16,128,128]{2,1,0:T(8,128)(2,1)}, u32[]{:S(2)}) copy-start(bf16[16,128,128]{2,1,0:T(8,128)(2,1)} %cpl_ref.1) | copy-start | bytes 1572868
  2.7 0.7 copy-start.2
  3.4 0.7 copy-start.4
  4.5 48.6 %collective-permute-start.13 = (bf16[4192,128]{1,0:T(8,128)(2,1)S(1)}, bf16[4192,128]{1,0:T(8,128)(2,1)S(1)}, u32[]{:S(2)}, u32[]{:S(2)}) collective-permute-start(bf16[4192,128]{1,0:T(8,128)(2,1)S(1)} %fronts.1.front_ref), channel_id=1, source_target_pairs={{4,2},{0,6},{12,10},{8,14},{20,18},{16,22},{28,26},{24,30}} | collective-permute-start | bytes 3219464 | tf_op jit(solution)/shard_map/ppermute | solution.py:516
  5.3 47.9 %collective-permute-start.14 = (bf16[4192,128]{1,0:T(8,128)(2,1)S(1)}, bf16[4192,128]{1,0:T(8,128)(2,1)S(1)}, u32[]{:S(2)}, u32[]{:S(2)}) collective-permute-start(bf16[4192,128]{1,0:T(8,128)(2,1)S(1)} %fronts.1.front_ref), channel_id=1, source_target_pairs={{4,6},{0,2},{12,14},{8,10},{20,22},{16,18},{28,30},{24,26}} | collective-permute-start | bytes 3219464 | tf_op jit(solution)/shard_map/ppermute | solution.py:516
  7.7 5.8 %collective-permute-start = (bf16[192,640]{1,0:T(8,128)(2,1)S(1)}, bf16[192,640]{1,0:T(8,128)(2,1)S(1)}, u32[]{:S(2)}, u32[]{:S(2)}) collective-permute-start(bf16[192,640]{1,0:T(8,128)(2,1)S(1)} %get-tuple-element.33), channel_id=1, source_target_pairs={{0,8},{8,0},{16,24},{24,16},{1,9},{9,1},{17,25},{25,17},{2,10},{10... | collective-permute-start | bytes 737288 | tf_op jit(solution)/shard_map/ppermute | solution.py:512
  9.0 5.8 %collective-permute-start.1 = (bf16[192,640]{1,0:T(8,128)(2,1)S(1)}, bf16[192,640]{1,0:T(8,128)(2,1)S(1)}, u32[]{:S(2)}, u32[]{:S(2)}) collective-permute-start(bf16[192,640]{1,0:T(8,128)(2,1)S(1)} %get-tuple-element.34), channel_id=1, source_target_pairs={{0,16},{8,24},{16,0},{24,8},{1,17},{9,25},{17,1},{25,9},{2,18},{10... | collective-permute-start | bytes 737288 | tf_op jit(solution)/shard_map/ppermute | solution.py:512
  10.2 9.5 %collective-permute-start.2 = (bf16[192,640]{1,0:T(8,128)(2,1)S(1)}, bf16[192,640]{1,0:T(8,128)(2,1)S(1)}, u32[]{:S(2)}, u32[]{:S(2)}) collective-permute-start(bf16[192,640]{1,0:T(8,128)(2,1)S(1)} %get-tuple-element.35), channel_id=1, source_target_pairs={{0,24},{8,16},{16,8},{24,0},{1,25},{9,17},{17,9},{25,1},{2,26},{10... | collective-permute-start | bytes 737288 | tf_op jit(solution)/shard_map/ppermute | solution.py:512
  20.6 12.5 %collective-permute-start.3 = (bf16[32,640]{1,0:T(8,128)(2,1)S(1)}, bf16[32,640]{1,0:T(8,128)(2,1)S(1)}, u32[]{:S(2)}, u32[]{:S(2)}) collective-permute-start(bf16[32,640]{1,0:T(8,128)(2,1)S(1)} %get-tuple-element.37), channel_id=1, source_target_pairs={{0,8},{8,0},{16,24},{24,16},{1,9},{9,1},{17,25},{25,17},{2,10},{10... | collective-permute-start | bytes 122888 | tf_op jit(solution)/shard_map/ppermute | solution.py:512
  21.8 11.2 %collective-permute-start.4 = (bf16[32,640]{1,0:T(8,128)(2,1)S(1)}, bf16[32,640]{1,0:T(8,128)(2,1)S(1)}, u32[]{:S(2)}, u32[]{:S(2)}) collective-permute-start(bf16[32,640]{1,0:T(8,128)(2,1)S(1)} %get-tuple-element.38), channel_id=1, source_target_pairs={{0,16},{8,24},{16,0},{24,8},{1,17},{9,25},{17,1},{25,9},{2,18},{10... | collective-permute-start | bytes 122888 | tf_op jit(solution)/shard_map/ppermute | solution.py:512
  22.1 11.0 %copy-start.5 = (s32[1,2,128]{2,1,0:T(2,128)S(1)}, s32[1,2,128]{2,1,0:T(2,128)}, u32[]{:S(2)}) copy-start(s32[1,2,128]{2,1,0:T(2,128)} %rows_ref.5) | copy-start | bytes 3076
  22.1 11.0 %collective-permute-start.5 = (bf16[32,640]{1,0:T(8,128)(2,1)S(1)}, bf16[32,640]{1,0:T(8,128)(2,1)S(1)}, u32[]{:S(2)}, u32[]{:S(2)}) collective-permute-start(bf16[32,640]{1,0:T(8,128)(2,1)S(1)} %get-tuple-element.39), channel_id=1, source_target_pairs={{0,24},{8,16},{16,8},{24,0},{1,25},{9,17},{17,9},{25,1},{2,26},{10... | collective-permute-start | bytes 122888 | tf_op jit(solution)/shard_map/ppermute | solution.py:512
  33.1 11.4 %copy-start.3 = (f32[2,16,128]{2,1,0:T(8,128)S(1)}, f32[2,16,128]{2,1,0:T(8,128)}, u32[]{:S(2)}) copy-start(f32[2,16,128]{2,1,0:T(8,128)} %source_ref.5) | copy-start | bytes 49156
  38.8 5.7 %collective-permute-start.9 = (f32[2,16,128]{2,1,0:T(8,128)S(1)}, f32[2,16,128]{2,1,0:T(8,128)S(1)}, u32[]{:S(2)}, u32[]{:S(2)}) collective-permute-start(f32[2,16,128]{2,1,0:T(8,128)S(1)} %get-tuple-element.45.one_ref), channel_id=1, source_target_pairs={{0,1},{2,3},{4,5},{6,7},{8,9},{10,11},{12,13},{14,15},{16,17},{18,... | collective-permute-start | bytes 49160 | tf_op jit(solution)/shard_map/ppermute | solution.py:516
  45.0 3.4 %collective-permute-start.10 = (f32[2,16,128]{2,1,0:T(8,128)S(1)}, f32[2,16,128]{2,1,0:T(8,128)S(1)}, u32[]{:S(2)}, u32[]{:S(2)}) collective-permute-start(f32[2,16,128]{2,1,0:T(8,128)S(1)} %get-tuple-element.46), channel_id=1, source_target_pairs={{1,2},{5,6},{9,10},{13,14},{17,18},{21,22},{25,26},{29,30}} | collective-permute-start | bytes 49160 | tf_op jit(solution)/shard_map/ppermute | solution.py:516
  45.7 3.5 %collective-permute-start.11 = (f32[2,16,128]{2,1,0:T(8,128)S(1)}, f32[2,16,128]{2,1,0:T(8,128)S(1)}, u32[]{:S(2)}, u32[]{:S(2)}) collective-permute-start(f32[2,16,128]{2,1,0:T(8,128)S(1)} %get-tuple-element.46), channel_id=1, source_target_pairs={{3,2},{7,6},{11,10},{15,14},{19,18},{23,22},{27,26},{31,30}} | collective-permute-start | bytes 49160 | tf_op jit(solution)/shard_map/ppermute | solution.py:516
  49.7 2.3 %collective-permute-start.12 = (f32[2,16,128]{2,1,0:T(8,128)S(1)}, f32[2,16,128]{2,1,0:T(8,128)S(1)}, u32[]{:S(2)}, u32[]{:S(2)}) collective-permute-start(f32[2,16,128]{2,1,0:T(8,128)S(1)} %get-tuple-element.47.one_ref), channel_id=1, source_target_pairs={{2,6},{6,2},{10,14},{14,10},{18,22},{22,18},{26,30},{30,26}} | collective-permute-start | bytes 49160 | tf_op jit(solution)/shard_map/ppermute | solution.py:516
  50.4 19.1 %collective-permute-start.6 = (bf16[64,640]{1,0:T(8,128)(2,1)S(1)}, bf16[64,640]{1,0:T(8,128)(2,1)S(1)}, u32[]{:S(2)}, u32[]{:S(2)}) collective-permute-start(bf16[64,640]{1,0:T(8,128)(2,1)S(1)} %get-tuple-element.41), channel_id=1, source_target_pairs={{0,8},{8,0},{16,24},{24,16},{1,9},{9,1},{17,25},{25,17},{2,10},{10... | collective-permute-start | bytes 245768 | tf_op jit(solution)/shard_map/ppermute | solution.py:512
  51.4 18.1 %collective-permute-start.7 = (bf16[64,640]{1,0:T(8,128)(2,1)S(1)}, bf16[64,640]{1,0:T(8,128)(2,1)S(1)}, u32[]{:S(2)}, u32[]{:S(2)}) collective-permute-start(bf16[64,640]{1,0:T(8,128)(2,1)S(1)} %get-tuple-element.42), channel_id=1, source_target_pairs={{0,16},{8,24},{16,0},{24,8},{1,17},{9,25},{17,1},{25,9},{2,18},{10... | collective-permute-start | bytes 245768 | tf_op jit(solution)/shard_map/ppermute | solution.py:512
  52.0 17.5 %collective-permute-start.8 = (bf16[64,640]{1,0:T(8,128)(2,1)S(1)}, bf16[64,640]{1,0:T(8,128)(2,1)S(1)}, u32[]{:S(2)}, u32[]{:S(2)}) collective-permute-start(bf16[64,640]{1,0:T(8,128)(2,1)S(1)} %get-tuple-element.43), channel_id=1, source_target_pairs={{0,24},{8,16},{16,8},{24,0},{1,25},{9,17},{17,9},{25,1},{2,26},{10... | collective-permute-start | bytes 245768 | tf_op jit(solution)/shard_map/ppermute | solution.py:512
  54.8 2.0 %collective-permute-start.15 = (bf16[2,16,128]{2,1,0:T(8,128)(2,1)S(1)}, bf16[2,16,128]{2,1,0:T(8,128)(2,1)S(1)}, u32[]{:S(2)}, u32[]{:S(2)}) collective-permute-start(bf16[2,16,128]{2,1,0:T(8,128)(2,1)S(1)} %get-tuple-element.49), channel_id=1, source_target_pairs={{2,1},{6,5},{10,9},{14,13},{18,17},{22,21},{26,25},{30,29}} | collective-permute-start | bytes 24584 | tf_op jit(solution)/shard_map/ppermute | solution.py:516
  55.5 8.6 %collective-permute-start.16 = (bf16[2,16,128]{2,1,0:T(8,128)(2,1)S(1)}, bf16[2,16,128]{2,1,0:T(8,128)(2,1)S(1)}, u32[]{:S(2)}, u32[]{:S(2)}) collective-permute-start(bf16[2,16,128]{2,1,0:T(8,128)(2,1)S(1)} %get-tuple-element.49), channel_id=1, source_target_pairs={{2,3},{6,7},{10,11},{14,15},{18,19},{22,23},{26,27},{30,31}} | collective-permute-start | bytes 24584 | tf_op jit(solution)/shard_map/ppermute | solution.py:516
  56.8 16.5 %collective-permute-start.18 = (f32[2,16,128]{2,1,0:T(8,128)S(1)}, f32[2,16,128]{2,1,0:T(8,128)S(1)}, u32[]{:S(2)}, u32[]{:S(2)}) collective-permute-start(f32[2,16,128]{2,1,0:T(8,128)S(1)} %get-tuple-element.56), channel_id=1, source_target_pairs={{2,0},{6,4},{10,8},{14,12},{18,16},{22,20},{26,24},{30,28}} | collective-permute-start | bytes 49160 | tf_op jit(solution)/shard_map/ppermute | solution.py:516
  64.5 6.0 %collective-permute-start.17 = (bf16[2,16,128]{2,1,0:T(8,128)(2,1)S(1)}, bf16[2,16,128]{2,1,0:T(8,128)(2,1)S(1)}, u32[]{:S(2)}, u32[]{:S(2)}) collective-permute-start(bf16[2,16,128]{2,1,0:T(8,128)(2,1)S(1)} %get-tuple-element.51.here_ref), channel_id=1, source_target_pairs={{1,0},{3,2},{5,4},{7,6},{9,8},{11,10},{13,12},{15,14},{17,16},{19,... | collective-permute-start | bytes 24584 | tf_op jit(solution)/shard_map/ppermute | solution.py:516

commit v4 on v3

--- a/solution.py
+++ b/solution.py
@@ -57,8 +57,9 @@
 
 
 def pack_kernel(groups, v_hbm, b_hbm, *refs):
-    outs, held, sems = refs[:groups], refs[groups], refs[groups + 1]
+    outs, azi_ref, held, sems = refs[:groups], refs[groups], refs[groups + 1], refs[groups + 2]
     rows, width = v_hbm.shape[0], outs[0].shape[1]
+    part = rows // 3
 
     def copy(field, k):
         span = pl.ds(pl.multiple_of((lax.axis_index("mode") ^ k) * width, 128), width)
@@ -73,6 +74,9 @@
         for field in range(2):
             copy(field, k).wait()
             outs[k][field * rows : (field + 1) * rows, :] = held[k, field].astype(BF16)
+    for k in order:
+        span = pl.ds(pl.multiple_of((lax.axis_index("mode") ^ k) * width, 128), width)
+        azi_ref[:, span] = held[k, 1, part : 2 * part]
 
 
 def pack(velocity, magnetic, groups):
@@ -80,9 +84,10 @@
     width = nodes // groups
     return pl.pallas_call(
         functools.partial(pack_kernel, groups),
-        out_shape=[jax.ShapeDtypeStruct((2 * rows, width), BF16)] * groups,
+        out_shape=[jax.ShapeDtypeStruct((2 * rows, width), BF16)] * groups
+        + [jax.ShapeDtypeStruct((rows // 3, nodes), F32)],
         in_specs=[pl.BlockSpec(memory_space=pltpu.HBM)] * 2,
-        out_specs=[pl.BlockSpec(memory_space=VMEM)] * groups,
+        out_specs=[pl.BlockSpec(memory_space=VMEM)] * (groups + 1),
         scratch_shapes=[VMEM((groups, 2, rows, width), F32), pltpu.SemaphoreType.DMA((groups, 2))],
         compiler_params=pltpu.CompilerParams(vmem_limit_bytes=SMALL),
         name="pack",
@@ -204,32 +209,29 @@
     )(inverse, coupling)
 
 
-def leaf_up_kernel(groups, rows_ref, mag_hbm, joint_ref, *refs):
+def leaf_up_kernel(groups, rows_ref, mag_ref, joint_ref, *refs):
     pieces = refs[:groups]
-    source_ref, update_ref, turned_v, mag_v, sem = refs[groups:]
-    copy = pltpu.make_async_copy(mag_hbm.at[1], mag_v, sem)
-    copy.start()
-    copy.wait()
+    source_ref, update_ref, turned_v = refs[groups:]
     modes, front, nodes = joint_ref.shape
     width = nodes // groups
     for k in range(groups):
-        span = pl.ds(pl.multiple_of((lax.axis_index("mode") ^ k) * width, 128), width)
-        for a in range(2):
-            term = pieces[k][a * modes : (a + 1) * modes, :].astype(F32)
-            source_ref[a, :, span] = mag_v[a, :, span] + DT_STEP * term
-    turned_v[...] = source_ref[...].reshape(2 * modes, nodes).T.astype(BF16)
+        at = pl.multiple_of((lax.axis_index("mode") ^ k) * width, 128)
+        span = pl.ds(at, width)
+        source = (mag_ref[:, span] + DT_STEP * pieces[k][...].astype(F32)).astype(BF16)
+        source_ref[:, :, span] = source.astype(F32).reshape(2, modes, width)
+        turned_v[pl.ds(at, width), :] = source.T
     turned = turned_v[...]
     lane = lax.broadcasted_iota(jnp.int32, (front, 2 * modes), 1) % modes
 
     def one_mode(m, total):
         return total + jnp.where(lane == m, dot(joint_ref[m], turned), 0.0)
 
-    total = lax.fori_loop(0, modes, one_mode, jnp.zeros((front, 2 * modes), F32), unroll=2)
+    total = lax.fori_loop(0, modes, one_mode, jnp.zeros((front, 2 * modes), F32), unroll=4)
     select = one_hot(rows_ref, 0).astype(F32)
     update_ref[...] = dot(total.T, select, precision=lax.Precision.HIGHEST).reshape(update_ref.shape)
 
 
-def leaf_up(rows, magnetic, pieces, joint):
+def leaf_up(rows, mag, pieces, joint):
     modes, front, nodes = joint.shape
     groups = len(pieces)
     whole = pl.BlockSpec(memory_space=VMEM)
@@ -239,23 +241,15 @@
             jax.ShapeDtypeStruct((2, modes, nodes), F32),
             jax.ShapeDtypeStruct((2, modes, front), F32),
         ],
-        in_specs=[
-            whole,
-            pl.BlockSpec(memory_space=pltpu.HBM),
-        ]
-        + [whole] * (1 + groups),
+        in_specs=[whole] * (3 + groups),
         out_specs=[whole] * 2,
-        scratch_shapes=[
-            VMEM((nodes, 2 * modes), BF16),
-            VMEM((2, modes, nodes), F32),
-            pltpu.SemaphoreType.DMA(()),
-        ],
+        scratch_shapes=[VMEM((nodes, 2 * modes), BF16)],
         compiler_params=pltpu.CompilerParams(vmem_limit_bytes=LARGE),
         cost_estimate=pl.CostEstimate(
             flops=128 * modes * nodes * front, bytes_accessed=2 * joint.size, transcendentals=0
         ),
         name="leaf_up",
-    )(rows, magnetic, joint, *pieces)
+    )(rows, mag, joint, *pieces)
 
 
 def leaf_local_kernel(source_ref, square_ref, out_ref):
@@ -354,51 +348,58 @@
     )(*azi, *rest)
 
 
-def fronts_kernel(rows_ref, inv_ref, cpl_ref, source_ref, out_ref):
-    modes, size, _ = inv_ref.shape
+def fronts_kernel(rows_ref, inv_hbm, cpl_hbm, source_hbm, send_ref, own_ref, source_ref, cpl_v, sems):
+    modes, size, _ = cpl_v.shape
     half = modes * size
-    out_ref[:half, :] = inv_ref[...].reshape(half, size)
+    copies = [
+        pltpu.make_async_copy(inv_hbm, own_ref.at[0], sems.at[0]),
+        pltpu.make_async_copy(cpl_hbm, cpl_v, sems.at[1]),
+        pltpu.make_async_copy(source_hbm, source_ref, sems.at[2]),
+    ]
+    for copy in copies:
+        copy.start()
     select = one_hot(rows_ref, 1).astype(F32).T.astype(BF16)
+    for copy in copies:
+        copy.wait()
     for m in range(modes):
-        at = half + m * size
-        out_ref[at : at + size, :] = dot(select, cpl_ref[m]).astype(BF16)
+        own_ref[1, m] = dot(select, cpl_v[m]).astype(BF16)
+        own_ref[2, m] = own_ref[0, m].T
+        own_ref[3, m] = own_ref[1, m].T
+    send_ref[:half, :] = own_ref[0].reshape(half, size)
     rest = flat(source_ref)
     for part in range(3):
-        at = 2 * half + part * rest.shape[0]
+        at = half + part * rest.shape[0]
         term = rest.astype(BF16)
-        out_ref[at : at + rest.shape[0], :] = term
+        send_ref[at : at + rest.shape[0], :] = term
         rest = rest - term.astype(F32)
 
 
 def fronts(rows, inverse, coupling, source):
     modes, size, _ = inverse.shape
-    total = 2 * modes * size + 3 * 2 * modes
     return pl.pallas_call(
         fronts_kernel,
-        out_shape=jax.ShapeDtypeStruct((total, size), BF16),
-        in_specs=[pl.BlockSpec(memory_space=VMEM)] * 4,
-        out_specs=pl.BlockSpec(memory_space=VMEM),
+        out_shape=[
+            jax.ShapeDtypeStruct((modes * size + 3 * 2 * modes, size), BF16),
+            jax.ShapeDtypeStruct((4, modes, size, size), BF16),
+            jax.ShapeDtypeStruct(source.shape, F32),
+        ],
+        in_specs=[pl.BlockSpec(memory_space=VMEM)] + [pl.BlockSpec(memory_space=pltpu.HBM)] * 3,
+        out_specs=[pl.BlockSpec(memory_space=VMEM)] * 3,
+        scratch_shapes=[VMEM(coupling.shape, BF16), pltpu.SemaphoreType.DMA((3,))],
         compiler_params=pltpu.CompilerParams(vmem_limit_bytes=SMALL),
         name="fronts",
-    )(rows, inverse, coupling, source)
-
-
-class Front:
-    def __init__(self, ref, like):
-        count, modes, size = like.shape
-        self.ref, self.modes, self.size, self.rows = ref, modes, size, count * modes
-
-    def __getitem__(self, which):
-        half = self.modes * self.size
-        return self.ref[which * half : (which + 1) * half, :].reshape(self.modes, self.size, self.size)
-
-    def source(self):
-        at = 2 * self.modes * self.size
-        parts = [self.ref[at + p * self.rows : at + (p + 1) * self.rows, :].astype(F32) for p in range(3)]
-        return parts[0] + parts[1] + parts[2]
-
-
-def apply_rows(x, matrix):
+    )(rows, stay(inverse), stay(coupling), stay(source))
+
+
+def apply(x, matrix):
+    modes, size, _ = matrix.shape
+    row = lax.broadcasted_iota(jnp.int32, x.shape, 0) % modes
+    x = x.astype(F32)
+    wide = jnp.concatenate([jnp.where(row == m, x, 0.0).astype(BF16) for m in range(modes)], axis=1)
+    return dot(wide, matrix.reshape(modes * size, size))
+
+
+def apply_turned(x, matrix):
     modes, size, _ = matrix.shape
     wide = dot(x, matrix.reshape(modes * size, size), NT)
     row = lax.broadcasted_iota(jnp.int32, x.shape, 0) % modes
@@ -408,24 +409,8 @@
     return total
 
 
-def apply_columns(x, matrix):
-    modes, size, _ = matrix.shape
-    row = lax.broadcasted_iota(jnp.int32, x.shape, 0) % modes
-    x = x.astype(F32)
-    wide = jnp.concatenate([jnp.where(row == m, x, 0.0).astype(BF16) for m in range(modes)], axis=1)
-    return dot(wide, matrix.reshape(modes * size, size))
-
-
 def flat(ref):
     return ref[...].reshape(ref.shape[0] * ref.shape[1], ref.shape[2])
-
-
-def rise_kernel(one_ref, two_ref, source_ref, front_ref, reduced_ref, outgoing_ref):
-    front_ref = Front(front_ref, one_ref)
-    g = (flat(source_ref) - (flat(one_ref) + flat(two_ref))).astype(BF16)
-    reduced = apply_rows(g, front_ref[0]).astype(BF16)
-    reduced_ref[...] = reduced.astype(F32).reshape(reduced_ref.shape)
-    outgoing_ref[...] = apply_rows(reduced, front_ref[1]).reshape(outgoing_ref.shape)
 
 
 def small_call(kernel, outs, args):
@@ -438,36 +423,34 @@
     )(*args)
 
 
-def crown_kernel(high, one_ref, two_ref, reduced_ref, front_ref, fa_ref, fb_ref, x_ref, x16_ref, far_ref):
-    front_ref, front_a, front_b = (Front(ref, one_ref) for ref in (front_ref, fa_ref, fb_ref))
-
-    def solve(f_mid, f_top, send_mid):
-        g = (f_mid.source() - (flat(one_ref) + flat(two_ref))).astype(BF16)
-        mid = apply_rows(g, f_mid[0]).astype(BF16)
-        g = (f_top.source() - apply_rows(mid, f_mid[1])).astype(BF16)
-        top = apply_columns(apply_rows(g, f_top[0]).astype(BF16), f_top[0])
-        residue = mid.astype(F32) - apply_columns(top.astype(BF16), f_mid[1])
-        x_mid = apply_columns(residue.astype(BF16), f_mid[0])
-        far_ref[...] = (x_mid if send_mid else top).reshape(far_ref.shape)
-        residue = flat(reduced_ref) - apply_columns(x_mid.astype(BF16), front_ref[1])
-        x = apply_columns(residue.astype(BF16), front_ref[0])
-        x_ref[...] = x.reshape(x_ref.shape)
-        x16_ref[...] = x.astype(BF16).reshape(x_ref.shape)
-
-    @pl.when(lax.axis_index("mesh") != high)
-    def _():
-        solve(front_a, front_b, False)
-
-    @pl.when(lax.axis_index("mesh") == high)
-    def _():
-        solve(front_b, front_a, True)
+def rise_kernel(one_ref, two_ref, source_ref, front_ref, reduced_ref, outgoing_ref):
+    g = (flat(source_ref) - (flat(one_ref) + flat(two_ref))).astype(BF16)
+    reduced = apply(g, front_ref[2]).astype(BF16)
+    reduced_ref[...] = reduced.astype(F32).reshape(reduced_ref.shape)
+    outgoing_ref[...] = apply(reduced, front_ref[3]).reshape(outgoing_ref.shape)
+
+
+def crown_kernel(one_ref, two_ref, source_ref, front_ref, lift_ref, x_ref, x16_ref, top_ref):
+    _, modes, size, _ = front_ref.shape
+    rows = 2 * modes
+    half = modes * size
+    g = (flat(source_ref) - (flat(one_ref) + flat(two_ref))).astype(BF16)
+    mid = apply(g, front_ref[2]).astype(BF16)
+    terms = [lift_ref[half + p * rows : half + (p + 1) * rows, :].astype(F32) for p in range(3)]
+    g = (terms[0] + terms[1] + terms[2] - apply(mid, front_ref[3])).astype(BF16)
+    inverse = lift_ref[:half, :].reshape(modes, size, size)
+    top = apply(apply_turned(g, inverse).astype(BF16), inverse)
+    top_ref[...] = top.reshape(top_ref.shape)
+    residue = mid.astype(F32) - apply(top.astype(BF16), front_ref[1])
+    x = apply(residue.astype(BF16), front_ref[0])
+    x_ref[...] = x.reshape(x_ref.shape)
+    x16_ref[...] = x.astype(BF16).reshape(x_ref.shape)
 
 
 def sink_kernel(one_ref, two_ref, reduced_ref, front_ref, x_ref, x16_ref):
-    front_ref = Front(front_ref, one_ref)
     above = (flat(one_ref).astype(F32) + flat(two_ref).astype(F32)).astype(BF16)
-    residue = flat(reduced_ref) - apply_columns(above, front_ref[1])
-    x = apply_columns(residue.astype(BF16), front_ref[0])
+    residue = flat(reduced_ref) - apply(above, front_ref[1])
+    x = apply(residue.astype(BF16), front_ref[0])
     x_ref[...] = x.reshape(x_ref.shape)
     x16_ref[...] = x.astype(BF16).reshape(x_ref.shape)
 
@@ -504,7 +487,7 @@
     levels = partitions.bit_length() - 1
     modes, nodes = velocity.shape[2], velocity.shape[3]
     exchange = [[(g, g ^ k) for g in range(groups)] for k in range(groups)]
-    low, mid, high = partitions // 4, partitions // 2, 3 * partitions // 4
+    mid = partitions // 2
 
     def swap(pieces):
         out = [pieces[0]]
@@ -515,17 +498,20 @@
     def hop(value, pairs):
         return lax.ppermute(value, "mesh", pairs)
 
-    packed = pack(stay(velocity.reshape(6 * modes, nodes)), stay(magnetic.reshape(6 * modes, nodes)), groups)
+    *packed, mag = pack(
+        stay(velocity.reshape(6 * modes, nodes)), stay(magnetic.reshape(6 * modes, nodes)), groups
+    )
     spread_in = swap(packed)
     fwd, bwd = tables(groups, modes)
-    front = fronts(front_rows, separator_inverse, separator_coupling, separator_source)
-    front_a = hop(front, [(mid, low), (0, high)])
-    front_b = hop(front, [(mid, high), (0, low)])
+    send, front, sep_source = fronts(
+        front_rows, separator_inverse, separator_coupling, separator_source
+    )
     square, joint = compose(stay(leaf_inverse), stay(leaf_coupling))
     azi, rest = transform(fwd, bwd, spread_in)
     azi = swap(azi)
+    lift = hop(send, [(0, mid)])
     rest = swap(rest)
-    source, update = leaf_up(front_rows, stay(magnetic), azi, joint)
+    source, update = leaf_up(front_rows, mag, azi, joint)
     local = leaf_local(source, square)
     nonlinear = spread(azi, rest).reshape(3, 2, modes, nodes)
 
@@ -535,25 +521,21 @@
     reduced = [None] * (levels + 1)
     one, two = update, hop(update, [(q - 1, q) for q in of_level[1]])
     for height in range(1, levels):
-        if height > 1:
-            gap = 2 ** (height - 2)
-            one = hop(outgoing, [(q - gap, q) for q in of_level[height]])
-            two = hop(outgoing, [(q + gap, q) for q in of_level[height]])
-        reduced[height], outgoing = small_call(rise_kernel, [wide, wide], [one, two, separator_source, front])
-    other = hop(outgoing, [(low, high), (high, low)])
-    x, x16, far = small_call(
-        functools.partial(crown_kernel, high),
-        [wide, half, wide],
-        [outgoing, other, reduced[levels - 1], front, front_a, front_b],
-    )
-    answers = [(levels - 1, x)]
-    for height in range(levels - 2, 0, -1):
+        reduced[height], outgoing = small_call(
+            rise_kernel, [wide, wide], [one, two, sep_source, front]
+        )
+        gap = 2 ** (height - 1)
+        one = hop(outgoing, [(q - gap, q) for q in of_level[height + 1]])
+        two = hop(outgoing, [(q + gap, q) for q in of_level[height + 1]])
+    x, x16, top = small_call(crown_kernel, [wide, half, wide], [one, two, sep_source, front, lift])
+    answers = [(levels, x)]
+    for height in range(levels - 1, 0, -1):
         gap = 2 ** (height - 1)
         one = hop(x16, [(q, q - gap) for q in of_level[height + 1]])
         two = hop(x16, [(q, q + gap) for q in of_level[height + 1]])
         x, x16 = small_call(sink_kernel, [wide, half], [one, two, reduced[height], front])
         answers.append((height, x))
-    far = hop(far, [(low, 0), (high, mid)])
+    far = hop(top, [(mid, 0)])
     beside = hop(x16, [(q, q - 1) for q in of_level[1]])
     azimuthal = leaf_down(front_rows, x16, beside, local, joint)
     answers.reverse()

time: 75.1 us -> 70.1 us (0.933)
  the two profiles are of different devices: /device:TPU:9 before, /device:TPU:1 now
where the time goes in v4:
time: 70.1 us; the launch traced here: 69.7 us
  Pallas kernels  28.3 us (40%)
  starting transfers between devices  21.2 us (30%)
  waiting for transfers between devices  18.6 us (27%)
  between operations  0.89 us (1%)
    ppermute x12, starting transfers between devices, hop(): return lax.ppermute(value, 'mesh', pairs)  12.4 us
    ppermute x12, waiting for transfers between devices, hop(): return lax.ppermute(value, 'mesh', pairs)  12 us
    pallas_call x1, Pallas kernels, compose(): pl.pallas_call(compose_kernel, out_shape=[jax.ShapeDtypeStruct(inverse.sh...  9.78 us
    ppermute x9, starting transfers between devices, swap(): out.append(lax.ppermute(pieces[k], 'mode', exchange[k]))  8.78 us
    ppermute x9, waiting for transfers between devices, swap(): out.append(lax.ppermute(pieces[k], 'mode', exchange[k]))  6.62 us
    pallas_call x1, Pallas kernels, leaf_up(): pl.pallas_call(functools.partial(leaf_up_kernel, groups), out_shape=[jax....  3.81 us
    pallas_call x6, Pallas kernels, small_call(): pl.pallas_call(kernel, out_shape=outs, in_specs=[pl.BlockSpec(memory_spac...  3.32 us
    pallas_call x1, Pallas kernels, leaf_down(): pl.pallas_call(leaf_down_kernel, out_shape=jax.ShapeDtypeStruct(local.sha...  2.77 us
  transfers between devices with their start and end apart: 21, of which 6 were waited for; matrix products, arithmetic and copies ran while one was open for 0% of the time, Pallas kernels for 34%

profile of v4, /device:TPU:1, one launch (start us, length us, event | category | flops | bytes accessed | tf_op | source)
XLA Modules:
  0.0 69.7 jit_solution(5342958507379326808)
XLA Ops:
  0.6 1.7 %pack.1 = (bf16[192,640]{1,0:T(8,128)(2,1)S(1)}, bf16[192,640]{1,0:T(8,128)(2,1)S(1)}, bf16[192,640]{1,0:T(8,128)(2,1)S(1)}, bf16[192,640]{1,0:T(8,128)(2,1)S(1)}, f32[32,2560]{1,0:T(8,128)S(1)}) custom-call(f32[96,2560]{1,0:T(8,128)} %bitcast.3, f32[96,2560]{1,0:T(8,128)} %bitcast.4), custom_call_target="tpu_custom_call" | custom-call | tf_op jit(solution)/shard_map/pack/pallas_call | solution.py:85
  2.4 2.1 %collective-permute-start = (bf16[192,640]{1,0:T(8,128)(2,1)S(1)}, bf16[192,640]{1,0:T(8,128)(2,1)S(1)}, u32[]{:S(2)}, u32[]{:S(2)}) collective-permute-start(bf16[192,640]{1,0:T(8,128)(2,1)S(1)} %get-tuple-element.39), channel_id=1, source_target_pairs={{0,8},{8,0},{16,24},{24,16},{1,9},{9,1},{17,25},{25,17},{2,10},{10... | collective-permute-start | bytes 737288 | tf_op jit(solution)/shard_map/ppermute | solution.py:495
  4.5 1.2 %collective-permute-start.1 = (bf16[192,640]{1,0:T(8,128)(2,1)S(1)}, bf16[192,640]{1,0:T(8,128)(2,1)S(1)}, u32[]{:S(2)}, u32[]{:S(2)}) collective-permute-start(bf16[192,640]{1,0:T(8,128)(2,1)S(1)} %get-tuple-element.40), channel_id=1, source_target_pairs={{0,16},{8,24},{16,0},{24,8},{1,17},{9,25},{17,1},{25,9},{2,18},{10... | collective-permute-start | bytes 737288 | tf_op jit(solution)/shard_map/ppermute | solution.py:495
  5.7 0.0 collective-permute-start.2
  5.7 0.0 copy-start
  5.7 0.7 copy-done
  6.4 1.8 %fronts.1 = (bf16[2144,128]{1,0:T(8,128)(2,1)S(1)}, bf16[4,16,128,128]{3,2,1,0:T(8,128)(2,1)S(1)}, f32[2,16,128]{2,1,0:T(8,128)S(1)}) custom-call(s32[1,2,128]{2,1,0:T(2,128)S(1)} %copy-done, bf16[16,128,128]{2,1,0:T(8,128)(2,1)} %inv_hbm.3, bf16[16,128,128]{2,1,0:T(8,128)(2,1)} %cpl_hbm.3, f32[2,16,128]{2,1,0:T(8,128)} %source_hbm.1), custom_call_target="tpu_custom_call" | custom-call | tf_op jit(solution)/shard_map/fronts/pallas_call | solution.py:379
  8.2 0.7 collective-permute-start.14
  8.9 0.9 %tables.1 = (bf16[192,128]{1,0:T(8,128)(2,1)S(1)}, bf16[128,192]{1,0:T(8,128)(2,1)S(1)}) custom-call(), custom_call_target="tpu_custom_call" | custom-call | tf_op jit(solution)/shard_map/tables/pallas_call | solution.py:50
  9.8 0.4 collective-permute-done.refs_1_
  10.1 0.9 %collective-permute-done.1.refs_2_ = bf16[192,640]{1,0:T(8,128)(2,1)S(1)} collective-permute-done((bf16[192,640]{1,0:T(8,128)(2,1)S(1)}, bf16[192,640]{1,0:T(8,128)(2,1)S(1)}, u32[]{:S(2)}, u32[]{:S(2)}) %collective-permute-start.1) | collective-permute-done | bytes 245792 | tf_op jit(solution)/shard_map/ppermute | solution.py:495
  11.0 5.3 %collective-permute-done.2.refs_3_ = bf16[192,640]{1,0:T(8,128)(2,1)S(1)} collective-permute-done((bf16[192,640]{1,0:T(8,128)(2,1)S(1)}, bf16[192,640]{1,0:T(8,128)(2,1)S(1)}, u32[]{:S(2)}, u32[]{:S(2)}) %collective-permute-start.2) | collective-permute-done | bytes 245792 | tf_op jit(solution)/shard_map/ppermute | solution.py:495
  16.4 0.8 %transform.1 = (bf16[32,640]{1,0:T(8,128)(2,1)S(1)}, bf16[32,640]{1,0:T(8,128)(2,1)S(1)}, bf16[32,640]{1,0:T(8,128)(2,1)S(1)}, bf16[32,640]{1,0:T(8,128)(2,1)S(1...) custom-call(bf16[192,128]{1,0:T(8,128)(2,1)S(1)} %get-tuple-element., ...), custom_call_target="tpu_custom_call" | custom-call | tf_op jit(solution)/shard_map/transform/pallas_call | solution.py:123
  17.2 1.2 %collective-permute-start.3 = (bf16[32,640]{1,0:T(8,128)(2,1)S(1)}, bf16[32,640]{1,0:T(8,128)(2,1)S(1)}, u32[]{:S(2)}, u32[]{:S(2)}) collective-permute-start(bf16[32,640]{1,0:T(8,128)(2,1)S(1)} %get-tuple-element.43), channel_id=1, source_target_pairs={{0,8},{8,0},{16,24},{24,16},{1,9},{9,1},{17,25},{25,17},{2,10},{10... | collective-permute-start | bytes 122888 | tf_op jit(solution)/shard_map/ppermute | solution.py:495
  18.4 0.3 collective-permute-start.4
  18.7 0.0 copy-start.1
  18.7 1.2 %collective-permute-start.5 = (bf16[32,640]{1,0:T(8,128)(2,1)S(1)}, bf16[32,640]{1,0:T(8,128)(2,1)S(1)}, u32[]{:S(2)}, u32[]{:S(2)}) collective-permute-start(bf16[32,640]{1,0:T(8,128)(2,1)S(1)} %get-tuple-element.45), channel_id=1, source_target_pairs={{0,24},{8,16},{16,8},{24,0},{1,25},{9,17},{17,9},{25,1},{2,26},{10... | collective-permute-start | bytes 122888 | tf_op jit(solution)/shard_map/ppermute | solution.py:495
  19.9 9.8 %compose.1 = (bf16[16,20,128,128]{3,2,1,0:T(8,128)(2,1)S(1)}, bf16[16,128,2560]{2,1,0:T(8,128)(2,1)S(1)}) custom-call(bf16[16,20,128,128]{3,2,1,0:T(8,128)(2,1)} %inv_hbm.2, bf16[16,128,2560]{2,1,0:T(8,128)(2,1)} %cpl_hbm.2), custom_call_target="tpu_custom_call" | custom-call | flops 5368709120 | bytes 41943040 | tf_op jit(solution)/shard_map/compose/pallas_call | solution.py:189
  29.7 0.0 collective-permute-done.3.refs_1_
  29.7 0.0 collective-permute-done.4.refs_2_
  29.7 0.0 collective-permute-done.5.refs_3_
  29.7 0.0 copy-done.1
  29.8 3.8 %leaf_up.1 = (f32[2,16,2560]{2,1,0:T(8,128)S(1)}, f32[2,16,128]{2,1,0:T(8,128)S(1)}) custom-call(s32[1,2,128]{2,1,0:T(2,128)S(1)} %copy-done.1, f32[32,2560]{1,0:T(8,128)S(1)} %get-tuple-element.50.mag_ref, bf16[16,128,2560]{2,1,0:T(8,128)(2,1)S(1)} %get-tuple-element.51.joint_ref, bf16[32,640]{1,0:T(8,128)(2,1)S(1)} %get-tuple-element.42.refs_0_, ...), custom_call_target="tpu_custom_call" | custom-call | flops 671088640 | bytes 10485760 | tf_op jit(solution)/shard_map/leaf_up/pallas_call | solution.py:238
  33.6 1.3 %collective-permute-start.9 = (f32[2,16,128]{2,1,0:T(8,128)S(1)}, f32[2,16,128]{2,1,0:T(8,128)S(1)}, u32[]{:S(2)}, u32[]{:S(2)}) collective-permute-start(f32[2,16,128]{2,1,0:T(8,128)S(1)} %get-tuple-element.52.one_ref), channel_id=1, source_target_pairs={{0,1},{2,3},{4,5},{6,7},{8,9},{10,11},{12,13},{14,15},{16,17},{18,... | collective-permute-start | bytes 49160 | tf_op jit(solution)/shard_map/ppermute | solution.py:499
  34.9 3.2 %collective-permute-done.9.two_ref = f32[2,16,128]{2,1,0:T(8,128)S(1)} collective-permute-done((f32[2,16,128]{2,1,0:T(8,128)S(1)}, f32[2,16,128]{2,1,0:T(8,128)S(1)}, u32[]{:S(2)}, u32[]{:S(2)}) %collective-permute-start.9) | collective-permute-done | bytes 16416 | tf_op jit(solution)/shard_map/ppermute | solution.py:499
  38.1 0.4 shard_map.103
  38.5 3.2 %collective-permute-start.10 = (f32[2,16,128]{2,1,0:T(8,128)S(1)}, f32[2,16,128]{2,1,0:T(8,128)S(1)}, u32[]{:S(2)}, u32[]{:S(2)}) collective-permute-start(f32[2,16,128]{2,1,0:T(8,128)S(1)} %get-tuple-element.55), channel_id=1, source_target_pairs={{1,2},{5,6},{9,10},{13,14},{17,18},{21,22},{25,26},{29,30}} | collective-permute-start | bytes 49160 | tf_op jit(solution)/shard_map/ppermute | solution.py:499
  41.8 0.7 collective-permute-start.11
  42.4 0.2 collective-permute-done.10.one_ref
  42.6 0.0 collective-permute-done.11.two_ref
  42.6 0.4 shard_map.104
  43.0 0.7 collective-permute-start.12
  43.7 0.7 collective-permute-start.13
  44.3 1.0 %collective-permute-start.6 = (bf16[64,640]{1,0:T(8,128)(2,1)S(1)}, bf16[64,640]{1,0:T(8,128)(2,1)S(1)}, u32[]{:S(2)}, u32[]{:S(2)}) collective-permute-start(bf16[64,640]{1,0:T(8,128)(2,1)S(1)} %get-tuple-element.47), channel_id=1, source_target_pairs={{0,8},{8,0},{16,24},{24,16},{1,9},{9,1},{17,25},{25,17},{2,10},{10... | collective-permute-start | bytes 245768 | tf_op jit(solution)/shard_map/ppermute | solution.py:495
  45.4 0.5 collective-permute-start.7
  45.9 0.0 collective-permute-done.12.one_ref
  45.9 1.1 %collective-permute-start.8 = (bf16[64,640]{1,0:T(8,128)(2,1)S(1)}, bf16[64,640]{1,0:T(8,128)(2,1)S(1)}, u32[]{:S(2)}, u32[]{:S(2)}) collective-permute-start(bf16[64,640]{1,0:T(8,128)(2,1)S(1)} %get-tuple-element.49), channel_id=1, source_target_pairs={{0,24},{8,16},{16,8},{24,0},{1,25},{9,17},{17,9},{25,1},{2,26},{10... | collective-permute-start | bytes 245768 | tf_op jit(solution)/shard_map/ppermute | solution.py:495
  47.1 0.0 collective-permute-done.13.two_ref
  47.1 0.0 collective-permute-done.14.lift_ref
  47.1 1.2 %shard_map.105 = (f32[2,16,128]{2,1,0:T(8,128)S(1)}, bf16[2,16,128]{2,1,0:T(8,128)(2,1)S(1)}, f32[2,16,128]{2,1,0:T(8,128)S(1)}) custom-call(f32[2,16,128]{2,1,0:T(8,128)S(1)} %collective-permute-done.12.one_ref, f32[2,16,128]{2,1,0:T(8,128)S(1)} %collective-permute-done.13.two_ref, f32[2,16,128]{2,1,0:T(8,128)S(1)} %get-tuple-element.53.source_ref, ...), custom_call_target="tpu_custom_call" | custom-call | tf_op jit(solution)/shard_map/pallas_call | solution.py:417
  48.2 0.7 collective-permute-start.15
  48.9 0.7 collective-permute-start.16
  49.6 0.0 collective-permute-done.15.one_ref
  49.6 0.0 collective-permute-done.16.two_ref
  49.6 0.4 shard_map.106
  50.0 1.3 %collective-permute-start.17 = (bf16[2,16,128]{2,1,0:T(8,128)(2,1)S(1)}, bf16[2,16,128]{2,1,0:T(8,128)(2,1)S(1)}, u32[]{:S(2)}, u32[]{:S(2)}) collective-permute-start(bf16[2,16,128]{2,1,0:T(8,128)(2,1)S(1)} %get-tuple-element.60), channel_id=1, source_target_pairs={{2,1},{6,5},{10,9},{14,13},{18,17},{22,21},{26,25},{30,29}} | collective-permute-start | bytes 24584 | tf_op jit(solution)/shard_map/ppermute | solution.py:499
  51.3 0.7 collective-permute-start.18
  52.0 8.6 %collective-permute-done.17.one_ref = bf16[2,16,128]{2,1,0:T(8,128)(2,1)S(1)} collective-permute-done((bf16[2,16,128]{2,1,0:T(8,128)(2,1)S(1)}, bf16[2,16,128]{2,1,0:T(8,128)(2,1)S(1)}, u32[]{:S(2)}, u32[]{:S(2)}) %collective-permute-start.17) | collective-permute-done | bytes 8224 | tf_op jit(solution)/shard_map/ppermute | solution.py:499
  60.6 0.7 collective-permute-start.20
  61.2 0.0 collective-permute-done.18.two_ref
  61.2 0.4 shard_map.107
  61.6 1.3 %collective-permute-start.19 = (bf16[2,16,128]{2,1,0:T(8,128)(2,1)S(1)}, bf16[2,16,128]{2,1,0:T(8,128)(2,1)S(1)}, u32[]{:S(2)}, u32[]{:S(2)}) collective-permute-start(bf16[2,16,128]{2,1,0:T(8,128)(2,1)S(1)} %get-tuple-element.62.here_ref), channel_id=1, source_target_pairs={{1,0},{3,2},{5,4},{7,6},{9,8},{11,10},{13,12},{15,14},{17,16},{19,... | collective-permute-start | bytes 24584 | tf_op jit(solution)/shard_map/ppermute | solution.py:499
  62.9 2.4 %leaf_local.1.local_ref = f32[2,16,2560]{2,1,0:T(8,128)S(1)} custom-call(f32[2,16,2560]{2,1,0:T(8,128)S(1)} %get-tuple-element.63.source_ref, bf16[16,20,128,128]{3,2,1,0:T(8,128)(2,1)S(1)} %get-tuple-element.64.square_ref), custom_call_target="tpu_custom_call" | custom-call | flops 671088640 | bytes 10485760 | tf_op jit(solution)/shard_map/leaf_local/pallas_call | solution.py:279
  65.3 0.0 collective-permute-done.6.refs_5_
  65.3 0.0 collective-permute-done.7.refs_6_
  65.3 0.0 collective-permute-done.8.refs_7_
  65.3 1.0 %spread.1 = f32[96,2560]{1,0:T(8,128)} custom-call(bf16[32,640]{1,0:T(8,128)(2,1)S(1)} %get-tuple-element.42.refs_0_, bf16[32,640]{1,0:T(8,128)(2,1)S(1)} %collective-permute-done.3.refs_1_, bf16[32,640]{1,0:T(8,128)(2,1)S(1)} %collective-permute-done.4.refs_2_, bf16[32,640]{1,0:T(8,128)(2,1)S(1)} %collective-permute-done.5.refs_3_, ...), custom_call_target="tpu_custom_call" | custom-call | tf_op jit(solution)/shard_map/spread/pallas_call | solution.py:341
  66.3 0.0 collective-permute-done.20.refs_3_
  66.3 0.6 shard_map.108
  66.9 0.0 collective-permute-done.19.beside_ref
  66.9 2.8 %leaf_down.1 = f32[2,16,2560]{2,1,0:T(8,128)} custom-call(s32[1,2,128]{2,1,0:T(2,128)S(1)} %copy-done.1, bf16[2,16,128]{2,1,0:T(8,128)(2,1)S(1)} %get-tuple-element.62.here_ref, bf16[2,16,128]{2,1,0:T(8,128)(2,1)S(1)} %collective-permute-done.19.beside_ref, f32[2,16,2560]{2,1,0:T(8,128)S(1)} %leaf_local.1.local_ref, ...), custom_call_target="tpu_custom_call" | custom-call | tf_op jit(solution)/shard_map/leaf_down/pallas_call | solution.py:317
Async XLA Ops:
  2.4 7.8 %collective-permute-start = (bf16[192,640]{1,0:T(8,128)(2,1)S(1)}, bf16[192,640]{1,0:T(8,128)(2,1)S(1)}, u32[]{:S(2)}, u32[]{:S(2)}) collective-permute-start(bf16[192,640]{1,0:T(8,128)(2,1)S(1)} %get-tuple-element.39), channel_id=1, source_target_pairs={{0,8},{8,0},{16,24},{24,16},{1,9},{9,1},{17,25},{25,17},{2,10},{10... | collective-permute-start | bytes 737288 | tf_op jit(solution)/shard_map/ppermute | solution.py:495
  4.5 6.6 %collective-permute-start.1 = (bf16[192,640]{1,0:T(8,128)(2,1)S(1)}, bf16[192,640]{1,0:T(8,128)(2,1)S(1)}, u32[]{:S(2)}, u32[]{:S(2)}) collective-permute-start(bf16[192,640]{1,0:T(8,128)(2,1)S(1)} %get-tuple-element.40), channel_id=1, source_target_pairs={{0,16},{8,24},{16,0},{24,8},{1,17},{9,25},{17,1},{25,9},{2,18},{10... | collective-permute-start | bytes 737288 | tf_op jit(solution)/shard_map/ppermute | solution.py:495
  5.7 10.7 %collective-permute-start.2 = (bf16[192,640]{1,0:T(8,128)(2,1)S(1)}, bf16[192,640]{1,0:T(8,128)(2,1)S(1)}, u32[]{:S(2)}, u32[]{:S(2)}) collective-permute-start(bf16[192,640]{1,0:T(8,128)(2,1)S(1)} %get-tuple-element.41), channel_id=1, source_target_pairs={{0,24},{8,16},{16,8},{24,0},{1,25},{9,17},{17,9},{25,1},{2,26},{10... | collective-permute-start | bytes 737288 | tf_op jit(solution)/shard_map/ppermute | solution.py:495
  5.7 0.7 copy-start
  8.2 38.9 %collective-permute-start.14 = (bf16[2144,128]{1,0:T(8,128)(2,1)S(1)}, bf16[2144,128]{1,0:T(8,128)(2,1)S(1)}, u32[]{:S(2)}, u32[]{:S(2)}) collective-permute-start(bf16[2144,128]{1,0:T(8,128)(2,1)S(1)} %get-tuple-element.57), channel_id=1, source_target_pairs={{0,4},{8,12},{16,20},{24,28}} | collective-permute-start | bytes 1646600 | tf_op jit(solution)/shard_map/ppermute | solution.py:499
  17.2 12.5 %collective-permute-start.3 = (bf16[32,640]{1,0:T(8,128)(2,1)S(1)}, bf16[32,640]{1,0:T(8,128)(2,1)S(1)}, u32[]{:S(2)}, u32[]{:S(2)}) collective-permute-start(bf16[32,640]{1,0:T(8,128)(2,1)S(1)} %get-tuple-element.43), channel_id=1, source_target_pairs={{0,8},{8,0},{16,24},{24,16},{1,9},{9,1},{17,25},{25,17},{2,10},{10... | collective-permute-start | bytes 122888 | tf_op jit(solution)/shard_map/ppermute | solution.py:495
  18.4 11.3 %collective-permute-start.4 = (bf16[32,640]{1,0:T(8,128)(2,1)S(1)}, bf16[32,640]{1,0:T(8,128)(2,1)S(1)}, u32[]{:S(2)}, u32[]{:S(2)}) collective-permute-start(bf16[32,640]{1,0:T(8,128)(2,1)S(1)} %get-tuple-element.44), channel_id=1, source_target_pairs={{0,16},{8,24},{16,0},{24,8},{1,17},{9,25},{17,1},{25,9},{2,18},{10... | collective-permute-start | bytes 122888 | tf_op jit(solution)/shard_map/ppermute | solution.py:495
  18.7 11.0 %copy-start.1 = (s32[1,2,128]{2,1,0:T(2,128)S(1)}, s32[1,2,128]{2,1,0:T(2,128)}, u32[]{:S(2)}) copy-start(s32[1,2,128]{2,1,0:T(2,128)} %rows_ref.5) | copy-start | bytes 3076
  18.7 11.0 %collective-permute-start.5 = (bf16[32,640]{1,0:T(8,128)(2,1)S(1)}, bf16[32,640]{1,0:T(8,128)(2,1)S(1)}, u32[]{:S(2)}, u32[]{:S(2)}) collective-permute-start(bf16[32,640]{1,0:T(8,128)(2,1)S(1)} %get-tuple-element.45), channel_id=1, source_target_pairs={{0,24},{8,16},{16,8},{24,0},{1,25},{9,17},{17,9},{25,1},{2,26},{10... | collective-permute-start | bytes 122888 | tf_op jit(solution)/shard_map/ppermute | solution.py:495
  33.6 4.5 %collective-permute-start.9 = (f32[2,16,128]{2,1,0:T(8,128)S(1)}, f32[2,16,128]{2,1,0:T(8,128)S(1)}, u32[]{:S(2)}, u32[]{:S(2)}) collective-permute-start(f32[2,16,128]{2,1,0:T(8,128)S(1)} %get-tuple-element.52.one_ref), channel_id=1, source_target_pairs={{0,1},{2,3},{4,5},{6,7},{8,9},{10,11},{12,13},{14,15},{16,17},{18,... | collective-permute-start | bytes 49160 | tf_op jit(solution)/shard_map/ppermute | solution.py:499
  38.5 4.1 %collective-permute-start.10 = (f32[2,16,128]{2,1,0:T(8,128)S(1)}, f32[2,16,128]{2,1,0:T(8,128)S(1)}, u32[]{:S(2)}, u32[]{:S(2)}) collective-permute-start(f32[2,16,128]{2,1,0:T(8,128)S(1)} %get-tuple-element.55), channel_id=1, source_target_pairs={{1,2},{5,6},{9,10},{13,14},{17,18},{21,22},{25,26},{29,30}} | collective-permute-start | bytes 49160 | tf_op jit(solution)/shard_map/ppermute | solution.py:499
  41.8 0.9 %collective-permute-start.11 = (f32[2,16,128]{2,1,0:T(8,128)S(1)}, f32[2,16,128]{2,1,0:T(8,128)S(1)}, u32[]{:S(2)}, u32[]{:S(2)}) collective-permute-start(f32[2,16,128]{2,1,0:T(8,128)S(1)} %get-tuple-element.55), channel_id=1, source_target_pairs={{3,2},{7,6},{11,10},{15,14},{19,18},{23,22},{27,26},{31,30}} | collective-permute-start | bytes 49160 | tf_op jit(solution)/shard_map/ppermute | solution.py:499
  43.0 2.9 %collective-permute-start.12 = (f32[2,16,128]{2,1,0:T(8,128)S(1)}, f32[2,16,128]{2,1,0:T(8,128)S(1)}, u32[]{:S(2)}, u32[]{:S(2)}) collective-permute-start(f32[2,16,128]{2,1,0:T(8,128)S(1)} %get-tuple-element.56), channel_id=1, source_target_pairs={{2,4},{10,12},{18,20},{26,28}} | collective-permute-start | bytes 49160 | tf_op jit(solution)/shard_map/ppermute | solution.py:499
  43.7 3.4 %collective-permute-start.13 = (f32[2,16,128]{2,1,0:T(8,128)S(1)}, f32[2,16,128]{2,1,0:T(8,128)S(1)}, u32[]{:S(2)}, u32[]{:S(2)}) collective-permute-start(f32[2,16,128]{2,1,0:T(8,128)S(1)} %get-tuple-element.56), channel_id=1, source_target_pairs={{6,4},{14,12},{22,20},{30,28}} | collective-permute-start | bytes 49160 | tf_op jit(solution)/shard_map/ppermute | solution.py:499
  44.3 20.9 %collective-permute-start.6 = (bf16[64,640]{1,0:T(8,128)(2,1)S(1)}, bf16[64,640]{1,0:T(8,128)(2,1)S(1)}, u32[]{:S(2)}, u32[]{:S(2)}) collective-permute-start(bf16[64,640]{1,0:T(8,128)(2,1)S(1)} %get-tuple-element.47), channel_id=1, source_target_pairs={{0,8},{8,0},{16,24},{24,16},{1,9},{9,1},{17,25},{25,17},{2,10},{10... | collective-permute-start | bytes 245768 | tf_op jit(solution)/shard_map/ppermute | solution.py:495
  45.4 19.9 %collective-permute-start.7 = (bf16[64,640]{1,0:T(8,128)(2,1)S(1)}, bf16[64,640]{1,0:T(8,128)(2,1)S(1)}, u32[]{:S(2)}, u32[]{:S(2)}) collective-permute-start(bf16[64,640]{1,0:T(8,128)(2,1)S(1)} %get-tuple-element.48), channel_id=1, source_target_pairs={{0,16},{8,24},{16,0},{24,8},{1,17},{9,25},{17,1},{25,9},{2,18},{10... | collective-permute-start | bytes 245768 | tf_op jit(solution)/shard_map/ppermute | solution.py:495
  45.9 19.4 %collective-permute-start.8 = (bf16[64,640]{1,0:T(8,128)(2,1)S(1)}, bf16[64,640]{1,0:T(8,128)(2,1)S(1)}, u32[]{:S(2)}, u32[]{:S(2)}) collective-permute-start(bf16[64,640]{1,0:T(8,128)(2,1)S(1)} %get-tuple-element.49), channel_id=1, source_target_pairs={{0,24},{8,16},{16,8},{24,0},{1,25},{9,17},{17,9},{25,1},{2,26},{10... | collective-permute-start | bytes 245768 | tf_op jit(solution)/shard_map/ppermute | solution.py:495
  48.2 1.3 %collective-permute-start.15 = (bf16[2,16,128]{2,1,0:T(8,128)(2,1)S(1)}, bf16[2,16,128]{2,1,0:T(8,128)(2,1)S(1)}, u32[]{:S(2)}, u32[]{:S(2)}) collective-permute-start(bf16[2,16,128]{2,1,0:T(8,128)(2,1)S(1)} %get-tuple-element.58), channel_id=1, source_target_pairs={{4,2},{12,10},{20,18},{28,26}} | collective-permute-start | bytes 24584 | tf_op jit(solution)/shard_map/ppermute | solution.py:499
  48.9 0.7 collective-permute-start.16
  50.0 10.6 %collective-permute-start.17 = (bf16[2,16,128]{2,1,0:T(8,128)(2,1)S(1)}, bf16[2,16,128]{2,1,0:T(8,128)(2,1)S(1)}, u32[]{:S(2)}, u32[]{:S(2)}) collective-permute-start(bf16[2,16,128]{2,1,0:T(8,128)(2,1)S(1)} %get-tuple-element.60), channel_id=1, source_target_pairs={{2,1},{6,5},{10,9},{14,13},{18,17},{22,21},{26,25},{30,29}} | collective-permute-start | bytes 24584 | tf_op jit(solution)/shard_map/ppermute | solution.py:499
  51.3 9.9 %collective-permute-start.18 = (bf16[2,16,128]{2,1,0:T(8,128)(2,1)S(1)}, bf16[2,16,128]{2,1,0:T(8,128)(2,1)S(1)}, u32[]{:S(2)}, u32[]{:S(2)}) collective-permute-start(bf16[2,16,128]{2,1,0:T(8,128)(2,1)S(1)} %get-tuple-element.60), channel_id=1, source_target_pairs={{2,3},{6,7},{10,11},{14,15},{18,19},{22,23},{26,27},{30,31}} | collective-permute-start | bytes 24584 | tf_op jit(solution)/shard_map/ppermute | solution.py:499
  60.6 5.8 %collective-permute-start.20 = (f32[2,16,128]{2,1,0:T(8,128)S(1)}, f32[2,16,128]{2,1,0:T(8,128)S(1)}, u32[]{:S(2)}, u32[]{:S(2)}) collective-permute-start(f32[2,16,128]{2,1,0:T(8,128)S(1)} %get-tuple-element.68), channel_id=1, source_target_pairs={{4,0},{12,8},{20,16},{28,24}} | collective-permute-start | bytes 49160 | tf_op jit(solution)/shard_map/ppermute | solution.py:499
  61.6 5.3 %collective-permute-start.19 = (bf16[2,16,128]{2,1,0:T(8,128)(2,1)S(1)}, bf16[2,16,128]{2,1,0:T(8,128)(2,1)S(1)}, u32[]{:S(2)}, u32[]{:S(2)}) collective-permute-start(bf16[2,16,128]{2,1,0:T(8,128)(2,1)S(1)} %get-tuple-element.62.here_ref), channel_id=1, source_target_pairs={{1,0},{3,2},{5,4},{7,6},{9,8},{11,10},{13,12},{15,14},{17,16},{19,... | collective-permute-start | bytes 24584 | tf_op jit(solution)/shard_map/ppermute | solution.py:499

commit v5 on v4

--- a/solution.py
+++ b/solution.py
@@ -29,20 +29,16 @@
 
 
 def tables_kernel(modes, fwd_ref, bwd_ref):
-    def phase(shape, angle_axis):
-        angle = lax.broadcasted_iota(jnp.int32, shape, angle_axis)
-        at = lax.broadcasted_iota(jnp.int32, shape, 1 - angle_axis)
-        step, kind, mode = at // (2 * modes), (at // modes) % 2, at % modes
-        order = jnp.bitwise_xor(step, lax.axis_index("mode")) * modes + mode
-        turn = (angle * order).astype(F32)
-        turn = turn - NPHI * jnp.floor((turn + 0.5) * (1.0 / NPHI))
-        return turn * (2.0 * jnp.pi / NPHI), kind, order
-
-    at, kind, _ = phase(fwd_ref.shape, 0)
-    fwd_ref[...] = jnp.where(kind == 0, jnp.cos(at), jnp.sin(at)).astype(BF16)
-    at, kind, order = phase(bwd_ref.shape, 1)
-    weight = jnp.where(order == 0, 1.0, 2.0) / NPHI
-    bwd_ref[...] = (jnp.where(kind == 0, jnp.cos(at), jnp.sin(at)) * weight).astype(BF16)
+    shape = fwd_ref.shape
+    angle = lax.broadcasted_iota(jnp.int32, shape, 0)
+    at = lax.broadcasted_iota(jnp.int32, shape, 1)
+    step, kind, mode = at // (2 * modes), (at // modes) % 2, at % modes
+    order = jnp.bitwise_xor(step, lax.axis_index("mode")) * modes + mode
+    turn = (angle * order).astype(F32) + jnp.where(kind == 0, NPHI / 4, 0.0)
+    turn = turn - NPHI * jnp.floor((turn + 0.5) * (1.0 / NPHI))
+    value = jnp.sin(turn * (2.0 * jnp.pi / NPHI))
+    fwd_ref[...] = value.astype(BF16)
+    bwd_ref[...] = (value * (jnp.where(order == 0, 1.0, 2.0) / NPHI)).T.astype(BF16)
 
 
 def tables(groups, modes):
@@ -137,7 +133,38 @@
     return lax.broadcasted_iota(jnp.int32, (n, n), 0) == rows_ref[0, which : which + 1, :]
 
 
-def compose_kernel(inv_hbm, cpl_hbm, square_ref, joint_ref, inv_v, cpl_v, sems):
+def side_copies(inv_hbm, cpl_hbm, source_hbm, rows_hbm, own_ref, cpl_v, source_ref, rows_ref, sems):
+    return [
+        pltpu.make_async_copy(inv_hbm, own_ref.at[0], sems.at[0]),
+        pltpu.make_async_copy(cpl_hbm, cpl_v, sems.at[1]),
+        pltpu.make_async_copy(source_hbm, source_ref, sems.at[2]),
+        pltpu.make_async_copy(rows_hbm, rows_ref, sems.at[3]),
+    ]
+
+
+def prepare_front(rows_ref, send_ref, own_ref, source_ref, cpl_v):
+    modes, size, _ = cpl_v.shape
+    half = modes * size
+    select = one_hot(rows_ref, 1).astype(F32).T.astype(BF16)
+    for m in range(modes):
+        own_ref[1, m] = dot(select, cpl_v[m]).astype(BF16)
+        own_ref[2, m] = own_ref[0, m].T
+        own_ref[3, m] = own_ref[1, m].T
+    send_ref[:half, :] = own_ref[0].reshape(half, size)
+    rest = flat(source_ref)
+    for part in range(3):
+        at = half + part * rest.shape[0]
+        term = rest.astype(BF16)
+        send_ref[at : at + rest.shape[0], :] = term
+        rest = rest - term.astype(F32)
+
+
+def compose_kernel(
+    rows_hbm, inv_hbm, cpl_hbm, sep_hbm, up_hbm, src_hbm,
+    square_ref, joint_ref, send_ref, own_ref, source_ref, rows_ref,
+    inv_v, cpl_v, sems, up_v, side_sems,
+):
+    side = side_copies(sep_hbm, up_hbm, src_hbm, rows_hbm, own_ref, up_v, source_ref, rows_ref, side_sems)
     modes, front, _ = joint_ref.shape
     blocks, size = inv_v.shape[1], inv_v.shape[2]
     depth = inv_v.shape[0]
@@ -180,10 +207,17 @@
 
         return carry
 
+    for copy in side:
+        copy.start()
     lax.fori_loop(0, modes, one_mode, 0)
-
-
-def compose(inverse, coupling, depth=4):
+    for copy in side:
+        copy.wait()
+    prepare_front(rows_ref, send_ref, own_ref, source_ref, up_v)
+
+
+def compose(rows, inverse, coupling, sep_inverse, sep_coupling, source, depth=4):
+    count = source.shape[0]
+    size_s = source.shape[2]
     modes, blocks, size, _ = inverse.shape
     front, nodes = coupling.shape[1:]
     return pl.pallas_call(
@@ -191,13 +225,19 @@
         out_shape=[
             jax.ShapeDtypeStruct(inverse.shape, BF16),
             jax.ShapeDtypeStruct(coupling.shape, BF16),
+            jax.ShapeDtypeStruct((modes * size_s + 3 * count * modes, size_s), BF16),
+            jax.ShapeDtypeStruct((4, modes, size_s, size_s), BF16),
+            jax.ShapeDtypeStruct(source.shape, F32),
+            jax.ShapeDtypeStruct(rows.shape, rows.dtype),
         ],
-        in_specs=[pl.BlockSpec(memory_space=pltpu.HBM)] * 2,
-        out_specs=[pl.BlockSpec(memory_space=VMEM)] * 2,
+        in_specs=[pl.BlockSpec(memory_space=pltpu.HBM)] * 6,
+        out_specs=[pl.BlockSpec(memory_space=VMEM)] * 6,
         scratch_shapes=[
             VMEM((depth, blocks, size, size), BF16),
             VMEM((depth, front, nodes), BF16),
             pltpu.SemaphoreType.DMA((2, depth)),
+            VMEM(sep_coupling.shape, BF16),
+            pltpu.SemaphoreType.DMA((4,)),
         ],
         compiler_params=pltpu.CompilerParams(vmem_limit_bytes=COMPOSE),
         cost_estimate=pl.CostEstimate(
@@ -206,7 +246,7 @@
             transcendentals=0,
         ),
         name="compose",
-    )(inverse, coupling)
+    )(*(stay(value) for value in (rows, inverse, coupling, sep_inverse, sep_coupling, source)))
 
 
 def leaf_up_kernel(groups, rows_ref, mag_ref, joint_ref, *refs):
@@ -346,49 +386,6 @@
         compiler_params=pltpu.CompilerParams(vmem_limit_bytes=16 * 2**20),
         name="spread",
     )(*azi, *rest)
-
-
-def fronts_kernel(rows_ref, inv_hbm, cpl_hbm, source_hbm, send_ref, own_ref, source_ref, cpl_v, sems):
-    modes, size, _ = cpl_v.shape
-    half = modes * size
-    copies = [
-        pltpu.make_async_copy(inv_hbm, own_ref.at[0], sems.at[0]),
-        pltpu.make_async_copy(cpl_hbm, cpl_v, sems.at[1]),
-        pltpu.make_async_copy(source_hbm, source_ref, sems.at[2]),
-    ]
-    for copy in copies:
-        copy.start()
-    select = one_hot(rows_ref, 1).astype(F32).T.astype(BF16)
-    for copy in copies:
-        copy.wait()
-    for m in range(modes):
-        own_ref[1, m] = dot(select, cpl_v[m]).astype(BF16)
-        own_ref[2, m] = own_ref[0, m].T
-        own_ref[3, m] = own_ref[1, m].T
-    send_ref[:half, :] = own_ref[0].reshape(half, size)
-    rest = flat(source_ref)
-    for part in range(3):
-        at = half + part * rest.shape[0]
-        term = rest.astype(BF16)
-        send_ref[at : at + rest.shape[0], :] = term
-        rest = rest - term.astype(F32)
-
-
-def fronts(rows, inverse, coupling, source):
-    modes, size, _ = inverse.shape
-    return pl.pallas_call(
-        fronts_kernel,
-        out_shape=[
-            jax.ShapeDtypeStruct((modes * size + 3 * 2 * modes, size), BF16),
-            jax.ShapeDtypeStruct((4, modes, size, size), BF16),
-            jax.ShapeDtypeStruct(source.shape, F32),
-        ],
-        in_specs=[pl.BlockSpec(memory_space=VMEM)] + [pl.BlockSpec(memory_space=pltpu.HBM)] * 3,
-        out_specs=[pl.BlockSpec(memory_space=VMEM)] * 3,
-        scratch_shapes=[VMEM(coupling.shape, BF16), pltpu.SemaphoreType.DMA((3,))],
-        compiler_params=pltpu.CompilerParams(vmem_limit_bytes=SMALL),
-        name="fronts",
-    )(rows, stay(inverse), stay(coupling), stay(source))
 
 
 def apply(x, matrix):
@@ -503,15 +500,14 @@
     )
     spread_in = swap(packed)
     fwd, bwd = tables(groups, modes)
-    send, front, sep_source = fronts(
-        front_rows, separator_inverse, separator_coupling, separator_source
+    square, joint, send, front, sep_source, rows = compose(
+        front_rows, leaf_inverse, leaf_coupling, separator_inverse, separator_coupling, separator_source
     )
-    square, joint = compose(stay(leaf_inverse), stay(leaf_coupling))
     azi, rest = transform(fwd, bwd, spread_in)
     azi = swap(azi)
     lift = hop(send, [(0, mid)])
     rest = swap(rest)
-    source, update = leaf_up(front_rows, mag, azi, joint)
+    source, update = leaf_up(rows, mag, azi, joint)
     local = leaf_local(source, square)
     nonlinear = spread(azi, rest).reshape(3, 2, modes, nodes)
 
@@ -521,9 +517,7 @@
     reduced = [None] * (levels + 1)
     one, two = update, hop(update, [(q - 1, q) for q in of_level[1]])
     for height in range(1, levels):
-        reduced[height], outgoing = small_call(
-            rise_kernel, [wide, wide], [one, two, sep_source, front]
-        )
+        reduced[height], outgoing = small_call(rise_kernel, [wide, wide], [one, two, sep_source, front])
         gap = 2 ** (height - 1)
         one = hop(outgoing, [(q - gap, q) for q in of_level[height + 1]])
         two = hop(outgoing, [(q + gap, q) for q in of_level[height + 1]])
@@ -537,7 +531,7 @@
         answers.append((height, x))
     far = hop(top, [(mid, 0)])
     beside = hop(x16, [(q, q - 1) for q in of_level[1]])
-    azimuthal = leaf_down(front_rows, x16, beside, local, joint)
+    azimuthal = leaf_down(rows, x16, beside, local, joint)
     answers.reverse()
     (solution,) = small_call(choose_kernel, [wide], [x for _, x in answers] + [far])
     return (nonlinear, azimuthal, solution)

time: 70.1 us -> 74.9 us (1.068)
  waiting for transfers between devices: 18.6 us -> 25.9 us
  Pallas kernels: 28.3 us -> 26.8 us
    ppermute x12, waiting for transfers between devices: 12 us -> 17.1 us  [hop(): return lax.ppermute(value, 'mesh', pairs)]
    ppermute x9, waiting for transfers between devices: 6.62 us -> 8.78 us  [swap(): out.append(lax.ppermute(pieces[k], 'mode', exchange[k]))]
    pallas_call x1 -> x0, Pallas kernels: 1.75 us -> none  [fronts(): pl.pallas_call(fronts_kernel, out_shape=[jax.ShapeDtypeStruct((modes * si...]
  transfers between devices with their start and end apart: 21 -> 21, of which waited for: 6 -> 8; matrix products, arithmetic and copies ran while one was open for 0% -> 0% of each run, Pallas kernels for 34% -> 18%
where the time goes in v5:
time: 74.9 us; the launch traced here: 74.6 us
  Pallas kernels  26.8 us (36%)
  waiting for transfers between devices  25.9 us (35%)
  starting transfers between devices  21 us (28%)
  between operations  0.86 us (1%)
    ppermute x12, waiting for transfers between devices, hop(): return lax.ppermute(value, 'mesh', pairs)  17.1 us
    ppermute x12, starting transfers between devices, hop(): return lax.ppermute(value, 'mesh', pairs)  12.2 us
    pallas_call x1, Pallas kernels, compose(): pl.pallas_call(compose_kernel, out_shape=[jax.ShapeDtypeStruct(inverse.sh...  10.4 us
    ppermute x9, waiting for transfers between devices, swap(): out.append(lax.ppermute(pieces[k], 'mode', exchange[k]))  8.78 us
    ppermute x9, starting transfers between devices, swap(): out.append(lax.ppermute(pieces[k], 'mode', exchange[k]))  8.78 us
    pallas_call x1, Pallas kernels, leaf_up(): pl.pallas_call(functools.partial(leaf_up_kernel, groups), out_shape=[jax....  3.93 us
    pallas_call x6, Pallas kernels, small_call(): pl.pallas_call(kernel, out_shape=outs, in_specs=[pl.BlockSpec(memory_spac...  3.31 us
    pallas_call x1, Pallas kernels, leaf_down(): pl.pallas_call(leaf_down_kernel, out_shape=jax.ShapeDtypeStruct(local.sha...  2.77 us
  transfers between devices with their start and end apart: 21, of which 8 were waited for; matrix products, arithmetic and copies ran while one was open for 0% of the time, Pallas kernels for 18%

profile of v5, /device:TPU:1, one launch (start us, length us, event | category | flops | bytes accessed | tf_op | source)
XLA Modules:
  0.0 74.6 jit_solution(2827543911792592542)
XLA Ops:
  0.6 10.4 %compose.1 = (bf16[16,20,128,128]{3,2,1,0:T(8,128)(2,1)S(1)}, bf16[16,128,2560]{2,1,0:T(8,128)(2,1)S(1)}, bf16[2144,128]{1,0:T(8,128)(2,1)S(1)}, bf16[4,16,128,1...) custom-call(s32[1,2,128]{2,1,0:T(2,128)} %rows_hbm.1, ...), custom_call_target="tpu_custom_call" | custom-call | flops 5368709120 | bytes 41943040 | tf_op jit(solution)/shard_map/compose/pallas_call | solution.py:223
  11.1 0.7 collective-permute-start.14
  11.8 1.7 %pack.1 = (bf16[192,640]{1,0:T(8,128)(2,1)S(1)}, bf16[192,640]{1,0:T(8,128)(2,1)S(1)}, bf16[192,640]{1,0:T(8,128)(2,1)S(1)}, bf16[192,640]{1,0:T(8,128)(2,1)S(1)}, f32[32,2560]{1,0:T(8,128)S(1)}) custom-call(f32[96,2560]{1,0:T(8,128)} %bitcast.3, f32[96,2560]{1,0:T(8,128)} %bitcast.4), custom_call_target="tpu_custom_call" | custom-call | tf_op jit(solution)/shard_map/pack/pallas_call | solution.py:81
  13.5 2.1 %collective-permute-start = (bf16[192,640]{1,0:T(8,128)(2,1)S(1)}, bf16[192,640]{1,0:T(8,128)(2,1)S(1)}, u32[]{:S(2)}, u32[]{:S(2)}) collective-permute-start(bf16[192,640]{1,0:T(8,128)(2,1)S(1)} %get-tuple-element.40), channel_id=1, source_target_pairs={{0,8},{8,0},{16,24},{24,16},{1,9},{9,1},{17,25},{25,17},{2,10},{10... | collective-permute-start | bytes 737288 | tf_op jit(solution)/shard_map/ppermute | solution.py:492
  15.6 1.2 %collective-permute-start.1 = (bf16[192,640]{1,0:T(8,128)(2,1)S(1)}, bf16[192,640]{1,0:T(8,128)(2,1)S(1)}, u32[]{:S(2)}, u32[]{:S(2)}) collective-permute-start(bf16[192,640]{1,0:T(8,128)(2,1)S(1)} %get-tuple-element.41), channel_id=1, source_target_pairs={{0,16},{8,24},{16,0},{24,8},{1,17},{9,25},{17,1},{25,9},{2,18},{10... | collective-permute-start | bytes 737288 | tf_op jit(solution)/shard_map/ppermute | solution.py:492
  16.8 0.0 collective-permute-start.2
  16.9 0.4 tables.1
  17.3 1.9 %collective-permute-done.refs_1_ = bf16[192,640]{1,0:T(8,128)(2,1)S(1)} collective-permute-done((bf16[192,640]{1,0:T(8,128)(2,1)S(1)}, bf16[192,640]{1,0:T(8,128)(2,1)S(1)}, u32[]{:S(2)}, u32[]{:S(2)}) %collective-permute-start) | collective-permute-done | bytes 245792 | tf_op jit(solution)/shard_map/ppermute | solution.py:492
  19.2 4.3 %collective-permute-done.1.refs_2_ = bf16[192,640]{1,0:T(8,128)(2,1)S(1)} collective-permute-done((bf16[192,640]{1,0:T(8,128)(2,1)S(1)}, bf16[192,640]{1,0:T(8,128)(2,1)S(1)}, u32[]{:S(2)}, u32[]{:S(2)}) %collective-permute-start.1) | collective-permute-done | bytes 245792 | tf_op jit(solution)/shard_map/ppermute | solution.py:492
  23.5 0.0 collective-permute-done.2.refs_3_
  23.5 0.9 %transform.1 = (bf16[32,640]{1,0:T(8,128)(2,1)S(1)}, bf16[32,640]{1,0:T(8,128)(2,1)S(1)}, bf16[32,640]{1,0:T(8,128)(2,1)S(1)}, bf16[32,640]{1,0:T(8,128)(2,1)S(1...) custom-call(bf16[192,128]{1,0:T(8,128)(2,1)S(1)} %get-tuple-element., ...), custom_call_target="tpu_custom_call" | custom-call | tf_op jit(solution)/shard_map/transform/pallas_call | solution.py:119
  24.3 1.2 %collective-permute-start.3 = (bf16[32,640]{1,0:T(8,128)(2,1)S(1)}, bf16[32,640]{1,0:T(8,128)(2,1)S(1)}, u32[]{:S(2)}, u32[]{:S(2)}) collective-permute-start(bf16[32,640]{1,0:T(8,128)(2,1)S(1)} %get-tuple-element.44), channel_id=1, source_target_pairs={{0,8},{8,0},{16,24},{24,16},{1,9},{9,1},{17,25},{25,17},{2,10},{10... | collective-permute-start | bytes 122888 | tf_op jit(solution)/shard_map/ppermute | solution.py:492
  25.5 0.4 collective-permute-start.4
  25.9 1.1 %collective-permute-start.5 = (bf16[32,640]{1,0:T(8,128)(2,1)S(1)}, bf16[32,640]{1,0:T(8,128)(2,1)S(1)}, u32[]{:S(2)}, u32[]{:S(2)}) collective-permute-start(bf16[32,640]{1,0:T(8,128)(2,1)S(1)} %get-tuple-element.46), channel_id=1, source_target_pairs={{0,24},{8,16},{16,8},{24,0},{1,25},{9,17},{17,9},{25,1},{2,26},{10... | collective-permute-start | bytes 122888 | tf_op jit(solution)/shard_map/ppermute | solution.py:492
  27.0 0.9 %collective-permute-done.3.refs_1_ = bf16[32,640]{1,0:T(8,128)(2,1)S(1)} collective-permute-done((bf16[32,640]{1,0:T(8,128)(2,1)S(1)}, bf16[32,640]{1,0:T(8,128)(2,1)S(1)}, u32[]{:S(2)}, u32[]{:S(2)}) %collective-permute-start.3) | collective-permute-done | bytes 40992 | tf_op jit(solution)/shard_map/ppermute | solution.py:492
  28.0 1.2 %collective-permute-done.4.refs_2_ = bf16[32,640]{1,0:T(8,128)(2,1)S(1)} collective-permute-done((bf16[32,640]{1,0:T(8,128)(2,1)S(1)}, bf16[32,640]{1,0:T(8,128)(2,1)S(1)}, u32[]{:S(2)}, u32[]{:S(2)}) %collective-permute-start.4) | collective-permute-done | bytes 40992 | tf_op jit(solution)/shard_map/ppermute | solution.py:492
  29.1 0.5 collective-permute-done.5.refs_3_
  29.7 3.9 %leaf_up.1 = (f32[2,16,2560]{2,1,0:T(8,128)S(1)}, f32[2,16,128]{2,1,0:T(8,128)S(1)}) custom-call(s32[1,2,128]{2,1,0:T(2,128)S(1)} %get-tuple-element.51.rows_ref, f32[32,2560]{1,0:T(8,128)S(1)} %get-tuple-element.52.mag_ref, bf16[16,128,2560]{2,1,0:T(8,128)(2,1)S(1)} %get-tuple-element.53.joint_ref, bf16[32,640]{1,0:T(8,128)(2,1)S(1)} %get-tuple-element.43.refs_0_, ...), custom_call_target="tpu_custom_call" | custom-call | flops 671088640 | bytes 10485760 | tf_op jit(solution)/shard_map/leaf_up/pallas_call | solution.py:278
  33.6 1.3 %collective-permute-start.9 = (f32[2,16,128]{2,1,0:T(8,128)S(1)}, f32[2,16,128]{2,1,0:T(8,128)S(1)}, u32[]{:S(2)}, u32[]{:S(2)}) collective-permute-start(f32[2,16,128]{2,1,0:T(8,128)S(1)} %get-tuple-element.54.one_ref), channel_id=1, source_target_pairs={{0,1},{2,3},{4,5},{6,7},{8,9},{10,11},{12,13},{14,15},{16,17},{18,... | collective-permute-start | bytes 49160 | tf_op jit(solution)/shard_map/ppermute | solution.py:496
  34.9 8.3 %collective-permute-done.9.two_ref = f32[2,16,128]{2,1,0:T(8,128)S(1)} collective-permute-done((f32[2,16,128]{2,1,0:T(8,128)S(1)}, f32[2,16,128]{2,1,0:T(8,128)S(1)}, u32[]{:S(2)}, u32[]{:S(2)}) %collective-permute-start.9) | collective-permute-done | bytes 16416 | tf_op jit(solution)/shard_map/ppermute | solution.py:496
  43.2 0.4 shard_map.103
  43.6 3.0 %collective-permute-start.10 = (f32[2,16,128]{2,1,0:T(8,128)S(1)}, f32[2,16,128]{2,1,0:T(8,128)S(1)}, u32[]{:S(2)}, u32[]{:S(2)}) collective-permute-start(f32[2,16,128]{2,1,0:T(8,128)S(1)} %get-tuple-element.57), channel_id=1, source_target_pairs={{1,2},{5,6},{9,10},{13,14},{17,18},{21,22},{25,26},{29,30}} | collective-permute-start | bytes 49160 | tf_op jit(solution)/shard_map/ppermute | solution.py:496
  46.7 0.7 collective-permute-start.11
  47.3 0.2 collective-permute-done.10.one_ref
  47.5 0.0 collective-permute-done.11.two_ref
  47.5 0.4 shard_map.104
  47.9 0.7 collective-permute-start.12
  48.6 0.7 collective-permute-start.13
  49.2 1.3 %collective-permute-start.6 = (bf16[64,640]{1,0:T(8,128)(2,1)S(1)}, bf16[64,640]{1,0:T(8,128)(2,1)S(1)}, u32[]{:S(2)}, u32[]{:S(2)}) collective-permute-start(bf16[64,640]{1,0:T(8,128)(2,1)S(1)} %get-tuple-element.48), channel_id=1, source_target_pairs={{0,8},{8,0},{16,24},{24,16},{1,9},{9,1},{17,25},{25,17},{2,10},{10... | collective-permute-start | bytes 245768 | tf_op jit(solution)/shard_map/ppermute | solution.py:492
  50.5 0.2 collective-permute-start.7
  50.7 0.0 collective-permute-done.12.one_ref
  50.8 1.2 %collective-permute-start.8 = (bf16[64,640]{1,0:T(8,128)(2,1)S(1)}, bf16[64,640]{1,0:T(8,128)(2,1)S(1)}, u32[]{:S(2)}, u32[]{:S(2)}) collective-permute-start(bf16[64,640]{1,0:T(8,128)(2,1)S(1)} %get-tuple-element.50), channel_id=1, source_target_pairs={{0,24},{8,16},{16,8},{24,0},{1,25},{9,17},{17,9},{25,1},{2,26},{10... | collective-permute-start | bytes 245768 | tf_op jit(solution)/shard_map/ppermute | solution.py:492
  52.0 0.0 collective-permute-done.13.two_ref
  52.0 0.0 collective-permute-done.14.lift_ref
  52.0 1.2 %shard_map.105 = (f32[2,16,128]{2,1,0:T(8,128)S(1)}, bf16[2,16,128]{2,1,0:T(8,128)(2,1)S(1)}, f32[2,16,128]{2,1,0:T(8,128)S(1)}) custom-call(f32[2,16,128]{2,1,0:T(8,128)S(1)} %collective-permute-done.12.one_ref, f32[2,16,128]{2,1,0:T(8,128)S(1)} %collective-permute-done.13.two_ref, f32[2,16,128]{2,1,0:T(8,128)S(1)} %get-tuple-element.55.source_ref, ...), custom_call_target="tpu_custom_call" | custom-call | tf_op jit(solution)/shard_map/pallas_call | solution.py:414
  53.1 0.7 collective-permute-start.15
  53.8 0.7 collective-permute-start.16
  54.5 0.0 collective-permute-done.15.one_ref
  54.5 0.0 collective-permute-done.16.two_ref
  54.5 0.4 shard_map.106
  54.9 1.3 %collective-permute-start.17 = (bf16[2,16,128]{2,1,0:T(8,128)(2,1)S(1)}, bf16[2,16,128]{2,1,0:T(8,128)(2,1)S(1)}, u32[]{:S(2)}, u32[]{:S(2)}) collective-permute-start(bf16[2,16,128]{2,1,0:T(8,128)(2,1)S(1)} %get-tuple-element.62), channel_id=1, source_target_pairs={{2,1},{6,5},{10,9},{14,13},{18,17},{22,21},{26,25},{30,29}} | collective-permute-start | bytes 24584 | tf_op jit(solution)/shard_map/ppermute | solution.py:496
  56.2 0.7 collective-permute-start.18
  56.9 8.6 %collective-permute-done.17.one_ref = bf16[2,16,128]{2,1,0:T(8,128)(2,1)S(1)} collective-permute-done((bf16[2,16,128]{2,1,0:T(8,128)(2,1)S(1)}, bf16[2,16,128]{2,1,0:T(8,128)(2,1)S(1)}, u32[]{:S(2)}, u32[]{:S(2)}) %collective-permute-start.17) | collective-permute-done | bytes 8224 | tf_op jit(solution)/shard_map/ppermute | solution.py:496
  65.5 0.7 collective-permute-start.20
  66.1 0.0 collective-permute-done.18.two_ref
  66.1 0.4 shard_map.107
  66.5 1.3 %collective-permute-start.19 = (bf16[2,16,128]{2,1,0:T(8,128)(2,1)S(1)}, bf16[2,16,128]{2,1,0:T(8,128)(2,1)S(1)}, u32[]{:S(2)}, u32[]{:S(2)}) collective-permute-start(bf16[2,16,128]{2,1,0:T(8,128)(2,1)S(1)} %get-tuple-element.64.here_ref), channel_id=1, source_target_pairs={{1,0},{3,2},{5,4},{7,6},{9,8},{11,10},{13,12},{15,14},{17,16},{19,... | collective-permute-start | bytes 24584 | tf_op jit(solution)/shard_map/ppermute | solution.py:496
  67.8 2.4 %leaf_local.1.local_ref = f32[2,16,2560]{2,1,0:T(8,128)S(1)} custom-call(f32[2,16,2560]{2,1,0:T(8,128)S(1)} %get-tuple-element.65.source_ref, bf16[16,20,128,128]{3,2,1,0:T(8,128)(2,1)S(1)} %get-tuple-element.66.square_ref), custom_call_target="tpu_custom_call" | custom-call | flops 671088640 | bytes 10485760 | tf_op jit(solution)/shard_map/leaf_local/pallas_call | solution.py:319
  70.2 0.0 collective-permute-done.6.refs_5_
  70.2 0.0 collective-permute-done.7.refs_6_
  70.2 0.0 collective-permute-done.8.refs_7_
  70.2 1.0 %spread.1 = f32[96,2560]{1,0:T(8,128)} custom-call(bf16[32,640]{1,0:T(8,128)(2,1)S(1)} %get-tuple-element.43.refs_0_, bf16[32,640]{1,0:T(8,128)(2,1)S(1)} %collective-permute-done.3.refs_1_, bf16[32,640]{1,0:T(8,128)(2,1)S(1)} %collective-permute-done.4.refs_2_, bf16[32,640]{1,0:T(8,128)(2,1)S(1)} %collective-permute-done.5.refs_3_, ...), custom_call_target="tpu_custom_call" | custom-call | tf_op jit(solution)/shard_map/spread/pallas_call | solution.py:381
  71.2 0.0 collective-permute-done.20.refs_3_
  71.2 0.6 shard_map.108
  71.9 0.0 collective-permute-done.19.beside_ref
  71.9 2.8 %leaf_down.1 = f32[2,16,2560]{2,1,0:T(8,128)} custom-call(s32[1,2,128]{2,1,0:T(2,128)S(1)} %get-tuple-element.51.rows_ref, bf16[2,16,128]{2,1,0:T(8,128)(2,1)S(1)} %get-tuple-element.64.here_ref, bf16[2,16,128]{2,1,0:T(8,128)(2,1)S(1)} %collective-permute-done.19.beside_ref, f32[2,16,2560]{2,1,0:T(8,128)S(1)} %leaf_local.1.local_ref, ...), custom_call_target="tpu_custom_call" | custom-call | tf_op jit(solution)/shard_map/leaf_down/pallas_call | solution.py:357
Async XLA Ops:
  11.1 40.9 %collective-permute-start.14 = (bf16[2144,128]{1,0:T(8,128)(2,1)S(1)}, bf16[2144,128]{1,0:T(8,128)(2,1)S(1)}, u32[]{:S(2)}, u32[]{:S(2)}) collective-permute-start(bf16[2144,128]{1,0:T(8,128)(2,1)S(1)} %get-tuple-element.59), channel_id=1, source_target_pairs={{0,4},{8,12},{16,20},{24,28}} | collective-permute-start | bytes 1646600 | tf_op jit(solution)/shard_map/ppermute | solution.py:496
  13.5 5.7 %collective-permute-start = (bf16[192,640]{1,0:T(8,128)(2,1)S(1)}, bf16[192,640]{1,0:T(8,128)(2,1)S(1)}, u32[]{:S(2)}, u32[]{:S(2)}) collective-permute-start(bf16[192,640]{1,0:T(8,128)(2,1)S(1)} %get-tuple-element.40), channel_id=1, source_target_pairs={{0,8},{8,0},{16,24},{24,16},{1,9},{9,1},{17,25},{25,17},{2,10},{10... | collective-permute-start | bytes 737288 | tf_op jit(solution)/shard_map/ppermute | solution.py:492
  15.6 7.8 %collective-permute-start.1 = (bf16[192,640]{1,0:T(8,128)(2,1)S(1)}, bf16[192,640]{1,0:T(8,128)(2,1)S(1)}, u32[]{:S(2)}, u32[]{:S(2)}) collective-permute-start(bf16[192,640]{1,0:T(8,128)(2,1)S(1)} %get-tuple-element.41), channel_id=1, source_target_pairs={{0,16},{8,24},{16,0},{24,8},{1,17},{9,25},{17,1},{25,9},{2,18},{10... | collective-permute-start | bytes 737288 | tf_op jit(solution)/shard_map/ppermute | solution.py:492
  16.8 6.6 %collective-permute-start.2 = (bf16[192,640]{1,0:T(8,128)(2,1)S(1)}, bf16[192,640]{1,0:T(8,128)(2,1)S(1)}, u32[]{:S(2)}, u32[]{:S(2)}) collective-permute-start(bf16[192,640]{1,0:T(8,128)(2,1)S(1)} %get-tuple-element.42), channel_id=1, source_target_pairs={{0,24},{8,16},{16,8},{24,0},{1,25},{9,17},{17,9},{25,1},{2,26},{10... | collective-permute-start | bytes 737288 | tf_op jit(solution)/shard_map/ppermute | solution.py:492
  24.3 3.6 %collective-permute-start.3 = (bf16[32,640]{1,0:T(8,128)(2,1)S(1)}, bf16[32,640]{1,0:T(8,128)(2,1)S(1)}, u32[]{:S(2)}, u32[]{:S(2)}) collective-permute-start(bf16[32,640]{1,0:T(8,128)(2,1)S(1)} %get-tuple-element.44), channel_id=1, source_target_pairs={{0,8},{8,0},{16,24},{24,16},{1,9},{9,1},{17,25},{25,17},{2,10},{10... | collective-permute-start | bytes 122888 | tf_op jit(solution)/shard_map/ppermute | solution.py:492
  25.5 3.6 %collective-permute-start.4 = (bf16[32,640]{1,0:T(8,128)(2,1)S(1)}, bf16[32,640]{1,0:T(8,128)(2,1)S(1)}, u32[]{:S(2)}, u32[]{:S(2)}) collective-permute-start(bf16[32,640]{1,0:T(8,128)(2,1)S(1)} %get-tuple-element.45), channel_id=1, source_target_pairs={{0,16},{8,24},{16,0},{24,8},{1,17},{9,25},{17,1},{25,9},{2,18},{10... | collective-permute-start | bytes 122888 | tf_op jit(solution)/shard_map/ppermute | solution.py:492
  25.9 3.8 %collective-permute-start.5 = (bf16[32,640]{1,0:T(8,128)(2,1)S(1)}, bf16[32,640]{1,0:T(8,128)(2,1)S(1)}, u32[]{:S(2)}, u32[]{:S(2)}) collective-permute-start(bf16[32,640]{1,0:T(8,128)(2,1)S(1)} %get-tuple-element.46), channel_id=1, source_target_pairs={{0,24},{8,16},{16,8},{24,0},{1,25},{9,17},{17,9},{25,1},{2,26},{10... | collective-permute-start | bytes 122888 | tf_op jit(solution)/shard_map/ppermute | solution.py:492
  33.6 9.6 %collective-permute-start.9 = (f32[2,16,128]{2,1,0:T(8,128)S(1)}, f32[2,16,128]{2,1,0:T(8,128)S(1)}, u32[]{:S(2)}, u32[]{:S(2)}) collective-permute-start(f32[2,16,128]{2,1,0:T(8,128)S(1)} %get-tuple-element.54.one_ref), channel_id=1, source_target_pairs={{0,1},{2,3},{4,5},{6,7},{8,9},{10,11},{12,13},{14,15},{16,17},{18,... | collective-permute-start | bytes 49160 | tf_op jit(solution)/shard_map/ppermute | solution.py:496
  43.6 3.9 %collective-permute-start.10 = (f32[2,16,128]{2,1,0:T(8,128)S(1)}, f32[2,16,128]{2,1,0:T(8,128)S(1)}, u32[]{:S(2)}, u32[]{:S(2)}) collective-permute-start(f32[2,16,128]{2,1,0:T(8,128)S(1)} %get-tuple-element.57), channel_id=1, source_target_pairs={{1,2},{5,6},{9,10},{13,14},{17,18},{21,22},{25,26},{29,30}} | collective-permute-start | bytes 49160 | tf_op jit(solution)/shard_map/ppermute | solution.py:496
  46.7 0.9 %collective-permute-start.11 = (f32[2,16,128]{2,1,0:T(8,128)S(1)}, f32[2,16,128]{2,1,0:T(8,128)S(1)}, u32[]{:S(2)}, u32[]{:S(2)}) collective-permute-start(f32[2,16,128]{2,1,0:T(8,128)S(1)} %get-tuple-element.57), channel_id=1, source_target_pairs={{3,2},{7,6},{11,10},{15,14},{19,18},{23,22},{27,26},{31,30}} | collective-permute-start | bytes 49160 | tf_op jit(solution)/shard_map/ppermute | solution.py:496
  47.9 2.8 %collective-permute-start.12 = (f32[2,16,128]{2,1,0:T(8,128)S(1)}, f32[2,16,128]{2,1,0:T(8,128)S(1)}, u32[]{:S(2)}, u32[]{:S(2)}) collective-permute-start(f32[2,16,128]{2,1,0:T(8,128)S(1)} %get-tuple-element.58), channel_id=1, source_target_pairs={{2,4},{10,12},{18,20},{26,28}} | collective-permute-start | bytes 49160 | tf_op jit(solution)/shard_map/ppermute | solution.py:496
  48.6 3.4 %collective-permute-start.13 = (f32[2,16,128]{2,1,0:T(8,128)S(1)}, f32[2,16,128]{2,1,0:T(8,128)S(1)}, u32[]{:S(2)}, u32[]{:S(2)}) collective-permute-start(f32[2,16,128]{2,1,0:T(8,128)S(1)} %get-tuple-element.58), channel_id=1, source_target_pairs={{6,4},{14,12},{22,20},{30,28}} | collective-permute-start | bytes 49160 | tf_op jit(solution)/shard_map/ppermute | solution.py:496
  49.2 20.9 %collective-permute-start.6 = (bf16[64,640]{1,0:T(8,128)(2,1)S(1)}, bf16[64,640]{1,0:T(8,128)(2,1)S(1)}, u32[]{:S(2)}, u32[]{:S(2)}) collective-permute-start(bf16[64,640]{1,0:T(8,128)(2,1)S(1)} %get-tuple-element.48), channel_id=1, source_target_pairs={{0,8},{8,0},{16,24},{24,16},{1,9},{9,1},{17,25},{25,17},{2,10},{10... | collective-permute-start | bytes 245768 | tf_op jit(solution)/shard_map/ppermute | solution.py:492
  50.5 19.7 %collective-permute-start.7 = (bf16[64,640]{1,0:T(8,128)(2,1)S(1)}, bf16[64,640]{1,0:T(8,128)(2,1)S(1)}, u32[]{:S(2)}, u32[]{:S(2)}) collective-permute-start(bf16[64,640]{1,0:T(8,128)(2,1)S(1)} %get-tuple-element.49), channel_id=1, source_target_pairs={{0,16},{8,24},{16,0},{24,8},{1,17},{9,25},{17,1},{25,9},{2,18},{10... | collective-permute-start | bytes 245768 | tf_op jit(solution)/shard_map/ppermute | solution.py:492
  50.8 19.5 %collective-permute-start.8 = (bf16[64,640]{1,0:T(8,128)(2,1)S(1)}, bf16[64,640]{1,0:T(8,128)(2,1)S(1)}, u32[]{:S(2)}, u32[]{:S(2)}) collective-permute-start(bf16[64,640]{1,0:T(8,128)(2,1)S(1)} %get-tuple-element.50), channel_id=1, source_target_pairs={{0,24},{8,16},{16,8},{24,0},{1,25},{9,17},{17,9},{25,1},{2,26},{10... | collective-permute-start | bytes 245768 | tf_op jit(solution)/shard_map/ppermute | solution.py:492
  53.1 1.3 %collective-permute-start.15 = (bf16[2,16,128]{2,1,0:T(8,128)(2,1)S(1)}, bf16[2,16,128]{2,1,0:T(8,128)(2,1)S(1)}, u32[]{:S(2)}, u32[]{:S(2)}) collective-permute-start(bf16[2,16,128]{2,1,0:T(8,128)(2,1)S(1)} %get-tuple-element.60), channel_id=1, source_target_pairs={{4,2},{12,10},{20,18},{28,26}} | collective-permute-start | bytes 24584 | tf_op jit(solution)/shard_map/ppermute | solution.py:496
  53.8 0.7 collective-permute-start.16
  54.9 10.6 %collective-permute-start.17 = (bf16[2,16,128]{2,1,0:T(8,128)(2,1)S(1)}, bf16[2,16,128]{2,1,0:T(8,128)(2,1)S(1)}, u32[]{:S(2)}, u32[]{:S(2)}) collective-permute-start(bf16[2,16,128]{2,1,0:T(8,128)(2,1)S(1)} %get-tuple-element.62), channel_id=1, source_target_pairs={{2,1},{6,5},{10,9},{14,13},{18,17},{22,21},{26,25},{30,29}} | collective-permute-start | bytes 24584 | tf_op jit(solution)/shard_map/ppermute | solution.py:496
  56.2 9.9 %collective-permute-start.18 = (bf16[2,16,128]{2,1,0:T(8,128)(2,1)S(1)}, bf16[2,16,128]{2,1,0:T(8,128)(2,1)S(1)}, u32[]{:S(2)}, u32[]{:S(2)}) collective-permute-start(bf16[2,16,128]{2,1,0:T(8,128)(2,1)S(1)} %get-tuple-element.62), channel_id=1, source_target_pairs={{2,3},{6,7},{10,11},{14,15},{18,19},{22,23},{26,27},{30,31}} | collective-permute-start | bytes 24584 | tf_op jit(solution)/shard_map/ppermute | solution.py:496
  65.5 5.8 %collective-permute-start.20 = (f32[2,16,128]{2,1,0:T(8,128)S(1)}, f32[2,16,128]{2,1,0:T(8,128)S(1)}, u32[]{:S(2)}, u32[]{:S(2)}) collective-permute-start(f32[2,16,128]{2,1,0:T(8,128)S(1)} %get-tuple-element.70), channel_id=1, source_target_pairs={{4,0},{12,8},{20,16},{28,24}} | collective-permute-start | bytes 49160 | tf_op jit(solution)/shard_map/ppermute | solution.py:496
  66.5 5.3 %collective-permute-start.19 = (bf16[2,16,128]{2,1,0:T(8,128)(2,1)S(1)}, bf16[2,16,128]{2,1,0:T(8,128)(2,1)S(1)}, u32[]{:S(2)}, u32[]{:S(2)}) collective-permute-start(bf16[2,16,128]{2,1,0:T(8,128)(2,1)S(1)} %get-tuple-element.64.here_ref), channel_id=1, source_target_pairs={{1,0},{3,2},{5,4},{7,6},{9,8},{11,10},{13,12},{15,14},{17,16},{19,... | collective-permute-start | bytes 24584 | tf_op jit(solution)/shard_map/ppermute | solution.py:496

commit v6 on v5

--- a/solution.py
+++ b/solution.py
@@ -90,42 +90,37 @@
     )(velocity, magnetic)
 
 
-def transform_kernel(groups, fwd_ref, bwd_ref, *refs):
-    ins, azi, rest = refs[:groups], refs[groups : 2 * groups], refs[2 * groups :]
+def transform_kernel(groups, components, fwd_ref, bwd_ref, *refs):
+    ins, outs = refs[:groups], refs[groups:]
     rows = ins[0].shape[0] // 6
     fwd, bwd = fwd_ref[...], bwd_ref[...]
-    phys = []
-    for field in range(6):
+    used = sorted({(c + s) % 3 for c in components for s in (1, 2)})
+
+    def phys(field):
         coef = jnp.concatenate([r[field * rows : (field + 1) * rows, :] for r in ins], axis=0)
-        phys.append(dot(fwd, coef))
-    v, b = phys[:3], phys[3:]
-    for c in range(3):
+        return dot(fwd, coef)
+
+    v, b = {c: phys(c) for c in used}, {c: phys(3 + c) for c in used}
+    for at, c in enumerate(components):
         p, q = (c + 1) % 3, (c + 2) % 3
         crossed = (v[p] * b[q] - v[q] * b[p]).astype(BF16)
         terms = dot(bwd, crossed).astype(BF16)
         for k in range(groups):
-            block = terms[k * rows : (k + 1) * rows, :]
-            if c == 1:
-                azi[k][...] = block
-            else:
-                at = 0 if c == 0 else rows
-                rest[k][at : at + rows, :] = block
-
-
-def transform(fwd, bwd, pieces):
+            outs[k][at * rows : (at + 1) * rows, :] = terms[k * rows : (k + 1) * rows, :]
+
+
+def transform(fwd, bwd, pieces, components):
     groups = len(pieces)
     rows, width = pieces[0].shape
-    rows = rows // 6
-    out = pl.pallas_call(
-        functools.partial(transform_kernel, groups),
-        out_shape=[jax.ShapeDtypeStruct((rows, width), BF16)] * groups
-        + [jax.ShapeDtypeStruct((2 * rows, width), BF16)] * groups,
+    rows = rows // 6 * len(components)
+    return pl.pallas_call(
+        functools.partial(transform_kernel, groups, components),
+        out_shape=[jax.ShapeDtypeStruct((rows, width), BF16)] * groups,
         in_specs=[pl.BlockSpec(memory_space=VMEM)] * (2 + groups),
-        out_specs=[pl.BlockSpec(memory_space=VMEM)] * (2 * groups),
+        out_specs=[pl.BlockSpec(memory_space=VMEM)] * groups,
         compiler_params=pltpu.CompilerParams(vmem_limit_bytes=24 * 2**20),
         name="transform",
     )(fwd, bwd, *pieces)
-    return out[:groups], out[groups:]
 
 
 def one_hot(rows_ref, which):
@@ -329,7 +324,18 @@
     )(source, square)
 
 
-def leaf_down_kernel(rows_ref, here_ref, beside_ref, local_ref, joint_ref, out_ref, x_v):
+def leaf_down_kernel(rows_ref, here_ref, beside_ref, local_ref, joint_ref, *refs):
+    answers, (out_ref, solution_ref, x_v) = refs[:-3], refs[-3:]
+    position = lax.axis_index("mesh")
+    for at, ref in enumerate(answers):
+        owner = position % 2**at == 0
+        if at < len(answers) - 1:
+            owner &= position % 2 ** (at + 1) != 0
+
+        @pl.when(owner)
+        def _(ref=ref):
+            solution_ref[...] = ref[...]
+
     modes, front, nodes = joint_ref.shape
     select = one_hot(rows_ref, 0).astype(F32).astype(BF16)
     above = jnp.where(lax.axis_index("mesh") % 2 == 1, here_ref[...].astype(F32), beside_ref[...].astype(F32))
@@ -352,17 +358,20 @@
     lax.fori_loop(0, modes // 2, two_modes, 0, unroll=2)
 
 
-def leaf_down(rows, here, beside, local, joint):
+def leaf_down(rows, here, beside, local, joint, answers):
     whole = pl.BlockSpec(memory_space=VMEM)
     return pl.pallas_call(
         leaf_down_kernel,
-        out_shape=jax.ShapeDtypeStruct(local.shape, F32),
-        in_specs=[whole] * 5,
-        out_specs=whole,
+        out_shape=[
+            jax.ShapeDtypeStruct(local.shape, F32),
+            jax.ShapeDtypeStruct(here.shape, F32),
+        ],
+        in_specs=[whole] * (5 + len(answers)),
+        out_specs=[whole] * 2,
         scratch_shapes=[VMEM(here.shape, F32)],
         compiler_params=pltpu.CompilerParams(vmem_limit_bytes=LARGE),
         name="leaf_down",
-    )(rows, here, beside, local, joint)
+    )(rows, here, beside, local, joint, *answers)
 
 
 def spread_kernel(groups, *refs):
@@ -427,21 +436,23 @@
     outgoing_ref[...] = apply(reduced, front_ref[3]).reshape(outgoing_ref.shape)
 
 
-def crown_kernel(one_ref, two_ref, source_ref, front_ref, lift_ref, x_ref, x16_ref, top_ref):
-    _, modes, size, _ = front_ref.shape
-    rows = 2 * modes
-    half = modes * size
-    g = (flat(source_ref) - (flat(one_ref) + flat(two_ref))).astype(BF16)
-    mid = apply(g, front_ref[2]).astype(BF16)
-    terms = [lift_ref[half + p * rows : half + (p + 1) * rows, :].astype(F32) for p in range(3)]
-    g = (terms[0] + terms[1] + terms[2] - apply(mid, front_ref[3])).astype(BF16)
-    inverse = lift_ref[:half, :].reshape(modes, size, size)
-    top = apply(apply_turned(g, inverse).astype(BF16), inverse)
-    top_ref[...] = top.reshape(top_ref.shape)
-    residue = mid.astype(F32) - apply(top.astype(BF16), front_ref[1])
-    x = apply(residue.astype(BF16), front_ref[0])
-    x_ref[...] = x.reshape(x_ref.shape)
-    x16_ref[...] = x.astype(BF16).reshape(x_ref.shape)
+def crown_kernel(mid_at, one_ref, two_ref, source_ref, front_ref, lift_ref, x_ref, x16_ref, top_ref):
+    @pl.when(lax.axis_index("mesh") == mid_at)
+    def _():
+        _, modes, size, _ = front_ref.shape
+        rows = 2 * modes
+        half = modes * size
+        g = (flat(source_ref) - (flat(one_ref) + flat(two_ref))).astype(BF16)
+        mid = apply(g, front_ref[2]).astype(BF16)
+        terms = [lift_ref[half + p * rows : half + (p + 1) * rows, :].astype(F32) for p in range(3)]
+        g = (terms[0] + terms[1] + terms[2] - apply(mid, front_ref[3])).astype(BF16)
+        inverse = lift_ref[:half, :].reshape(modes, size, size)
+        top = apply(apply_turned(g, inverse).astype(BF16), inverse)
+        top_ref[...] = top.reshape(top_ref.shape)
+        residue = mid.astype(F32) - apply(top.astype(BF16), front_ref[1])
+        x = apply(residue.astype(BF16), front_ref[0])
+        x_ref[...] = x.reshape(x_ref.shape)
+        x16_ref[...] = x.astype(BF16).reshape(x_ref.shape)
 
 
 def sink_kernel(one_ref, two_ref, reduced_ref, front_ref, x_ref, x16_ref):
@@ -454,19 +465,6 @@
 
 def level_of(q, levels):
     return levels + 1 if q == 0 else (q & -q).bit_length()
-
-
-def choose_kernel(*refs):
-    position = lax.axis_index("mesh")
-    last = len(refs) - 2
-    for at, ref in enumerate(refs[:-1]):
-        here = position % 2**at == 0
-        if at < last:
-            here &= position % 2 ** (at + 1) != 0
-
-        @pl.when(here)
-        def _(ref=ref):
-            refs[-1][...] = ref[...]
 
 
 def shards(
@@ -503,9 +501,9 @@
     square, joint, send, front, sep_source, rows = compose(
         front_rows, leaf_inverse, leaf_coupling, separator_inverse, separator_coupling, separator_source
     )
-    azi, rest = transform(fwd, bwd, spread_in)
-    azi = swap(azi)
+    azi = swap(transform(fwd, bwd, spread_in, (1,)))
     lift = hop(send, [(0, mid)])
+    rest = transform(fwd, bwd, spread_in, (0, 2))
     rest = swap(rest)
     source, update = leaf_up(rows, mag, azi, joint)
     local = leaf_local(source, square)
@@ -521,19 +519,19 @@
         gap = 2 ** (height - 1)
         one = hop(outgoing, [(q - gap, q) for q in of_level[height + 1]])
         two = hop(outgoing, [(q + gap, q) for q in of_level[height + 1]])
-    x, x16, top = small_call(crown_kernel, [wide, half, wide], [one, two, sep_source, front, lift])
-    answers = [(levels, x)]
+    x, x16, top = small_call(
+        functools.partial(crown_kernel, mid), [wide, half, wide], [one, two, sep_source, front, lift]
+    )
+    far = hop(top, [(mid, 0)])
+    answers = [x, far]
     for height in range(levels - 1, 0, -1):
         gap = 2 ** (height - 1)
         one = hop(x16, [(q, q - gap) for q in of_level[height + 1]])
         two = hop(x16, [(q, q + gap) for q in of_level[height + 1]])
         x, x16 = small_call(sink_kernel, [wide, half], [one, two, reduced[height], front])
-        answers.append((height, x))
-    far = hop(top, [(mid, 0)])
+        answers.insert(0, x)
     beside = hop(x16, [(q, q - 1) for q in of_level[1]])
-    azimuthal = leaf_down(rows, x16, beside, local, joint)
-    answers.reverse()
-    (solution,) = small_call(choose_kernel, [wide], [x for _, x in answers] + [far])
+    azimuthal, solution = leaf_down(rows, x16, beside, local, joint, answers)
     return (nonlinear, azimuthal, solution)
 
 

time: 74.9 us -> 78 us (1.041)
  waiting for transfers between devices: 25.9 us -> 29.8 us
  Pallas kernels: 26.8 us -> 25.6 us
    ppermute x12, waiting for transfers between devices: 17.1 us -> 20.9 us  [hop(): return lax.ppermute(value, 'mesh', pairs)]
    pallas_call x6 -> x5, Pallas kernels: 3.31 us -> 1.54 us  [small_call(): pl.pallas_call(kernel, out_shape=outs, in_specs=[pl.BlockSpec(memory_spac...]
    pallas_call x2 -> x3, Pallas kernels: 3.62 us -> 4.14 us  [the longest x1 2.79 us: leaf_down(): pl.pallas_call(leaf_down_kernel, out_shape=[jax.ShapeDtypeStruct(local.sh...]
  transfers between devices with their start and end apart: 21 -> 21, of which waited for: 8 -> 7; matrix products, arithmetic and copies ran while one was open for 0% -> 0% of each run, Pallas kernels for 18% -> 16%
where the time goes in v6:
time: 78 us; the launch traced here: 77.7 us
  waiting for transfers between devices  29.8 us (38%)
  Pallas kernels  25.6 us (33%)
  starting transfers between devices  21.4 us (27%)
  between operations  0.86 us (1%)
    ppermute x12, waiting for transfers between devices, hop(): return lax.ppermute(value, 'mesh', pairs)  20.9 us
    ppermute x12, starting transfers between devices, hop(): return lax.ppermute(value, 'mesh', pairs)  12.7 us
    pallas_call x1, Pallas kernels, compose(): pl.pallas_call(compose_kernel, out_shape=[jax.ShapeDtypeStruct(inverse.sh...  10.4 us
    ppermute x9, waiting for transfers between devices, swap(): out.append(lax.ppermute(pieces[k], 'mode', exchange[k]))  8.87 us
    ppermute x9, starting transfers between devices, swap(): out.append(lax.ppermute(pieces[k], 'mode', exchange[k]))  8.78 us
    pallas_call x1, Pallas kernels, leaf_up(): pl.pallas_call(functools.partial(leaf_up_kernel, groups), out_shape=[jax....  3.93 us
    pallas_call x1, Pallas kernels, leaf_down(): pl.pallas_call(leaf_down_kernel, out_shape=[jax.ShapeDtypeStruct(local.sh...  2.79 us
    pallas_call x1, Pallas kernels, leaf_local(): pl.pallas_call(leaf_local_kernel, out_shape=jax.ShapeDtypeStruct(source.s...  2.36 us
  transfers between devices with their start and end apart: 21, of which 7 were waited for; matrix products, arithmetic and copies ran while one was open for 0% of the time, Pallas kernels for 16%

profile of v6, /device:TPU:1, one launch (start us, length us, event | category | flops | bytes accessed | tf_op | source)
XLA Modules:
  0.0 77.7 jit_solution(9492604902925109097)
XLA Ops:
  0.6 10.4 %compose.1 = (bf16[16,20,128,128]{3,2,1,0:T(8,128)(2,1)S(1)}, bf16[16,128,2560]{2,1,0:T(8,128)(2,1)S(1)}, bf16[2144,128]{1,0:T(8,128)(2,1)S(1)}, bf16[4,16,128,1...) custom-call(s32[1,2,128]{2,1,0:T(2,128)} %rows_hbm.1, ...), custom_call_target="tpu_custom_call" | custom-call | flops 5368709120 | bytes 41943040 | tf_op jit(solution)/shard_map/compose/pallas_call | solution.py:218
  11.1 0.7 collective-permute-start.14
  11.8 1.7 %pack.1 = (bf16[192,640]{1,0:T(8,128)(2,1)S(1)}, bf16[192,640]{1,0:T(8,128)(2,1)S(1)}, bf16[192,640]{1,0:T(8,128)(2,1)S(1)}, bf16[192,640]{1,0:T(8,128)(2,1)S(1)}, f32[32,2560]{1,0:T(8,128)S(1)}) custom-call(f32[96,2560]{1,0:T(8,128)} %bitcast.3, f32[96,2560]{1,0:T(8,128)} %bitcast.4), custom_call_target="tpu_custom_call" | custom-call | tf_op jit(solution)/shard_map/pack/pallas_call | solution.py:81
  13.5 2.1 %collective-permute-start = (bf16[192,640]{1,0:T(8,128)(2,1)S(1)}, bf16[192,640]{1,0:T(8,128)(2,1)S(1)}, u32[]{:S(2)}, u32[]{:S(2)}) collective-permute-start(bf16[192,640]{1,0:T(8,128)(2,1)S(1)} %get-tuple-element.42), channel_id=1, source_target_pairs={{0,8},{8,0},{16,24},{24,16},{1,9},{9,1},{17,25},{25,17},{2,10},{10... | collective-permute-start | bytes 737288 | tf_op jit(solution)/shard_map/ppermute | solution.py:490
  15.6 1.2 %collective-permute-start.1 = (bf16[192,640]{1,0:T(8,128)(2,1)S(1)}, bf16[192,640]{1,0:T(8,128)(2,1)S(1)}, u32[]{:S(2)}, u32[]{:S(2)}) collective-permute-start(bf16[192,640]{1,0:T(8,128)(2,1)S(1)} %get-tuple-element.43), channel_id=1, source_target_pairs={{0,16},{8,24},{16,0},{24,8},{1,17},{9,25},{17,1},{25,9},{2,18},{10... | collective-permute-start | bytes 737288 | tf_op jit(solution)/shard_map/ppermute | solution.py:490
  16.8 0.0 collective-permute-start.2
  16.9 0.4 tables.1
  17.3 1.9 %collective-permute-done.refs_1_ = bf16[192,640]{1,0:T(8,128)(2,1)S(1)} collective-permute-done((bf16[192,640]{1,0:T(8,128)(2,1)S(1)}, bf16[192,640]{1,0:T(8,128)(2,1)S(1)}, u32[]{:S(2)}, u32[]{:S(2)}) %collective-permute-start) | collective-permute-done | bytes 245792 | tf_op jit(solution)/shard_map/ppermute | solution.py:490
  19.2 4.3 %collective-permute-done.1.refs_2_ = bf16[192,640]{1,0:T(8,128)(2,1)S(1)} collective-permute-done((bf16[192,640]{1,0:T(8,128)(2,1)S(1)}, bf16[192,640]{1,0:T(8,128)(2,1)S(1)}, u32[]{:S(2)}, u32[]{:S(2)}) %collective-permute-start.1) | collective-permute-done | bytes 245792 | tf_op jit(solution)/shard_map/ppermute | solution.py:490
  23.5 0.0 collective-permute-done.2.refs_3_
  23.5 0.6 transform.2
  24.0 1.2 %collective-permute-start.3 = (bf16[32,640]{1,0:T(8,128)(2,1)S(1)}, bf16[32,640]{1,0:T(8,128)(2,1)S(1)}, u32[]{:S(2)}, u32[]{:S(2)}) collective-permute-start(bf16[32,640]{1,0:T(8,128)(2,1)S(1)} %get-tuple-element.46), channel_id=1, source_target_pairs={{0,8},{8,0},{16,24},{24,16},{1,9},{9,1},{17,25},{25,17},{2,10},{10... | collective-permute-start | bytes 122888 | tf_op jit(solution)/shard_map/ppermute | solution.py:490
  25.2 0.4 collective-permute-start.4
  25.7 1.1 %collective-permute-start.5 = (bf16[32,640]{1,0:T(8,128)(2,1)S(1)}, bf16[32,640]{1,0:T(8,128)(2,1)S(1)}, u32[]{:S(2)}, u32[]{:S(2)}) collective-permute-start(bf16[32,640]{1,0:T(8,128)(2,1)S(1)} %get-tuple-element.48), channel_id=1, source_target_pairs={{0,24},{8,16},{16,8},{24,0},{1,25},{9,17},{17,9},{25,1},{2,26},{10... | collective-permute-start | bytes 122888 | tf_op jit(solution)/shard_map/ppermute | solution.py:490
  26.8 0.9 %collective-permute-done.3.refs_1_ = bf16[32,640]{1,0:T(8,128)(2,1)S(1)} collective-permute-done((bf16[32,640]{1,0:T(8,128)(2,1)S(1)}, bf16[32,640]{1,0:T(8,128)(2,1)S(1)}, u32[]{:S(2)}, u32[]{:S(2)}) %collective-permute-start.3) | collective-permute-done | bytes 40992 | tf_op jit(solution)/shard_map/ppermute | solution.py:490
  27.7 1.8 %collective-permute-done.4.refs_2_ = bf16[32,640]{1,0:T(8,128)(2,1)S(1)} collective-permute-done((bf16[32,640]{1,0:T(8,128)(2,1)S(1)}, bf16[32,640]{1,0:T(8,128)(2,1)S(1)}, u32[]{:S(2)}, u32[]{:S(2)}) %collective-permute-start.4) | collective-permute-done | bytes 40992 | tf_op jit(solution)/shard_map/ppermute | solution.py:490
  29.5 0.0 collective-permute-done.5.refs_3_
  29.5 3.9 %leaf_up.1 = (f32[2,16,2560]{2,1,0:T(8,128)S(1)}, f32[2,16,128]{2,1,0:T(8,128)S(1)}) custom-call(s32[1,2,128]{2,1,0:T(2,128)S(1)} %get-tuple-element.53.rows_ref, f32[32,2560]{1,0:T(8,128)S(1)} %get-tuple-element.54.mag_ref, bf16[16,128,2560]{2,1,0:T(8,128)(2,1)S(1)} %get-tuple-element.55.joint_ref, bf16[32,640]{1,0:T(8,128)(2,1)S(1)} %get-tuple-element.45.refs_0_, ...), custom_call_target="tpu_custom_call" | custom-call | flops 671088640 | bytes 10485760 | tf_op jit(solution)/shard_map/leaf_up/pallas_call | solution.py:273
  33.4 1.3 %collective-permute-start.9 = (f32[2,16,128]{2,1,0:T(8,128)S(1)}, f32[2,16,128]{2,1,0:T(8,128)S(1)}, u32[]{:S(2)}, u32[]{:S(2)}) collective-permute-start(f32[2,16,128]{2,1,0:T(8,128)S(1)} %get-tuple-element.56.one_ref), channel_id=1, source_target_pairs={{0,1},{2,3},{4,5},{6,7},{8,9},{10,11},{12,13},{14,15},{16,17},{18,... | collective-permute-start | bytes 49160 | tf_op jit(solution)/shard_map/ppermute | solution.py:494
  34.7 8.4 %collective-permute-done.9.two_ref = f32[2,16,128]{2,1,0:T(8,128)S(1)} collective-permute-done((f32[2,16,128]{2,1,0:T(8,128)S(1)}, f32[2,16,128]{2,1,0:T(8,128)S(1)}, u32[]{:S(2)}, u32[]{:S(2)}) %collective-permute-start.9) | collective-permute-done | bytes 16416 | tf_op jit(solution)/shard_map/ppermute | solution.py:494
  43.2 0.4 shard_map.103
  43.6 0.7 collective-permute-start.11
  44.2 3.5 %collective-permute-start.10 = (f32[2,16,128]{2,1,0:T(8,128)S(1)}, f32[2,16,128]{2,1,0:T(8,128)S(1)}, u32[]{:S(2)}, u32[]{:S(2)}) collective-permute-start(f32[2,16,128]{2,1,0:T(8,128)S(1)} %get-tuple-element.59), channel_id=1, source_target_pairs={{1,2},{5,6},{9,10},{13,14},{17,18},{21,22},{25,26},{29,30}} | collective-permute-start | bytes 49160 | tf_op jit(solution)/shard_map/ppermute | solution.py:494
  47.7 0.0 collective-permute-done.11.two_ref
  47.7 0.8 %collective-permute-done.10.one_ref = f32[2,16,128]{2,1,0:T(8,128)S(1)} collective-permute-done((f32[2,16,128]{2,1,0:T(8,128)S(1)}, f32[2,16,128]{2,1,0:T(8,128)S(1)}, u32[]{:S(2)}, u32[]{:S(2)}) %collective-permute-start.10) | collective-permute-done | bytes 16416 | tf_op jit(solution)/shard_map/ppermute | solution.py:494
  48.6 0.4 shard_map.104
  48.9 0.7 collective-permute-start.13
  49.6 0.7 collective-permute-start.12
  50.3 0.8 transform.3
  51.1 1.3 %collective-permute-start.6 = (bf16[64,640]{1,0:T(8,128)(2,1)S(1)}, bf16[64,640]{1,0:T(8,128)(2,1)S(1)}, u32[]{:S(2)}, u32[]{:S(2)}) collective-permute-start(bf16[64,640]{1,0:T(8,128)(2,1)S(1)} %get-tuple-element.50), channel_id=1, source_target_pairs={{0,8},{8,0},{16,24},{24,16},{1,9},{9,1},{17,25},{25,17},{2,10},{10... | collective-permute-start | bytes 245768 | tf_op jit(solution)/shard_map/ppermute | solution.py:490
  52.3 0.2 collective-permute-start.7
  52.5 0.0 collective-permute-done.13.two_ref
  52.5 1.2 %collective-permute-start.8 = (bf16[64,640]{1,0:T(8,128)(2,1)S(1)}, bf16[64,640]{1,0:T(8,128)(2,1)S(1)}, u32[]{:S(2)}, u32[]{:S(2)}) collective-permute-start(bf16[64,640]{1,0:T(8,128)(2,1)S(1)} %get-tuple-element.52), channel_id=1, source_target_pairs={{0,24},{8,16},{16,8},{24,0},{1,25},{9,17},{17,9},{25,1},{2,26},{10... | collective-permute-start | bytes 245768 | tf_op jit(solution)/shard_map/ppermute | solution.py:490
  53.8 0.0 collective-permute-done.12.one_ref
  53.8 0.0 collective-permute-done.14.lift_ref
  53.8 0.7 collective-permute-start.16
  54.4 0.7 collective-permute-start.15
  55.1 0.0 collective-permute-done.16.two_ref
  55.1 0.0 collective-permute-done.15.one_ref
  55.1 0.4 shard_map.106
  55.5 0.7 collective-permute-start.18
  56.2 1.3 %collective-permute-start.17 = (bf16[2,16,128]{2,1,0:T(8,128)(2,1)S(1)}, bf16[2,16,128]{2,1,0:T(8,128)(2,1)S(1)}, u32[]{:S(2)}, u32[]{:S(2)}) collective-permute-start(bf16[2,16,128]{2,1,0:T(8,128)(2,1)S(1)} %get-tuple-element.64), channel_id=1, source_target_pairs={{2,1},{6,5},{10,9},{14,13},{18,17},{22,21},{26,25},{30,29}} | collective-permute-start | bytes 24584 | tf_op jit(solution)/shard_map/ppermute | solution.py:494
  57.5 0.0 collective-permute-done.18.two_ref
  57.5 0.7 collective-permute-start.20
  58.2 11.6 %collective-permute-done.17.one_ref = bf16[2,16,128]{2,1,0:T(8,128)(2,1)S(1)} collective-permute-done((bf16[2,16,128]{2,1,0:T(8,128)(2,1)S(1)}, bf16[2,16,128]{2,1,0:T(8,128)(2,1)S(1)}, u32[]{:S(2)}, u32[]{:S(2)}) %collective-permute-start.17) | collective-permute-done | bytes 8224 | tf_op jit(solution)/shard_map/ppermute | solution.py:494
  69.8 0.4 shard_map.107
  70.2 1.3 %collective-permute-start.19 = (bf16[2,16,128]{2,1,0:T(8,128)(2,1)S(1)}, bf16[2,16,128]{2,1,0:T(8,128)(2,1)S(1)}, u32[]{:S(2)}, u32[]{:S(2)}) collective-permute-start(bf16[2,16,128]{2,1,0:T(8,128)(2,1)S(1)} %get-tuple-element.66.here_ref), channel_id=1, source_target_pairs={{1,0},{3,2},{5,4},{7,6},{9,8},{11,10},{13,12},{15,14},{17,16},{19,... | collective-permute-start | bytes 24584 | tf_op jit(solution)/shard_map/ppermute | solution.py:494
  71.5 2.4 %leaf_local.1.local_ref = f32[2,16,2560]{2,1,0:T(8,128)S(1)} custom-call(f32[2,16,2560]{2,1,0:T(8,128)S(1)} %get-tuple-element.67.source_ref, bf16[16,20,128,128]{3,2,1,0:T(8,128)(2,1)S(1)} %get-tuple-element.68.square_ref), custom_call_target="tpu_custom_call" | custom-call | flops 671088640 | bytes 10485760 | tf_op jit(solution)/shard_map/leaf_local/pallas_call | solution.py:314
  73.9 0.0 collective-permute-done.6.refs_5_
  73.9 0.0 collective-permute-done.7.refs_6_
  73.9 0.0 collective-permute-done.8.refs_7_
  73.9 1.0 %spread.1 = f32[96,2560]{1,0:T(8,128)} custom-call(bf16[32,640]{1,0:T(8,128)(2,1)S(1)} %get-tuple-element.45.refs_0_, bf16[32,640]{1,0:T(8,128)(2,1)S(1)} %collective-permute-done.3.refs_1_, bf16[32,640]{1,0:T(8,128)(2,1)S(1)} %collective-permute-done.4.refs_2_, bf16[32,640]{1,0:T(8,128)(2,1)S(1)} %collective-permute-done.5.refs_3_, ...), custom_call_target="tpu_custom_call" | custom-call | tf_op jit(solution)/shard_map/spread/pallas_call | solution.py:390
  74.9 0.0 collective-permute-done.20.refs_3_
  74.9 0.0 collective-permute-done.19.beside_ref
  74.9 2.8 %leaf_down.1 = (f32[2,16,2560]{2,1,0:T(8,128)}, f32[2,16,128]{2,1,0:T(8,128)}) custom-call(s32[1,2,128]{2,1,0:T(2,128)S(1)} %get-tuple-element.53.rows_ref, bf16[2,16,128]{2,1,0:T(8,128)(2,1)S(1)} %get-tuple-element.66.here_ref, bf16[2,16,128]{2,1,0:T(8,128)(2,1)S(1)} %collective-permute-done.19.beside_ref, f32[2,16,2560]{2,1,0:T(8,128)S(1)} %leaf_local.1.local_ref, ...), custom_call_target="tpu_custom_call" | custom-call | tf_op jit(solution)/shard_map/leaf_down/pallas_call | solution.py:363
  (1 shorter events, 0.0 us)
Async XLA Ops:
  11.1 42.7 %collective-permute-start.14 = (bf16[2144,128]{1,0:T(8,128)(2,1)S(1)}, bf16[2144,128]{1,0:T(8,128)(2,1)S(1)}, u32[]{:S(2)}, u32[]{:S(2)}) collective-permute-start(bf16[2144,128]{1,0:T(8,128)(2,1)S(1)} %get-tuple-element.61), channel_id=1, source_target_pairs={{0,4},{8,12},{16,20},{24,28}} | collective-permute-start | bytes 1646600 | tf_op jit(solution)/shard_map/ppermute | solution.py:494
  13.5 5.7 %collective-permute-start = (bf16[192,640]{1,0:T(8,128)(2,1)S(1)}, bf16[192,640]{1,0:T(8,128)(2,1)S(1)}, u32[]{:S(2)}, u32[]{:S(2)}) collective-permute-start(bf16[192,640]{1,0:T(8,128)(2,1)S(1)} %get-tuple-element.42), channel_id=1, source_target_pairs={{0,8},{8,0},{16,24},{24,16},{1,9},{9,1},{17,25},{25,17},{2,10},{10... | collective-permute-start | bytes 737288 | tf_op jit(solution)/shard_map/ppermute | solution.py:490
  15.6 7.8 %collective-permute-start.1 = (bf16[192,640]{1,0:T(8,128)(2,1)S(1)}, bf16[192,640]{1,0:T(8,128)(2,1)S(1)}, u32[]{:S(2)}, u32[]{:S(2)}) collective-permute-start(bf16[192,640]{1,0:T(8,128)(2,1)S(1)} %get-tuple-element.43), channel_id=1, source_target_pairs={{0,16},{8,24},{16,0},{24,8},{1,17},{9,25},{17,1},{25,9},{2,18},{10... | collective-permute-start | bytes 737288 | tf_op jit(solution)/shard_map/ppermute | solution.py:490
  16.8 6.6 %collective-permute-start.2 = (bf16[192,640]{1,0:T(8,128)(2,1)S(1)}, bf16[192,640]{1,0:T(8,128)(2,1)S(1)}, u32[]{:S(2)}, u32[]{:S(2)}) collective-permute-start(bf16[192,640]{1,0:T(8,128)(2,1)S(1)} %get-tuple-element.44), channel_id=1, source_target_pairs={{0,24},{8,16},{16,8},{24,0},{1,25},{9,17},{17,9},{25,1},{2,26},{10... | collective-permute-start | bytes 737288 | tf_op jit(solution)/shard_map/ppermute | solution.py:490
  24.0 3.6 %collective-permute-start.3 = (bf16[32,640]{1,0:T(8,128)(2,1)S(1)}, bf16[32,640]{1,0:T(8,128)(2,1)S(1)}, u32[]{:S(2)}, u32[]{:S(2)}) collective-permute-start(bf16[32,640]{1,0:T(8,128)(2,1)S(1)} %get-tuple-element.46), channel_id=1, source_target_pairs={{0,8},{8,0},{16,24},{24,16},{1,9},{9,1},{17,25},{25,17},{2,10},{10... | collective-permute-start | bytes 122888 | tf_op jit(solution)/shard_map/ppermute | solution.py:490
  25.2 4.3 %collective-permute-start.4 = (bf16[32,640]{1,0:T(8,128)(2,1)S(1)}, bf16[32,640]{1,0:T(8,128)(2,1)S(1)}, u32[]{:S(2)}, u32[]{:S(2)}) collective-permute-start(bf16[32,640]{1,0:T(8,128)(2,1)S(1)} %get-tuple-element.47), channel_id=1, source_target_pairs={{0,16},{8,24},{16,0},{24,8},{1,17},{9,25},{17,1},{25,9},{2,18},{10... | collective-permute-start | bytes 122888 | tf_op jit(solution)/shard_map/ppermute | solution.py:490
  25.7 3.8 %collective-permute-start.5 = (bf16[32,640]{1,0:T(8,128)(2,1)S(1)}, bf16[32,640]{1,0:T(8,128)(2,1)S(1)}, u32[]{:S(2)}, u32[]{:S(2)}) collective-permute-start(bf16[32,640]{1,0:T(8,128)(2,1)S(1)} %get-tuple-element.48), channel_id=1, source_target_pairs={{0,24},{8,16},{16,8},{24,0},{1,25},{9,17},{17,9},{25,1},{2,26},{10... | collective-permute-start | bytes 122888 | tf_op jit(solution)/shard_map/ppermute | solution.py:490
  33.4 9.7 %collective-permute-start.9 = (f32[2,16,128]{2,1,0:T(8,128)S(1)}, f32[2,16,128]{2,1,0:T(8,128)S(1)}, u32[]{:S(2)}, u32[]{:S(2)}) collective-permute-start(f32[2,16,128]{2,1,0:T(8,128)S(1)} %get-tuple-element.56.one_ref), channel_id=1, source_target_pairs={{0,1},{2,3},{4,5},{6,7},{8,9},{10,11},{12,13},{14,15},{16,17},{18,... | collective-permute-start | bytes 49160 | tf_op jit(solution)/shard_map/ppermute | solution.py:494
  43.6 4.1 %collective-permute-start.11 = (f32[2,16,128]{2,1,0:T(8,128)S(1)}, f32[2,16,128]{2,1,0:T(8,128)S(1)}, u32[]{:S(2)}, u32[]{:S(2)}) collective-permute-start(f32[2,16,128]{2,1,0:T(8,128)S(1)} %get-tuple-element.59), channel_id=1, source_target_pairs={{3,2},{7,6},{11,10},{15,14},{19,18},{23,22},{27,26},{31,30}} | collective-permute-start | bytes 49160 | tf_op jit(solution)/shard_map/ppermute | solution.py:494
  44.2 4.3 %collective-permute-start.10 = (f32[2,16,128]{2,1,0:T(8,128)S(1)}, f32[2,16,128]{2,1,0:T(8,128)S(1)}, u32[]{:S(2)}, u32[]{:S(2)}) collective-permute-start(f32[2,16,128]{2,1,0:T(8,128)S(1)} %get-tuple-element.59), channel_id=1, source_target_pairs={{1,2},{5,6},{9,10},{13,14},{17,18},{21,22},{25,26},{29,30}} | collective-permute-start | bytes 49160 | tf_op jit(solution)/shard_map/ppermute | solution.py:494
  48.9 3.6 %collective-permute-start.13 = (f32[2,16,128]{2,1,0:T(8,128)S(1)}, f32[2,16,128]{2,1,0:T(8,128)S(1)}, u32[]{:S(2)}, u32[]{:S(2)}) collective-permute-start(f32[2,16,128]{2,1,0:T(8,128)S(1)} %get-tuple-element.60), channel_id=1, source_target_pairs={{6,4},{14,12},{22,20},{30,28}} | collective-permute-start | bytes 49160 | tf_op jit(solution)/shard_map/ppermute | solution.py:494
  49.6 4.2 %collective-permute-start.12 = (f32[2,16,128]{2,1,0:T(8,128)S(1)}, f32[2,16,128]{2,1,0:T(8,128)S(1)}, u32[]{:S(2)}, u32[]{:S(2)}) collective-permute-start(f32[2,16,128]{2,1,0:T(8,128)S(1)} %get-tuple-element.60), channel_id=1, source_target_pairs={{2,4},{10,12},{18,20},{26,28}} | collective-permute-start | bytes 49160 | tf_op jit(solution)/shard_map/ppermute | solution.py:494
  51.1 22.8 %collective-permute-start.6 = (bf16[64,640]{1,0:T(8,128)(2,1)S(1)}, bf16[64,640]{1,0:T(8,128)(2,1)S(1)}, u32[]{:S(2)}, u32[]{:S(2)}) collective-permute-start(bf16[64,640]{1,0:T(8,128)(2,1)S(1)} %get-tuple-element.50), channel_id=1, source_target_pairs={{0,8},{8,0},{16,24},{24,16},{1,9},{9,1},{17,25},{25,17},{2,10},{10... | collective-permute-start | bytes 245768 | tf_op jit(solution)/shard_map/ppermute | solution.py:490
  52.3 21.5 %collective-permute-start.7 = (bf16[64,640]{1,0:T(8,128)(2,1)S(1)}, bf16[64,640]{1,0:T(8,128)(2,1)S(1)}, u32[]{:S(2)}, u32[]{:S(2)}) collective-permute-start(bf16[64,640]{1,0:T(8,128)(2,1)S(1)} %get-tuple-element.51), channel_id=1, source_target_pairs={{0,16},{8,24},{16,0},{24,8},{1,17},{9,25},{17,1},{25,9},{2,18},{10... | collective-permute-start | bytes 245768 | tf_op jit(solution)/shard_map/ppermute | solution.py:490
  52.5 21.3 %collective-permute-start.8 = (bf16[64,640]{1,0:T(8,128)(2,1)S(1)}, bf16[64,640]{1,0:T(8,128)(2,1)S(1)}, u32[]{:S(2)}, u32[]{:S(2)}) collective-permute-start(bf16[64,640]{1,0:T(8,128)(2,1)S(1)} %get-tuple-element.52), channel_id=1, source_target_pairs={{0,24},{8,16},{16,8},{24,0},{1,25},{9,17},{17,9},{25,1},{2,26},{10... | collective-permute-start | bytes 245768 | tf_op jit(solution)/shard_map/ppermute | solution.py:490
  53.8 1.3 %collective-permute-start.16 = (bf16[2,16,128]{2,1,0:T(8,128)(2,1)S(1)}, bf16[2,16,128]{2,1,0:T(8,128)(2,1)S(1)}, u32[]{:S(2)}, u32[]{:S(2)}) collective-permute-start(bf16[2,16,128]{2,1,0:T(8,128)(2,1)S(1)} %get-tuple-element.62), channel_id=1, source_target_pairs={{4,6},{12,14},{20,22},{28,30}} | collective-permute-start | bytes 24584 | tf_op jit(solution)/shard_map/ppermute | solution.py:494
  54.4 0.7 collective-permute-start.15
  55.5 2.0 %collective-permute-start.18 = (bf16[2,16,128]{2,1,0:T(8,128)(2,1)S(1)}, bf16[2,16,128]{2,1,0:T(8,128)(2,1)S(1)}, u32[]{:S(2)}, u32[]{:S(2)}) collective-permute-start(bf16[2,16,128]{2,1,0:T(8,128)(2,1)S(1)} %get-tuple-element.64), channel_id=1, source_target_pairs={{2,3},{6,7},{10,11},{14,15},{18,19},{22,23},{26,27},{30,31}} | collective-permute-start | bytes 24584 | tf_op jit(solution)/shard_map/ppermute | solution.py:494
  56.2 13.6 %collective-permute-start.17 = (bf16[2,16,128]{2,1,0:T(8,128)(2,1)S(1)}, bf16[2,16,128]{2,1,0:T(8,128)(2,1)S(1)}, u32[]{:S(2)}, u32[]{:S(2)}) collective-permute-start(bf16[2,16,128]{2,1,0:T(8,128)(2,1)S(1)} %get-tuple-element.64), channel_id=1, source_target_pairs={{2,1},{6,5},{10,9},{14,13},{18,17},{22,21},{26,25},{30,29}} | collective-permute-start | bytes 24584 | tf_op jit(solution)/shard_map/ppermute | solution.py:494
  57.5 17.4 %collective-permute-start.20 = (f32[2,16,128]{2,1,0:T(8,128)S(1)}, f32[2,16,128]{2,1,0:T(8,128)S(1)}, u32[]{:S(2)}, u32[]{:S(2)}) collective-permute-start(f32[2,16,128]{2,1,0:T(8,128)S(1)} %get-tuple-element.72), channel_id=1, source_target_pairs={{4,0},{12,8},{20,16},{28,24}} | collective-permute-start | bytes 49160 | tf_op jit(solution)/shard_map/ppermute | solution.py:494
  70.2 4.7 %collective-permute-start.19 = (bf16[2,16,128]{2,1,0:T(8,128)(2,1)S(1)}, bf16[2,16,128]{2,1,0:T(8,128)(2,1)S(1)}, u32[]{:S(2)}, u32[]{:S(2)}) collective-permute-start(bf16[2,16,128]{2,1,0:T(8,128)(2,1)S(1)} %get-tuple-element.66.here_ref), channel_id=1, source_target_pairs={{1,0},{3,2},{5,4},{7,6},{9,8},{11,10},{13,12},{15,14},{17,16},{19,... | collective-permute-start | bytes 24584 | tf_op jit(solution)/shard_map/ppermute | solution.py:494
